TPU v7x, 32 devices: a whole 2x2x4 slice. The times are simulated.
32 devices in a mesh: dp: 2 (over x), fsdp: 16 (over z, y, core).
Axes of the slice: x: 2, y: 2, z: 4, core: 2. Of those that a mesh axis runs over, the one named last changes fastest.
Arguments:
- tok_ids: int32 [96, 96], P(('dp', 'fsdp')), parts along dimension 0
- grad_out: bfloat16 [96, 96, 2048], P(('dp', 'fsdp')), parts along dimension 0
- emb_table: bfloat16 [102400, 2048], P('fsdp')
- norm_gain: bfloat16 [2048], P('fsdp')
- w_query: bfloat16 [2048, 3072], P('fsdp')
- w_kv_down: bfloat16 [2048, 576], P('fsdp')
- kv_gain: bfloat16 [512], P('fsdp')
- w_kv_up: bfloat16 [512, 4096], P('fsdp')
- w_out: bfloat16 [2048, 2048], P('fsdp')
Outputs:
- output 1: bfloat16 [96, 96, 2048], P(('dp', 'fsdp')), parts along dimension 0
- output 2: bfloat16 [204800, 2048], P(('dp', 'fsdp')), parts along dimension 0
- output 3: float32 [4096], P(('dp', 'fsdp')), parts along dimension 0
- output 4: float32 [4096, 3072], P(('dp', 'fsdp')), parts along dimension 0
- output 5: float32 [4096, 576], P(('dp', 'fsdp')), parts along dimension 0
- output 6: float32 [1024], P(('dp', 'fsdp')), parts along dimension 0
- output 7: float32 [1024, 4096], P(('dp', 'fsdp')), parts along dimension 0
- output 8: float32 [4096, 2048], P(('dp', 'fsdp')), parts along dimension 0
There are 2 independent parts. A program takes and returns all parts, laid end to end along the dimension named above; an argument that names none is the same for every part.
All inputs are finite; a program needn't handle non-finite values.
Results may differ from a plain program's by a relative error of at most 0.0117806.
Values are sent between devices in bfloat16 or wider.
A program may use at most 1 GiB of HBM per device.

v0:
```python
import math
import jax
import jax.numpy as jnp
from jax import lax
from jax.sharding import PartitionSpec as P

NOPE_DIM = 128
ROPE_DIM = 64
VALUE_DIM = 128
ROPE_THETA = 50000.0
RMS_EPS = 1e-6
ATTN_SCALE = (NOPE_DIM + ROPE_DIM) ** -0.5 * (0.1 * math.log(32.0) + 1.0) ** 2
ROW_DIMS = (((0,), (0,)), ((), ()))
COL_DIMS = (((1,), (1,)), ((), ()))


def rms_scale(in_vals, gain_vec):
    vals_f32 = in_vals.astype(jnp.float32)
    inv_rms = lax.rsqrt(jnp.mean(vals_f32 * vals_f32, axis=-1, keepdims=True) + RMS_EPS)
    return (vals_f32 * inv_rms * gain_vec).astype(jnp.bfloat16)


def rope_tables(seq_len):
    positions = jnp.arange(seq_len, dtype=jnp.float32)
    inv_freq = ROPE_THETA ** (-2.0 * jnp.arange(ROPE_DIM // 2, dtype=jnp.float32) / ROPE_DIM)
    rot_angle = positions[:, None] * inv_freq[None, :]
    rot_angle = jnp.concatenate([rot_angle, rot_angle], axis=-1)
    return jnp.cos(rot_angle), jnp.sin(rot_angle)


def apply_rope(in_vals, cos_tab, sin_tab):
    half_dim = ROPE_DIM // 2
    vals_f32 = in_vals.astype(jnp.float32)
    turned = jnp.concatenate([-vals_f32[..., half_dim:], vals_f32[..., :half_dim]], axis=-1)
    return (vals_f32 * cos_tab + turned * sin_tab).astype(jnp.bfloat16)


def attend_local(q_proj, pe_raw, kv_up):
    seq_len = q_proj.shape[1]
    cos_tab, sin_tab = rope_tables(seq_len)
    q_rot = apply_rope(q_proj[..., NOPE_DIM:], cos_tab[:, None, :], sin_tab[:, None, :])
    k_rot = apply_rope(pe_raw, cos_tab, sin_tab)
    scores = jnp.einsum('bshd,bthd->bhst', q_proj[..., :NOPE_DIM], kv_up[..., :NOPE_DIM], preferred_element_type=jnp.float32)
    scores = scores + jnp.einsum('bshd,btd->bhst', q_rot, k_rot, preferred_element_type=jnp.float32)
    positions = jnp.arange(seq_len)
    causal = positions[:, None] >= positions[None, :]
    scores = jnp.where(causal, scores * ATTN_SCALE, -1e30)
    attn_probs = jax.nn.softmax(scores, axis=-1).astype(jnp.bfloat16)
    attn_mix = jnp.einsum('bhst,bthd->bshd', attn_probs, kv_up[..., NOPE_DIM:], preferred_element_type=jnp.float32)
    return attn_mix.astype(jnp.bfloat16)


def block_step(tok_rows, grad_rows, full_weights, seq_count):
    gain_vec, w_query, w_kv_down, kv_gain, w_kv_up, w_out = full_weights
    kv_rank = kv_gain.shape[0]
    tok_count = tok_rows.shape[0]
    seq_len = tok_count // seq_count
    rows_f32 = tok_rows.astype(jnp.float32)
    normed, norm_pull = jax.vjp(rms_scale, rows_f32, gain_vec.astype(jnp.float32))
    q_proj = jnp.dot(normed, w_query, preferred_element_type=jnp.float32).astype(jnp.bfloat16)
    kv_down = jnp.dot(normed, w_kv_down, preferred_element_type=jnp.float32).astype(jnp.bfloat16)
    latent, latent_pull = jax.vjp(rms_scale, kv_down[:, :kv_rank], kv_gain.astype(jnp.float32))
    kv_up = jnp.dot(latent, w_kv_up, preferred_element_type=jnp.float32).astype(jnp.bfloat16)
    attn_mix, attn_pull = jax.vjp(attend_local, q_proj.reshape(seq_count, seq_len, -1, NOPE_DIM + ROPE_DIM), kv_down[:, kv_rank:].reshape(seq_count, seq_len, ROPE_DIM), kv_up.reshape(seq_count, seq_len, -1, NOPE_DIM + VALUE_DIM))
    mix_rows = attn_mix.reshape(tok_count, -1)
    out_f32 = rows_f32 + jnp.dot(mix_rows, w_out, preferred_element_type=jnp.float32)
    d_w_out = lax.dot_general(mix_rows, grad_rows, ROW_DIMS, preferred_element_type=jnp.float32)
    d_mix = lax.dot_general(grad_rows, w_out, COL_DIMS, preferred_element_type=jnp.float32).astype(jnp.bfloat16)
    d_query, d_pe, d_up = attn_pull(d_mix.reshape(attn_mix.shape))
    d_query = d_query.reshape(tok_count, -1)
    d_up = d_up.reshape(tok_count, -1)
    d_w_kv_up = lax.dot_general(latent, d_up, ROW_DIMS, preferred_element_type=jnp.float32)
    d_latent = lax.dot_general(d_up, w_kv_up, COL_DIMS, preferred_element_type=jnp.float32).astype(jnp.bfloat16)
    d_ckv, d_kv_gain = latent_pull(d_latent)
    d_down = jnp.concatenate([d_ckv, d_pe.reshape(tok_count, ROPE_DIM)], axis=1)
    d_w_kv_down = lax.dot_general(normed, d_down, ROW_DIMS, preferred_element_type=jnp.float32)
    d_w_query = lax.dot_general(normed, d_query, ROW_DIMS, preferred_element_type=jnp.float32)
    d_normed = lax.dot_general(d_query, w_query, COL_DIMS, preferred_element_type=jnp.float32)
    d_normed = d_normed + lax.dot_general(d_down, w_kv_down, COL_DIMS, preferred_element_type=jnp.float32)
    d_rows, d_gain = norm_pull(d_normed.astype(jnp.bfloat16))
    d_rows = d_rows + grad_rows.astype(jnp.float32)
    return out_f32.astype(jnp.bfloat16), d_rows, (d_gain, d_w_query, d_w_kv_down, d_kv_gain, d_w_kv_up, d_w_out)


def solution(mesh):
    tok_spec = P(('dp', 'fsdp'), None)
    seq_spec = P(('dp', 'fsdp'), None, None)
    part_vec = P(('dp', 'fsdp'))
    vec_spec = P('fsdp')
    mat_spec = P('fsdp', None)

    def device_step(tok_ids, grad_out, emb_table, norm_gain, w_query, w_kv_down, kv_gain, w_kv_up, w_out):
        seq_count, seq_len = tok_ids.shape
        vocab_dev, d_model = emb_table.shape
        tok_count = seq_count * seq_len
        all_ids = lax.all_gather(tok_ids.reshape(tok_count), 'fsdp', tiled=True)
        local_ids = all_ids - lax.axis_index('fsdp') * vocab_dev
        is_owned = (local_ids >= 0) & (local_ids < vocab_dev)
        picked = jnp.take(emb_table, jnp.where(is_owned, local_ids, 0), axis=0)
        picked = jnp.where(is_owned[:, None], picked, jnp.zeros((), picked.dtype))
        tok_rows = lax.psum_scatter(picked, 'fsdp', scatter_dimension=0, tiled=True)
        full_weights = tuple(lax.all_gather(shard_piece, 'fsdp', tiled=True) for shard_piece in (norm_gain, w_query, w_kv_down, kv_gain, w_kv_up, w_out))
        block_out, d_rows, weight_grads = block_step(tok_rows, grad_out.reshape(tok_count, d_model), full_weights, seq_count)
        all_grads = lax.all_gather(d_rows, 'fsdp', tiled=True)
        seg_ids = jnp.where(is_owned, local_ids, vocab_dev)
        grad_table = jax.ops.segment_sum(all_grads, seg_ids, num_segments=vocab_dev).astype(jnp.bfloat16)
        grad_shards = tuple(lax.psum_scatter(full_grad, 'fsdp', scatter_dimension=0, tiled=True) for full_grad in weight_grads)
        return (block_out.reshape(seq_count, seq_len, d_model), grad_table) + grad_shards

    return jax.shard_map(device_step, mesh=mesh, in_specs=(tok_spec, seq_spec, mat_spec, vec_spec, mat_spec, mat_spec, vec_spec, mat_spec, mat_spec), out_specs=(seq_spec, tok_spec, part_vec, tok_spec, tok_spec, part_vec, tok_spec, tok_spec), check_vma=False)
```

profile of v0, /device:TPU:0, one launch (start us, length us, event | category | flops | bytes accessed | tf_op | source)
XLA Modules:
  0.0 1385.3 jit_solution(15751249490089540305)
XLA Ops:
  11.0 63.8 %all-reduce.8 = s32[4608]{0:T(1024)S(1)} all-reduce(s32[4608]{0:T(1024)S(1)} %dynamic-update-slice), channel_id=1, replica_groups=mesh['dp'=2,'fsdp'=16] {'fsdp'}, use_global_device_ids=true, to_apply=%add.8 | all-reduce | flops 4608 | bytes 36864
  74.9 46.9 %gather_fusion = bf16[4608,2048]{1,0:T(8,128)(2,1)} fusion(bf16[6400,2048]{1,0:T(8,128)(2,1)} %param.11, s32[5120]{0:T(1024)S(1)} %pad_clamp_fusion), kind=kCustom, calls=%fused_computation | custom fusion | bytes 37767168 | tf_op jit(solution)/shard_map/jit(_take)/gather | solution.py:99
  121.8 18.0 %select_select_fusion = bf16[4608,2048]{1,0:T(8,128)(2,1)} fusion(bf16[4608,2048]{1,0:T(8,128)(2,1)} %gather_fusion, pred[4608]{0:T(1024)(128)(4,1)S(1)} %get-tuple-element.16, pred[4608]{0:T(1024)(128)(4,1)S(1)} %get-tuple-element.32), kind=kLoop, calls=%fused_computation.4 | loop fusion | flops 18874368 | bytes 37757952 | tf_op jit(solution)/shard_map/jit(_where)/select_n | solution.py:100
  142.6 29.5 %all-reduce.9 = bf16[512]{0:T(512)(128)(2,1)S(1)} all-reduce(bf16[512]{0:T(512)(128)(2,1)S(1)} %dynamic-update-slice.1), channel_id=1, replica_groups=mesh['dp'=2,'fsdp'=16] {'fsdp'}, use_global_device_ids=true, to_apply=%add.9 | all-reduce | flops 512 | bytes 2048
  172.1 17.8 %all-gather = bf16[16,1,128]{2,1,0:T(2,128)(2,1)S(1)} all-gather(bf16[1,1,128]{2,1,0:T(2,128)(2,1)S(1)} %bitcast.133), channel_id=1, replica_groups=mesh['dp'=2,'fsdp'=16] {'fsdp'}, dimensions={0}, use_global_device_ids=true | all-gather | bytes 4352 | tf_op jit(solution)/shard_map/all_gather | solution.py:102
  192.8 6.0 fusion.38
  200.2 129.0 %reduce-scatter.6.cloned.1.call-done = bf16[288,2048]{1,0:T(8,128)(2,1)} async-done(((bf16[4608,2048]{1,0:T(8,128)(2,1)}), bf16[288,2048]{1,0:T(8,128)(2,1)}) %reduce-scatter.6.cloned.1.call-update) | async-done | bytes 1179664 | tf_op jit(solution)/shard_map/reduce_scatter | solution.py:101
  331.3 99.7 %all-gather.11.cloned.1.call-done = bf16[2048,3072]{1,0:T(8,128)(2,1)} async-done(((bf16[128,3072]{1,0:T(8,128)(2,1)}), bf16[2048,3072]{1,0:T(8,128)(2,1)}) %all-gather.11.cloned.1.call-update) | async-done | bytes 12582928 | tf_op jit(solution)/shard_map/all_gather | solution.py:102
  431.0 10.1 convolution_convert_fusion.1
  441.1 4.2 reshape.193
  447.7 26.5 %all-gather.7.cloned.1.call-done = bf16[2048,576]{0,1:T(8,128)(2,1)} async-done(((bf16[128,576]{0,1:T(8,128)(2,1)}), bf16[2048,576]{0,1:T(8,128)(2,1)}) %all-gather.7.cloned.1.call-update) | async-done | bytes 2359312 | tf_op jit(solution)/shard_map/all_gather | solution.py:102
  474.3 2.8 convolution_convert_fusion.9
  480.2 45.6 %all-gather.9.cloned.1.call-done = bf16[512,4096]{1,0:T(8,128)(2,1)} async-done(((bf16[32,4096]{1,0:T(8,128)(2,1)}), bf16[512,4096]{1,0:T(8,128)(2,1)}) %all-gather.9.cloned.1.call-update) | async-done | bytes 4194320 | tf_op jit(solution)/shard_map/all_gather | solution.py:102
  525.8 3.7 convolution_convert_fusion
  541.1 2.4 fusion.34
  551.3 2.8 fusion.61
  561.5 3.4 reshape.198
  566.2 8.0 fusion.93
  576.3 2.2 fusion.22
  578.6 3.8 fusion.65
  584.0 6.7 fusion.69
  592.4 2.0 fusion.36
  596.0 8.3 fusion.40
  605.7 12.0 fusion.81
  619.2 60.6 %all-reduce.12 = (f32[2048]{0:T(1024)S(1)}, f32[512]{0:T(512)S(1)}) all-reduce(f32[2048]{0:T(1024)S(1)} %copy-done.42, f32[512]{0:T(512)S(1)} %copy-done.43), channel_id=3, replica_groups=mesh['dp'=2,'fsdp'=16] {'fsdp'}, use_global_device_ids=true, to_apply=%region_10.11.clone | all-reduce | flops 2560 | bytes 20480
  681.0 7.0 fusion.5
  688.0 78.1 %all-gather.15.cloned.1.call-done = f32[4608,2048]{1,0:T(8,128)} async-done(((f32[288,2048]{1,0:T(8,128)}), f32[4608,2048]{1,0:T(8,128)}) %all-gather.15.cloned.1.call-update) | async-done | bytes 37748752 | tf_op jit(solution)/shard_map/all_gather | solution.py:104
  766.1 79.1 %scatter_custom_fusion = f32[6400,2048]{1,0:T(8,128)} fusion(s32[4608]{0:T(1024)S(1)} %subtract_select_fusion, f32[4608,2048]{1,0:T(8,128)} %all-gather.15.cloned.1.call-done, f32[]{:T(128)} %constant.23.clone.1), kind=kCustom, calls=%fused_computation.2 | custom fusion | flops 9437184 | bytes 52429312 | tf_op jit(solution)/shard_map/scatter-add | solution.py:106
  845.2 26.5 %convert_element_type.170 = bf16[6400,2048]{1,0:T(8,128)(2,1)} convert(f32[6400,2048]{1,0:T(8,128)} %scatter_custom_fusion) | non-fusion elementwise | flops 13107200 | bytes 78643200 | tf_op jit(solution)/shard_map/convert_element_type | solution.py:106
  871.7 82.8 %reduce-scatter.12.cloned.1.call-done = f32[32,4096]{1,0:T(8,128)} async-done(((f32[512,4096]{1,0:T(8,128)}), f32[32,4096]{1,0:T(8,128)}) %reduce-scatter.12.cloned.1.call-update) | async-done | bytes 524304 | tf_op jit(solution)/shard_map/reduce_scatter | solution.py:107
  954.4 179.8 %reduce-scatter.14.cloned.1.call-done = f32[128,2048]{1,0:T(8,128)} async-done(((f32[2048,2048]{1,0:T(8,128)}), f32[128,2048]{1,0:T(8,128)}) %reduce-scatter.14.cloned.1.call-update) | async-done | bytes 1048592 | tf_op jit(solution)/shard_map/reduce_scatter | solution.py:107
  1134.2 244.0 %reduce-scatter.8.cloned.1.call-done = f32[128,3072]{1,0:T(8,128)} async-done(((f32[2048,3072]{1,0:T(8,128)}), f32[128,3072]{1,0:T(8,128)}) %reduce-scatter.8.cloned.1.call-update) | async-done | bytes 1572880 | tf_op jit(solution)/shard_map/reduce_scatter | solution.py:107
  (180 shorter events, 54.3 us)
Async XLA Ops:
  7.2 185.7 %all-gather.13.cloned.1.call-start = ((), (), s32[]{:S(2)}) async-start(), calls=%async_computation.9 | async-start | bytes 8912896 | tf_op jit(solution)/shard_map/all_gather | solution.py:102
  7.9 321.2 %reduce-scatter.6.cloned.1.call-start = ((), (), s32[]{:S(2)}) async-start(), calls=%async_computation.5 | async-start | bytes 20054016 | tf_op jit(solution)/shard_map/reduce_scatter | solution.py:101
  74.8 46.9 %copy-start.33 = (s32[4608]{0:T(1024)}, s32[4608]{0:T(1024)S(1)}, u32[]{:S(2)}) copy-start(s32[4608]{0:T(1024)S(1)} %all-reduce.8) | copy-start | bytes 55300
  139.7 2.6 copy-start.47
  139.7 32.4 %copy-start.44 = (bf16[128]{0:T(256)(128)(2,1)S(1)}, bf16[128]{0:T(256)(128)(2,1)}, u32[]{:S(2)}) copy-start(bf16[128]{0:T(256)(128)(2,1)} %param.12) | copy-start | bytes 772
  139.7 53.1 %copy-start.9 = (bf16[3,96,2048]{2,1,0:T(8,128)(2,1)S(1)}, bf16[3,96,2048]{2,1,0:T(8,128)(2,1)}, u32[]{:S(2)}) copy-start(bf16[3,96,2048]{2,1,0:T(8,128)(2,1)} %param.10) | copy-start | bytes 3538948
  139.7 291.2 %all-gather.11.cloned.1.call-start = ((), (), s32[]{:S(2)}) async-start(), calls=%async_computation.8 | async-start | bytes 13369344 | tf_op jit(solution)/shard_map/all_gather | solution.py:102
  140.5 333.8 %all-gather.7.cloned.1.call-start = ((), (), s32[]{:S(2)}) async-start(), calls=%async_computation.6 | async-start | bytes 2506752 | tf_op jit(solution)/shard_map/all_gather | solution.py:102
  141.1 384.8 %all-gather.9.cloned.1.call-start = ((), (), s32[]{:S(2)}) async-start(), calls=%async_computation.7 | async-start | bytes 4456448 | tf_op jit(solution)/shard_map/all_gather | solution.py:102
  141.7 624.5 %all-gather.15.cloned.1.call-start = ((), (), s32[]{:S(2)}) async-start(), calls=%async_computation.10 | async-start | bytes 40108032 | tf_op jit(solution)/shard_map/all_gather | solution.py:104
  190.2 8.7 copy-start.21
  190.2 8.7 copy-start.24
  445.3 29.0 %copy-start = (bf16[288,2048]{1,0:T(8,128)(2,1)S(1)}, bf16[288,2048]{1,0:T(8,128)(2,1)}, u32[]{:S(2)}) copy-start(bf16[288,2048]{1,0:T(8,128)(2,1)} %reduce-scatter.6.cloned.1.call-done) | copy-start | bytes 3538948
  530.8 7.9 copy-start.17
  530.8 1.7 copy-start.1
  535.8 5.2 copy-start.2
  535.8 7.6 copy-start.30
  535.8 2.1 copy-start.16
  536.4 7.1 copy-start.29
  541.1 2.4 copy-start.36
  548.5 2.8 copy-start.45
  549.7 4.5 copy-start.4
  551.3 2.8 copy-start.41
  566.2 8.1 copy-start.26
  566.2 8.1 copy-start.46
  574.3 2.0 copy-start.39
  574.3 2.0 copy-start.10
  578.6 293.1 %reduce-scatter.10.cloned.1.call-start = ((), (), s32[]{:S(2)}) async-start(), calls=%async_computation.12 | async-start | bytes 5013504 | tf_op jit(solution)/shard_map/reduce_scatter | solution.py:107
  582.4 372.0 %reduce-scatter.12.cloned.1.call-start = ((), (), s32[]{:S(2)}) async-start(), calls=%async_computation.13 | async-start | bytes 8912896 | tf_op jit(solution)/shard_map/reduce_scatter | solution.py:107
  590.8 543.4 %reduce-scatter.14.cloned.1.call-start = ((), (), s32[]{:S(2)}) async-start(), calls=%async_computation.14 | async-start | bytes 17825792 | tf_op jit(solution)/shard_map/reduce_scatter | solution.py:107
  604.3 773.9 %reduce-scatter.8.cloned.1.call-start = ((), (), s32[]{:S(2)}) async-start(), calls=%async_computation.11 | async-start | bytes 26738688 | tf_op jit(solution)/shard_map/reduce_scatter | solution.py:107
  617.8 63.2 %copy-start.8 = (bf16[3,96,16,128]{3,2,1,0:T(8,128)(2,1)S(1)}, bf16[3,96,16,128]{3,2,1,0:T(8,128)(2,1)}, u32[]{:S(2)}) copy-start(bf16[3,96,16,128]{3,2,1,0:T(8,128)(2,1)} %copy-done.7) | copy-start | bytes 3538948
  (26 other events, 31.1 us)
Sparse Core Ops, SparseCore 0:
  10.1 77.5 all-gather.12
  139.9 189.2 reduce-scatter.5
  331.4 99.5 all-gather.10
  433.0 41.2 all-gather.6
  476.3 49.5 all-gather.8
  578.7 187.4 all-gather.14
  770.6 76.5 reduce-scatter.9
  851.8 102.5 reduce-scatter.11
  959.1 175.0 reduce-scatter.13
  1138.7 239.4 reduce-scatter.7
where the time goes:
time: 1390 us
  waiting for transfers between devices  888 us (64%)
  blocking collectives  172 us (12%)
  other arithmetic  140 us (10%)
  matrix products  85 us (6%)
  local copies, waits for them, and re-layouts  81.8 us (6%)
  between operations  17.8 us (1%)
    reduce_scatter x4, waiting for transfers between devices, device_step(): lax.psum_scatter(full_grad, 'fsdp', scatter_dimension=0, tiled=True)  507 us
    all_gather x4, waiting for transfers between devices, device_step(): lax.all_gather(shard_piece, 'fsdp', tiled=True)  172 us
    unnamed x3, blocking collectives  154 us
    reduce_scatter x1, waiting for transfers between devices, device_step(): tok_rows = lax.psum_scatter(picked, 'fsdp', scatter_dimension=0, tiled=True)  129 us
    scatter-add x1, other arithmetic, device_step(): jax.ops.segment_sum(all_grads, seg_ids, num_segments=vocab_dev)  79.1 us
    all_gather x1, waiting for transfers between devices, device_step(): all_grads = lax.all_gather(d_rows, 'fsdp', tiled=True)  78.1 us
    gather x1, local copies, waits for them, and re-layouts, device_step(): picked = jnp.take(emb_table, jnp.where(is_owned, local_ids, 0), axis=0)  46.9 us
  transfers between devices with their start and end apart: 10, of which 8 were waited for; matrix products, arithmetic and copies ran while one was open for 18% of the time, Pallas kernels for 0%

commit v1 on v0

v1 whole, which is shorter than its diff:
```python
import math
import jax
import jax.numpy as jnp
from jax import lax
from jax.sharding import PartitionSpec as P
from jax.experimental import pallas as pl
from jax.experimental.pallas import tpu as pltpu

NOPE_DIM = 128
ROPE_DIM = 64
VALUE_DIM = 128
ROPE_THETA = 50000.0
RMS_EPS = 1e-6
ATTN_SCALE = (NOPE_DIM + ROPE_DIM) ** -0.5 * (0.1 * math.log(32.0) + 1.0) ** 2
ROW_DIMS = (((0,), (0,)), ((), ()))
COL_DIMS = (((1,), (1,)), ((), ()))


def rms_scale(in_vals, gain_vec):
    vals_f32 = in_vals.astype(jnp.float32)
    inv_rms = lax.rsqrt(jnp.mean(vals_f32 * vals_f32, axis=-1, keepdims=True) + RMS_EPS)
    return (vals_f32 * inv_rms * gain_vec).astype(jnp.bfloat16)


def rope_tables(seq_len):
    positions = jnp.arange(seq_len, dtype=jnp.float32)
    inv_freq = ROPE_THETA ** (-2.0 * jnp.arange(ROPE_DIM // 2, dtype=jnp.float32) / ROPE_DIM)
    rot_angle = positions[:, None] * inv_freq[None, :]
    rot_angle = jnp.concatenate([rot_angle, rot_angle], axis=-1)
    return jnp.cos(rot_angle), jnp.sin(rot_angle)


def apply_rope(in_vals, cos_tab, sin_tab):
    half_dim = ROPE_DIM // 2
    vals_f32 = in_vals.astype(jnp.float32)
    turned = jnp.concatenate([-vals_f32[..., half_dim:], vals_f32[..., :half_dim]], axis=-1)
    return (vals_f32 * cos_tab + turned * sin_tab).astype(jnp.bfloat16)


def attend_local(q_proj, pe_raw, kv_up):
    seq_len = q_proj.shape[1]
    cos_tab, sin_tab = rope_tables(seq_len)
    q_rot = apply_rope(q_proj[..., NOPE_DIM:], cos_tab[:, None, :], sin_tab[:, None, :])
    k_rot = apply_rope(pe_raw, cos_tab, sin_tab)
    scores = jnp.einsum('bshd,bthd->bhst', q_proj[..., :NOPE_DIM], kv_up[..., :NOPE_DIM], preferred_element_type=jnp.float32)
    scores = scores + jnp.einsum('bshd,btd->bhst', q_rot, k_rot, preferred_element_type=jnp.float32)
    positions = jnp.arange(seq_len)
    causal = positions[:, None] >= positions[None, :]
    scores = jnp.where(causal, scores * ATTN_SCALE, -1e30)
    attn_probs = jax.nn.softmax(scores, axis=-1).astype(jnp.bfloat16)
    attn_mix = jnp.einsum('bhst,bthd->bshd', attn_probs, kv_up[..., NOPE_DIM:], preferred_element_type=jnp.float32)
    return attn_mix.astype(jnp.bfloat16)


F32, BF16 = jnp.float32, jnp.bfloat16
MESH = pl.DeviceIdType.MESH
ANY = pl.BlockSpec(memory_space=pl.ANY)
RING = 8
GROUP = 16

def chip_at(pos):
    side = pos // 4
    return (pos + side * (7 - 2 * pos)) * 2 + side

def place():
    me = lax.axis_index('fsdp')
    core = me % 2
    chip = me // 2
    side = chip % 2
    zz = chip // 2
    return me, core, zz + side * (7 - 2 * zz)

def at_pos(pos, core):
    return chip_at(pos % RING) * 2 + core

def meet_all(me):
    barrier = pltpu.get_barrier_semaphore()
    for step in range(1, GROUP):
        pl.semaphore_signal(barrier, inc=1, device_id={'fsdp': (me + step) % GROUP}, device_id_type=MESH)
    pl.semaphore_wait(barrier, GROUP - 1)

TOK = 288
D_OUT, D_CAT, D_UP, D_DOWN = 2048, 3712, 4096, 640
CUT = 1792
PARTS = (('o', 0, 0, 1024), ('o', 1, 1024, 1024), ('n', 0, 0, CUT), ('n', 1, CUT, D_CAT - CUT), ('u', 0, 0, 2048), ('u', 1, 2048, 2048))
ROWS = {'o': 128, 'n': 128, 'u': 32}

def col_tiles(width):
    step = 512
    return [(c, min(step, width - c)) for c in range(0, width, step)]

def grad_kernel(mix_h, dy_h, nrm_h, dd_h, dq_h, lat_h, du_h, sm_h, go_h, gn_h, gu_h, gs_h,
                mix, dy, nrm, cat, lat, du, b0, b1, b2, b3, b4, b5, smr, ssum, loc_sem, xs_sem, xr_sem, s_sem, r_sem, ms_sem, mr_sem, out_sem):
    me, core, pos = place()
    partner = me + 1 - 2 * core
    meet_all(me)
    acts = ((mix_h, mix), (dy_h, dy), (nrm_h, nrm), (dd_h, cat.at[:, :, 0:D_DOWN]), (dq_h, cat.at[:, :, D_DOWN:D_CAT]), (lat_h, lat), (du_h, du))
    local, cross = [], []
    for i, (src, dst) in enumerate(acts):
        cp = pltpu.make_async_copy(src, dst.at[core], loc_sem.at[i]); cp.start(); local.append(cp)
        rc = pltpu.make_async_remote_copy(src, dst.at[core], xs_sem.at[i], xr_sem.at[i], device_id={'fsdp': partner}, device_id_type=MESH)
        rc.start(); cross.append(rc)
    own_small = pltpu.make_async_copy(sm_h.at[me], smr.at[0], loc_sem.at[7]); own_small.start()
    smalls = []
    for i in range(1, GROUP):
        peer = (me + i) % GROUP
        rc = pltpu.make_async_remote_copy(sm_h.at[peer], smr.at[i], ms_sem.at[i], mr_sem.at[i], device_id={'fsdp': peer}, device_id_type=MESH)
        rc.start(); smalls.append(rc)
    bufs = (b0, b1, b2, b3, b4, b5)
    peers = (at_pos(pos + 1, core), at_pos(pos + 7, core))
    left_ops = {'o': (mix, dy), 'n': (nrm, cat), 'u': (lat, du)}

    def hop(p, step):
        return pltpu.make_async_remote_copy(bufs[p].at[step], bufs[p].at[step + 1], s_sem.at[p, step], r_sem.at[p, step + 1],
                                            device_id={'fsdp': peers[PARTS[p][1]]}, device_id_type=MESH)

    def work(p, step, first):
        kind, way, c0, width = PARTS[p]
        chip = chip_at((pos + 7 - step + way * (2 * step + 2)) % RING)
        lhs_ref, rhs_ref = left_ops[kind]
        if kind == 'u':
            row = pl.multiple_of(chip * 64 + core * 32, 32)
            lhs = [lhs_ref[b, pl.ds(row, 32), :] for b in range(2)]
            dims = (((1,), (0,)), ((), ()))
        else:
            col = pl.multiple_of(chip * 256 + core * 128, 128)
            lhs = [lhs_ref[b, :, pl.ds(col, 128)] for b in range(2)]
            dims = (((0,), (0,)), ((), ()))
        for c, w in col_tiles(width):
            part = sum(lax.dot_general(lhs[b], rhs_ref[b, :, c0 + c:c0 + c + w], dims, preferred_element_type=F32) for b in range(2))
            if first:
                bufs[p][step, :, c:c + w] = part
            else:
                bufs[p][step, :, c:c + w] = bufs[p][step, :, c:c + w] + part

    need = {'o': (0, 1), 'n': (2, 3, 4), 'u': (5, 6)}
    for p in range(6):
        if PARTS[p][1] == 0:
            for i in need[PARTS[p][0]]:
                local[i].wait(); cross[i].wait_recv()
        work(p, 0, True)
        hop(p, 0).start()

    @pl.loop(1, RING - 1)
    def _(step):
        for p in range(6):
            hop(p, step - 1).wait_recv()
            work(p, step, False)
            hop(p, step).start()

    last = RING - 1
    outs = []
    targets = (go_h.at[:, 0:1024], go_h.at[:, 1024:2048], gn_h.at[:, 0:CUT], gn_h.at[:, CUT:D_CAT], gu_h.at[:, 0:2048], gu_h.at[:, 2048:4096])
    for p in range(6):
        hop(p, last - 1).wait_recv()
        work(p, last, False)
        cp = pltpu.make_async_copy(bufs[p].at[last], targets[p], out_sem.at[p]); cp.start(); outs.append(cp)
    own_small.wait()
    for rc in smalls:
        rc.wait()
    ssum[...] = jnp.sum(smr[...], axis=0)
    cp = pltpu.make_async_copy(ssum, gs_h, out_sem.at[6]); cp.start(); outs.append(cp)
    for rc in cross:
        rc.wait_send()
    for p in range(6):
        @pl.loop(0, last)
        def _(step):
            hop(p, step).wait_send()
    for cp in outs:
        cp.wait()

def grad_shards(mix, dy, nrm, dd, dq, lat_t, du, small):
    shapes = [(ROWS[k], RING, w) for k, _, _, w in PARTS]
    scratch = [pltpu.VMEM((2, TOK, 2048), BF16), pltpu.VMEM((2, TOK, 2048), BF16), pltpu.VMEM((2, TOK, 2048), BF16),
               pltpu.VMEM((2, TOK, D_CAT), BF16), pltpu.VMEM((2, 512, TOK), BF16), pltpu.VMEM((2, TOK, D_UP), BF16)]
    scratch += [pltpu.VMEM((RING, r, w), F32) for r, _, w in shapes]
    scratch += [pltpu.VMEM((GROUP, 8, 128), F32), pltpu.VMEM((8, 128), F32)]
    dma = pltpu.SemaphoreType.DMA
    scratch += [dma((8,)), dma((7,)), dma((7,)), dma((6, RING)), dma((6, RING)), dma((GROUP,)), dma((GROUP,)), dma((7,))]
    return pl.pallas_call(
        grad_kernel,
        out_shape=(jax.ShapeDtypeStruct((128, 2048), F32), jax.ShapeDtypeStruct((128, D_CAT), F32), jax.ShapeDtypeStruct((32, D_UP), F32), jax.ShapeDtypeStruct((8, 128), F32)),
        in_specs=[ANY] * 8, out_specs=(ANY,) * 4, scratch_shapes=scratch,
        compiler_params=pltpu.CompilerParams(collective_id=1, has_side_effects=True, vmem_limit_bytes=60 * 1024 * 1024),
        cost_estimate=pl.CostEstimate(flops=8 * 10**9, bytes_accessed=20 * 10**6, transcendentals=0), name='grad_shards',
    )(mix, dy, nrm, dd, dq, lat_t, du, small)


W_SHARDS = ((128, 3072), (128, 576), (32, 4096), (128, 2048))
HALF_TOK = TOK // 2


def spread_kernel(n_w, *refs):
    rows_h = refs[0]
    srcs = refs[1:1 + n_w]
    got_h = refs[1 + n_w]
    outs = refs[2 + n_w:2 + 2 * n_w]
    stage = refs[2 + 2 * n_w:2 + 3 * n_w]
    own, mate, way0, way1 = refs[2 + 3 * n_w:6 + 3 * n_w]
    in_sem, own_sem, s_sem, r_sem, ps_sem, pr_sem, h_in, m_s, m_r, hs_sem, hr_sem, out_sem = refs[6 + 3 * n_w:]
    me, core, pos = place()
    partner = me + 1 - 2 * core
    barrier = pltpu.get_barrier_semaphore()
    peers = (at_pos(pos + 1, core), at_pos(pos + 7, core))
    for peer in peers + (partner,):
        pl.semaphore_signal(barrier, inc=1, device_id={'fsdp': peer}, device_id_type=MESH)
    pl.semaphore_wait(barrier, 3)
    loads = []
    for i in range(n_w):
        cp = pltpu.make_async_copy(srcs[i], stage[i], in_sem.at[i])
        cp.start()
        loads.append(cp)

    def row_load(q):
        return pltpu.make_async_copy(rows_h.at[at_pos(q, core)], own.at[q], h_in.at[q])

    def row_share(q):
        return pltpu.make_async_remote_copy(rows_h.at[at_pos(q, 1 - core)], mate.at[q], m_s.at[q], m_r.at[q],
                                            device_id={'fsdp': partner}, device_id_type=MESH)
    for j in (7, 1, 6, 2, 5, 3, 4, 0):
        row_share((pos + j) % RING).start()
        row_load((pos + j) % RING).start()

    def where(i, way, source):
        rows = W_SHARDS[i][0]
        half = rows // 2
        return outs[i].at[pl.ds(pl.multiple_of(source * rows + way * half, half), half), :]

    def origin(way, step):
        return at_pos(pos + 8 - step + way * 2 * step, core)

    def hop(i, way, step, src=None):
        spot = where(i, way, origin(way, step))
        return pltpu.make_async_remote_copy(spot if src is None else src, spot, s_sem.at[i, way, step], r_sem.at[i, way, step + 1],
                                            device_id={'fsdp': peers[way]}, device_id_type=MESH)

    def arrive(i, way, step):
        spot = where(i, way, origin(way, step))
        return pltpu.make_async_remote_copy(spot, spot, s_sem.at[i, way, step], r_sem.at[i, way, step],
                                            device_id={'fsdp': peers[way]}, device_id_type=MESH)

    def share(i, way, step, src=None):
        spot = where(i, way, origin(way, step))
        return pltpu.make_async_remote_copy(spot if src is None else src, spot, ps_sem.at[i, way, step], pr_sem.at[i, way, step],
                                            device_id={'fsdp': partner}, device_id_type=MESH)
    ways = (way0, way1)

    def row_hop(way, step):
        return pltpu.make_async_remote_copy(ways[way].at[step], ways[way].at[step + 1], hs_sem.at[way, step], hr_sem.at[way, step + 1],
                                            device_id={'fsdp': peers[way]}, device_id_type=MESH)

    def fill(way, step, first):
        q = (pos + 7 - step + way * (2 * step + 2)) % RING
        for c in range(0, HALF_TOK, 48):
            lo = way * HALF_TOK + c
            part = own[q, lo:lo + 48, :] + mate[q, lo:lo + 48, :]
            if not first:
                part = part + ways[way][step, c:c + 48, :]
            ways[way][step, c:c + 48, :] = part

    kept = []
    for i in range(n_w):
        loads[i].wait()
        half = W_SHARDS[i][0] // 2
        for way in range(2):
            src = stage[i].at[way * half:(way + 1) * half, :]
            hop(i, way, 0, src).start()
            share(i, way, 0, src).start()
            cp = pltpu.make_async_copy(src, where(i, way, me), own_sem.at[i, way])
            cp.start()
            kept.append(cp)
    for j in (7, 1, 6, 2, 5, 3, 4, 0):
        row_load((pos + j) % RING).wait()
        row_share((pos + j) % RING).wait_recv()
        if j in (7, 1):
            way = 0 if j == 7 else 1
            fill(way, 0, True)
            row_hop(way, 0).start()

    @pl.loop(1, RING)
    def _(step):
        for i in range(n_w):
            for way in range(2):
                arrive(i, way, step).wait_recv()

                @pl.when(step < RING - 1)
                def _():
                    hop(i, way, step).start()
                share(i, way, step).start()
        for way in range(2):
            row_hop(way, step - 1).wait_recv()
            fill(way, step, False)

            @pl.when(step < RING - 1)
            def _():
                row_hop(way, step).start()

    for way in range(2):
        cp = pltpu.make_async_copy(ways[way].at[RING - 1], got_h.at[way * HALF_TOK:(way + 1) * HALF_TOK, :], out_sem.at[way])
        cp.start()
        kept.append(cp)
    for cp in kept:
        cp.wait()

    @pl.loop(0, RING)
    def _(step):
        row_share(step).wait_send()

        @pl.when(step < RING - 1)
        def _():
            for way in range(2):
                row_hop(way, step).wait_send()
        for i in range(n_w):
            for way in range(2):
                @pl.when(step < RING - 1)
                def _():
                    hop(i, way, step).wait_send()
                share(i, way, step).wait()


def spread(rows, shards):
    dma = pltpu.SemaphoreType.DMA
    n_w = len(shards)
    return pl.pallas_call(
        lambda *refs: spread_kernel(n_w, *refs),
        out_shape=(jax.ShapeDtypeStruct((TOK, 2048), BF16),) + tuple(jax.ShapeDtypeStruct((GROUP * r, w), BF16) for r, w in W_SHARDS[:n_w]),
        in_specs=[ANY] * (n_w + 1), out_specs=(ANY,) * (n_w + 1),
        scratch_shapes=[pltpu.VMEM(s, BF16) for s in W_SHARDS[:n_w]] + [pltpu.VMEM((RING, TOK, 2048), BF16)] * 2 + [pltpu.VMEM((RING, HALF_TOK, 2048), BF16)] * 2
        + [dma((n_w,)), dma((n_w, 2))] + [dma((n_w, 2, RING)) for _ in range(4)] + [dma((RING,)) for _ in range(3)] + [dma((2, RING)) for _ in range(2)] + [dma((2,))],
        compiler_params=pltpu.CompilerParams(collective_id=2, has_side_effects=True, vmem_limit_bytes=60 * 1024 * 1024),
        cost_estimate=pl.CostEstimate(flops=8 * 10**9, bytes_accessed=27 * 10**6, transcendentals=0), name='spread',
    )(rows, *shards)


def small_kernel(src, out, loc_sem, s_sem, r_sem):
    me = lax.axis_index('fsdp')
    meet_all(me)
    own = pltpu.make_async_copy(src, out.at[me], loc_sem)
    own.start()

    def send(step):
        return pltpu.make_async_remote_copy(src, out.at[me], s_sem.at[step], r_sem.at[step],
                                            device_id={'fsdp': (me + step) % GROUP}, device_id_type=MESH)
    for step in range(1, GROUP):
        send(step).start()
    for step in range(1, GROUP):
        send(step).wait()
    own.wait()


def small_gather(tile):
    dma = pltpu.SemaphoreType.DMA
    return pl.pallas_call(
        small_kernel, out_shape=jax.ShapeDtypeStruct((GROUP, 8, 128), F32),
        in_specs=[pl.BlockSpec(memory_space=pltpu.VMEM)], out_specs=pl.BlockSpec(memory_space=pltpu.VMEM),
        scratch_shapes=[dma, dma((GROUP,)), dma((GROUP,))],
        compiler_params=pltpu.CompilerParams(collective_id=0, has_side_effects=True),
        cost_estimate=pl.CostEstimate(flops=10**7, bytes_accessed=10**5, transcendentals=0), name='small_gather',
    )(tile)


def blank(shape, dtype):
    return pl.pallas_call(lambda out: None, out_shape=jax.ShapeDtypeStruct(shape, dtype), out_specs=ANY, name='blank')()


def block_step(rows_f32, grad_rows, full_weights, seq_count):
    gain_vec, w_query, w_kv_down, kv_gain, w_kv_up, w_out = full_weights
    kv_rank = kv_gain.shape[0]
    tok_count = rows_f32.shape[0]
    seq_len = tok_count // seq_count
    normed, norm_pull = jax.vjp(rms_scale, rows_f32, gain_vec)
    q_proj = jnp.dot(normed, w_query, preferred_element_type=jnp.float32).astype(jnp.bfloat16)
    kv_down = jnp.dot(normed, w_kv_down, preferred_element_type=jnp.float32).astype(jnp.bfloat16)
    latent, latent_pull = jax.vjp(rms_scale, kv_down[:, :kv_rank], kv_gain)
    kv_up = jnp.dot(latent, w_kv_up, preferred_element_type=jnp.float32).astype(jnp.bfloat16)
    attn_mix, attn_pull = jax.vjp(attend_local, q_proj.reshape(seq_count, seq_len, -1, NOPE_DIM + ROPE_DIM), kv_down[:, kv_rank:].reshape(seq_count, seq_len, ROPE_DIM), kv_up.reshape(seq_count, seq_len, -1, NOPE_DIM + VALUE_DIM))
    mix_rows = attn_mix.reshape(tok_count, -1)
    out_f32 = rows_f32 + jnp.dot(mix_rows, w_out, preferred_element_type=jnp.float32)
    d_mix = lax.dot_general(grad_rows, w_out, COL_DIMS, preferred_element_type=jnp.float32).astype(jnp.bfloat16)
    d_query, d_pe, d_up = attn_pull(d_mix.reshape(attn_mix.shape))
    d_query = d_query.reshape(tok_count, -1)
    d_up = d_up.reshape(tok_count, -1)
    d_latent = lax.dot_general(d_up, w_kv_up, COL_DIMS, preferred_element_type=jnp.float32).astype(jnp.bfloat16)
    d_ckv, d_kv_gain = latent_pull(d_latent)
    d_down = jnp.concatenate([d_ckv, d_pe.reshape(tok_count, ROPE_DIM)], axis=1)
    d_normed = lax.dot_general(d_query, w_query, COL_DIMS, preferred_element_type=jnp.float32)
    d_normed = d_normed + lax.dot_general(d_down, w_kv_down, COL_DIMS, preferred_element_type=jnp.float32)
    d_rows, d_gain = norm_pull(d_normed.astype(jnp.bfloat16))
    d_rows = d_rows + grad_rows.astype(jnp.float32)
    return out_f32.astype(jnp.bfloat16), d_rows, normed, mix_rows, latent, d_query, d_down, d_up, d_gain, d_kv_gain


def solution(mesh):
    tok_spec = P(('dp', 'fsdp'), None)
    seq_spec = P(('dp', 'fsdp'), None, None)
    part_vec = P(('dp', 'fsdp'))
    vec_spec = P('fsdp')
    mat_spec = P('fsdp', None)

    def device_step(tok_ids, grad_out, emb_table, norm_gain, w_query, w_kv_down, kv_gain, w_kv_up, w_out):
        seq_count, seq_len = tok_ids.shape
        vocab_dev, d_model = emb_table.shape
        tok_count = seq_count * seq_len
        me = lax.axis_index('fsdp')
        fill = lambda rows: jnp.pad(rows, ((0, 0), (0, 128 - rows.shape[1])))
        tile = jnp.concatenate([fill(tok_ids.astype(F32)), norm_gain.astype(F32).reshape(1, 128), fill(kv_gain.astype(F32).reshape(1, 32)), jnp.zeros((3, 128), F32)], axis=0)
        table = small_gather(tile)
        all_ids = table[:, :seq_count, :seq_len].reshape(GROUP, tok_count).astype(jnp.int32)
        gain_full = table[:, 3, :].reshape(-1)
        kv_gain_full = table[:, 4, :32].reshape(-1)

        owner = all_ids // vocab_dev
        mine = (owner == me)
        picked = jnp.where(mine.reshape(-1, 1), jnp.take(emb_table, jnp.where(mine, all_ids - me * vocab_dev, 0).reshape(-1), axis=0), jnp.zeros((), BF16))
        tok_rows, full_wq, full_kva, full_kvb, full_wo = spread(picked.reshape(GROUP, tok_count, d_model), (w_query, w_kv_down, w_kv_up, w_out))
        grad_rows = grad_out.reshape(tok_count, d_model)
        block_out, d_rows, normed, mix, latent, d_query, d_down, d_up, d_gain, d_kv_gain = block_step(
            tok_rows.astype(F32), grad_rows, (gain_full, full_wq, full_kva, kv_gain_full, full_kvb, full_wo), seq_count)
        small = jnp.concatenate([d_gain.reshape(GROUP, 1, 128), jnp.pad(d_kv_gain.reshape(GROUP, 1, 32), ((0, 0), (0, 0), (0, 96))), jnp.zeros((GROUP, 6, 128), F32)], axis=1)
        g_out, g_cat, g_up, g_small = grad_shards(mix, grad_rows, normed, jnp.pad(d_down, ((0, 0), (0, D_DOWN - d_down.shape[1]))), d_query, latent.T, d_up, small)
        all_grads = lax.all_gather(d_rows, 'fsdp', tiled=True)
        seg = jnp.where(mine, all_ids - me * vocab_dev, vocab_dev).reshape(-1)
        grad_table = jax.ops.segment_sum(all_grads, seg, num_segments=vocab_dev).astype(jnp.bfloat16)
        return (block_out.reshape(seq_count, seq_len, d_model), grad_table, g_small[0], g_cat[:, D_DOWN:], g_cat[:, :576], g_small[1, :32], g_up, g_out)

    return jax.shard_map(device_step, mesh=mesh, in_specs=(tok_spec, seq_spec, mat_spec, vec_spec, mat_spec, mat_spec, vec_spec, mat_spec, mat_spec), out_specs=(seq_spec, tok_spec, part_vec, tok_spec, tok_spec, part_vec, tok_spec, tok_spec), check_vma=False)
```

time: 1390 us -> 1000 us (0.72)
  waiting for transfers between devices: 888 us -> 0.02 us
  Pallas kernels: 0 us -> 686 us
  blocking collectives: 172 us -> 0 us
  matrix products: 85 us -> 60.3 us
    pallas_call x0 -> x3, Pallas kernels: none -> 686 us  [the longest x1 448 us: grad_shards(): pl.pallas_call(grad_kernel, out_shape=(jax.ShapeDtypeStruct((128, 2048),...]
    reduce_scatter x5 -> x0, waiting for transfers between devices: 636 us -> none  [the longest x4 507 us: device_step(): lax.psum_scatter(full_grad, 'fsdp', scatter_dimension=0, tiled=True)]
    all_gather x4 -> x0, waiting for transfers between devices: 172 us -> none  [device_step(): lax.all_gather(shard_piece, 'fsdp', tiled=True)]
    unnamed x3 -> x0, blocking collectives: 154 us -> none
    all_gather x1, waiting for transfers between devices: 78.1 us -> 0.01 us  [device_step(): all_grads = lax.all_gather(d_rows, 'fsdp', tiled=True)]
    dot_general x4 -> x0, matrix products: 30.8 us -> none  [the longest x1 12 us: block_step(): lax.dot_general(normed, d_query, ROW_DIMS, preferred_element_type=jnp.flo...]
    all_gather x1 -> x0, blocking collectives: 17.8 us -> none  [device_step(): lax.all_gather(shard_piece, 'fsdp', tiled=True)]
    convert_element_type x4 -> x3, other arithmetic: 27.8 us -> 28.9 us  [the longest x1 26.6 us: device_step(): jax.ops.segment_sum(all_grads, seg, num_segments=vocab_dev)]
  transfers between devices with their start and end apart: 10 -> 1, of which waited for: 8 -> 0; matrix products, arithmetic and copies ran while one was open for 18% -> 2% of each run, Pallas kernels for 0% -> 45%
where the time goes in v1:
time: 1000 us; the launch traced here: 993 us
  Pallas kernels  686 us (69%)
  other arithmetic  147 us (15%)
  local copies, waits for them, and re-layouts  85.3 us (9%)
  matrix products  60.3 us (6%)
  between operations  15.3 us (2%)
    pallas_call x1, Pallas kernels, grad_shards(): pl.pallas_call(grad_kernel, out_shape=(jax.ShapeDtypeStruct((128, 2048),...  448 us
    pallas_call x1, Pallas kernels, spread(): pl.pallas_call(lambda *refs: spread_kernel(n_w, *refs), out_shape=(jax.Sh...  228 us
    scatter-add x1, other arithmetic, device_step(): jax.ops.segment_sum(all_grads, seg, num_segments=vocab_dev)  79.1 us
    gather x1, local copies, waits for them, and re-layouts, device_step(): jnp.take(emb_table, jnp.where(mine, all_ids - me * vocab_dev, 0).reshape(...  46.9 us
    convert_element_type x1, other arithmetic, device_step(): jax.ops.segment_sum(all_grads, seg, num_segments=vocab_dev)  26.6 us
  transfers between devices with their start and end apart: 1, of which 0 were waited for; matrix products, arithmetic and copies ran while one was open for 2% of the time, Pallas kernels for 45%

profile of v1, /device:TPU:0, one launch (start us, length us, event | category | flops | bytes accessed | tf_op | source)
XLA Modules:
  0.0 993.4 jit_solution(5839546934618615247)
XLA Ops:
  11.7 10.2 %small_gather.1 = f32[16,8,128]{2,1,0:T(8,128)} custom-call(f32[8,128]{1,0:T(8,128)} %fusion.74.src), custom_call_target="tpu_custom_call" | custom-call | flops 10000000 | bytes 100000 | tf_op jit(solution)/shard_map/small_gather/pallas_call | solution.py:353
  26.7 1.7 copy.41.refs_2_
  28.4 46.9 %gather_fusion = bf16[4608,2048]{1,0:T(8,128)(2,1)} fusion(bf16[6400,2048]{1,0:T(8,128)(2,1)} %param.11, s32[5120]{0:T(1024)S(1)} %pad_clamp_fusion), kind=kCustom, calls=%fused_computation | custom fusion | bytes 37767168 | tf_op jit(solution)/shard_map/jit(_take)/gather | solution.py:414
  75.4 17.5 %select_select_fusion.refs_0_ = bf16[16,288,2048]{2,1,0:T(8,128)(2,1)} fusion(bf16[16,288,2048]{2,1,0:T(8,128)(2,1)} %bitcast.119, pred[16,288]{1,0:T(8,128)(4,1)S(1)} %get-tuple-element.50, pred[16,288]{1,0:T(8,128)(4,1)S(1)} %get-tuple-element.51), kind=kLoop, calls=%fused_computation.4 | loop fusion | flops 18874368 | bytes 37757952 | tf_op jit(solution)/shard_map/jit(_where)/select_n | solution.py:414
  92.9 227.7 %spread.1 = (bf16[288,2048]{1,0:T(8,128)(2,1)}, bf16[2048,3072]{1,0:T(8,128)(2,1)}, bf16[2048,576]{1,0:T(8,128)(2,1)}, bf16[512,4096]{1,0:T(8,128)(2,1)}, bf16[2048,2048]{1,0:T(8,128)(2,1)}) custom-call(bf16[16,288,2048]{2,1,0:T(8,128)(2,1)} %select_select_fusion.refs_0_, bf16[128,3072]{1,0:T(8,128)(2,1)} %refs_1_.1, bf16[128,576]{1,0:T(8,128)(2,1)} %copy.41.refs_2_, ...), custom_call_target="tpu_custom_call" | custom-call | flops 8000000000 | bytes 27000000 | tf_op jit(solution)/shard_map/spread/pallas_call | solution.py:324
  320.6 1.7 fusion.23
  322.9 1.6 fusion.6.nrm_h
  324.5 1.5 convolution_convert_fusion.9
  327.5 20.0 %convolution_convert_fusion.1 = bf16[288,3072]{1,0:T(8,128)(2,1)} fusion(bf16[288,2048]{1,0:T(8,128)(2,1)S(1)} %fusion.6.nrm_h, bf16[2048,3072]{1,0:T(8,128)(2,1)} %get-tuple-element.20), kind=kOutput, calls=%fused_computation.11 | convolution fusion | flops 3624763392 | bytes 15532032 | tf_op jit(solution)/shard_map/dot_general | solution.py:372
  347.5 4.0 reshape.314
  355.2 6.3 fusion.38
  362.1 1.6 copy-done.4
  363.8 1.5 convolution_convert_fusion
  372.0 1.3 fusion.16
  373.3 1.5 fusion.35
  374.8 2.2 fusion.34
  379.9 1.4 copy.59
  382.5 3.8 fusion.56
  387.6 1.6 reshape.321
  392.0 1.5 copy.58
  393.6 3.4 reshape.319.dq_h
  397.0 7.5 fusion.87
  405.7 1.7 fusion.10
  407.4 2.2 fusion.22
  409.7 1.6 copy-done.2
  411.3 2.0 fusion.36
  413.8 1.3 copy.117
  417.0 447.7 %grad_shards.1 = (f32[128,2048]{1,0:T(8,128)}, f32[128,3712]{1,0:T(8,128)}, f32[32,4096]{1,0:T(8,128)}, f32[8,128]{1,0:T(8,128)}) custom-call(bf16[288,2048]{1,0:T(8,128)(2,1)} %bitcast.131, bf16[288,2048]{1,0:T(8,128)(2,1)} %bitcast.128, bf16[288,2048]{1,0:T(8,128)(2,1)} %copy-done.12, bf16[288,640]{1,0:T(8,128)(2,1)} %pad.54.clone.dd_h, ...), custom_call_target="tpu_custom_call" | custom-call | flops 8000000000 | bytes 20000000 | tf_op jit(solution)/shard_map/grad_shards/pallas_call | solution.py:180
  865.7 2.7 slice.65
  871.7 7.0 fusion.5
  878.7 79.1 %scatter_custom_fusion = f32[6400,2048]{1,0:T(8,128)} fusion(s32[4608]{0:T(1024)} %get-tuple-element.46, f32[4608,2048]{1,0:T(8,128)} %all-gather.2.cloned.1.call-done, f32[]{:T(128)} %constant.21.clone.1), kind=kCustom, calls=%fused_computation.2 | custom fusion | flops 9437184 | bytes 52429312 | tf_op jit(solution)/shard_map/scatter-add | solution.py:423
  957.8 26.6 %convert_element_type.204 = bf16[6400,2048]{1,0:T(8,128)(2,1)} convert(f32[6400,2048]{1,0:T(8,128)} %scatter_custom_fusion) | non-fusion elementwise | flops 13107200 | bytes 78643200 | tf_op jit(solution)/shard_map/convert_element_type | solution.py:423
  (162 shorter events, 39.8 us)
Async XLA Ops:
  7.2 871.5 %all-gather.2.cloned.1.call-start = ((), (), s32[]{:S(2)}) async-start(), calls=%async_computation | async-start | bytes 40108032 | tf_op jit(solution)/shard_map/all_gather | solution.py:421
  320.6 4.0 copy-start.40
  324.5 2.9 copy-start.12
  353.2 14.2 %copy-start.16 = (f32[96,64]{1,0:T(8,128)}, f32[96,64]{1,0:T(8,128)S(1)}, u32[]{:S(2)}) copy-start(f32[96,64]{1,0:T(8,128)S(1)} %get-tuple-element.66) | copy-start | bytes 73732
  353.2 14.2 %copy-start.18 = (f32[96,64]{1,0:T(8,128)}, f32[96,64]{1,0:T(8,128)S(1)}, u32[]{:S(2)}) copy-start(f32[96,64]{1,0:T(8,128)S(1)} %get-tuple-element.67) | copy-start | bytes 73732
  353.3 15.0 %copy-start.22 = (f32[96,64]{0,1:T(8,128)}, f32[96,64]{0,1:T(8,128)S(1)}, u32[]{:S(2)}) copy-start(f32[96,64]{0,1:T(8,128)S(1)} %copy.46) | copy-start | bytes 73732
  353.5 8.6 copy-start.32
  361.5 2.2 copy-start.4
  361.8 2.1 copy-start.6
  366.5 5.5 copy-start.13
  370.8 4.0 copy-start.1
  370.8 6.2 copy-start.25
  371.3 5.7 copy-start.24
  374.8 2.2 copy-start.28
  382.4 3.9 copy-start.8
  382.4 3.9 copy-start.36
  382.5 4.5 copy-start.23
  397.0 7.6 copy-start.7
  397.0 7.6 copy-start.20
  397.0 7.6 copy-start.37
  397.0 8.7 copy-start
  397.0 8.6 copy-start.26
  397.0 8.6 copy-start.31
  397.0 8.6 copy-start.41
  405.6 1.7 copy-start.9
  405.7 1.7 copy-start.35
  405.7 1.7 copy-start.11
  413.3 1.8 copy-start.38
  413.3 1.9 copy-start.10
  413.3 1.9 copy-start.27
  957.8 26.6 %copy-start.21 = (f32[32,4096]{1,0:T(8,128)S(1)}, f32[32,4096]{1,0:T(8,128)}, u32[]{:S(2)}) copy-start(f32[32,4096]{1,0:T(8,128)} %get-tuple-element.93) | copy-start | bytes 1572868
  957.8 27.4 %copy-start.15 = (f32[128,2048]{1,0:T(8,128)S(1)}, f32[128,2048]{1,0:T(8,128)}, u32[]{:S(2)}) copy-start(f32[128,2048]{1,0:T(8,128)} %get-tuple-element.94) | copy-start | bytes 3145732
  (11 other events, 12.7 us)
Sparse Core Ops, SparseCore 0:
  409.7 358.5 all-gather.1

commit v2 on v1

--- a/solution.py
+++ b/solution.py
@@ -82,33 +82,49 @@
 TOK = 288
 D_OUT, D_CAT, D_UP, D_DOWN = 2048, 3712, 4096, 640
 CUT = 1792
-PARTS = (('o', 0, 0, 1024), ('o', 1, 1024, 1024), ('n', 0, 0, CUT), ('n', 1, CUT, D_CAT - CUT), ('u', 0, 0, 2048), ('u', 1, 2048, 2048))
-ROWS = {'o': 128, 'n': 128, 'u': 32}
+PARTS = (('u', 0, 0, 2048), ('u', 1, 2048, 2048), ('n', 0, 0, CUT), ('n', 1, CUT, D_CAT - CUT))
+N_PARTS = len(PARTS)
+ROWS = {'n': 128, 'u': 32}
 
 def col_tiles(width):
     step = 512
     return [(c, min(step, width - c)) for c in range(0, width, step)]
 
-def grad_kernel(mix_h, dy_h, nrm_h, dd_h, dq_h, lat_h, du_h, sm_h, go_h, gn_h, gu_h, gs_h,
-                mix, dy, nrm, cat, lat, du, b0, b1, b2, b3, b4, b5, smr, ssum, loc_sem, xs_sem, xr_sem, s_sem, r_sem, ms_sem, mr_sem, out_sem):
+def grad_kernel(mix_h, dy_h, nrm_h, dd_h, dq_h, lat_h, du_h, sm_h, go_h, gq_h, gd_h, gu_h, gs_h,
+                mix, dy, go, nrm, cat, lat, du, b0, b1, b2, b3, smr, ssum, loc_sem, xs_sem, xr_sem, s_sem, r_sem, ms_sem, mr_sem, cs_sem, cr_sem, dy_sem, out_sem):
     me, core, pos = place()
     partner = me + 1 - 2 * core
     meet_all(me)
-    acts = ((mix_h, mix), (dy_h, dy), (nrm_h, nrm), (dd_h, cat.at[:, :, 0:D_DOWN]), (dq_h, cat.at[:, :, D_DOWN:D_CAT]), (lat_h, lat), (du_h, du))
+    acts = ((lat_h, lat), (du_h, du), (nrm_h, nrm), (dd_h, cat.at[:, :, 0:D_DOWN]), (dq_h, cat.at[:, :, D_DOWN:D_CAT]))
     local, cross = [], []
     for i, (src, dst) in enumerate(acts):
-        cp = pltpu.make_async_copy(src, dst.at[core], loc_sem.at[i]); cp.start(); local.append(cp)
+        cp = pltpu.make_async_copy(src, dst.at[core], loc_sem.at[i])
+        cp.start()
+        local.append(cp)
         rc = pltpu.make_async_remote_copy(src, dst.at[core], xs_sem.at[i], xr_sem.at[i], device_id={'fsdp': partner}, device_id_type=MESH)
-        rc.start(); cross.append(rc)
-    own_small = pltpu.make_async_copy(sm_h.at[me], smr.at[0], loc_sem.at[7]); own_small.start()
-    smalls = []
+        rc.start()
+        cross.append(rc)
+    own_small = pltpu.make_async_copy(sm_h.at[me], smr.at[0], loc_sem.at[5])
+    own_small.start()
+    own_mix = pltpu.make_async_copy(mix_h.at[:, pl.ds(pl.multiple_of(me * 128, 128), 128)], mix.at[me], loc_sem.at[6])
+    own_mix.start()
+    smalls, mixes = [], []
     for i in range(1, GROUP):
         peer = (me + i) % GROUP
         rc = pltpu.make_async_remote_copy(sm_h.at[peer], smr.at[i], ms_sem.at[i], mr_sem.at[i], device_id={'fsdp': peer}, device_id_type=MESH)
-        rc.start(); smalls.append(rc)
-    bufs = (b0, b1, b2, b3, b4, b5)
+        rc.start()
+        smalls.append(rc)
+    bufs = (b0, b1, b2, b3)
     peers = (at_pos(pos + 1, core), at_pos(pos + 7, core))
-    left_ops = {'o': (mix, dy), 'n': (nrm, cat), 'u': (lat, du)}
+    left_ops = {'n': (nrm, cat), 'u': (lat, du)}
+
+    def mix_send(i):
+        peer = (me + i) % GROUP
+        return pltpu.make_async_remote_copy(mix_h.at[:, pl.ds(pl.multiple_of(peer * 128, 128), 128)], mix.at[me], cs_sem.at[i], cr_sem.at[i],
+                                            device_id={'fsdp': peer}, device_id_type=MESH)
+
+    def dy_load(blk):
+        return pltpu.make_async_copy(dy_h.at[pl.ds(pl.multiple_of(blk * TOK, TOK), TOK), :], dy.at[blk % 2], dy_sem.at[blk % 2])
 
     def hop(p, step):
         return pltpu.make_async_remote_copy(bufs[p].at[step], bufs[p].at[step + 1], s_sem.at[p, step], r_sem.at[p, step + 1],
@@ -133,71 +149,102 @@
             else:
                 bufs[p][step, :, c:c + w] = bufs[p][step, :, c:c + w] + part
 
-    need = {'o': (0, 1), 'n': (2, 3, 4), 'u': (5, 6)}
-    for p in range(6):
+    need = {'u': (0, 1), 'n': (2, 3, 4)}
+    for p in range(N_PARTS):
         if PARTS[p][1] == 0:
             for i in need[PARTS[p][0]]:
-                local[i].wait(); cross[i].wait_recv()
+                local[i].wait()
+                cross[i].wait_recv()
         work(p, 0, True)
         hop(p, 0).start()
+    for i in range(1, GROUP):
+        mix_send(i).start()
+    dy_load(0).start()
+    own_mix.wait()
+    for i in range(1, GROUP):
+        mix_send(i).wait()
+    go[...] = jnp.zeros_like(go)
 
     @pl.loop(1, RING - 1)
     def _(step):
-        for p in range(6):
+        for p in range(N_PARTS):
             hop(p, step - 1).wait_recv()
             work(p, step, False)
             hop(p, step).start()
 
+        @pl.when(step < 5)
+        def _():
+            @pl.loop(0, 4)
+            def _(j):
+                blk = (step - 1) * 4 + j
+                dy_load(blk).wait()
+
+                @pl.when(blk < GROUP - 1)
+                def _():
+                    dy_load(blk + 1).start()
+                for c, w in col_tiles(D_OUT):
+                    go[:, c:c + w] += lax.dot_general(mix[blk], dy[blk % 2, :, c:c + w], (((0,), (0,)), ((), ())), preferred_element_type=F32)
+
     last = RING - 1
     outs = []
-    targets = (go_h.at[:, 0:1024], go_h.at[:, 1024:2048], gn_h.at[:, 0:CUT], gn_h.at[:, CUT:D_CAT], gu_h.at[:, 0:2048], gu_h.at[:, 2048:4096])
-    for p in range(6):
+    cp = pltpu.make_async_copy(go, go_h, out_sem.at[7])
+    cp.start()
+    outs.append(cp)
+    cut_q = CUT - D_DOWN
+    targets = ((gu_h.at[:, 0:2048], 0, 2048),), ((gu_h.at[:, 2048:4096], 0, 2048),), ((gd_h, 0, D_DOWN), (gq_h.at[:, 0:cut_q], D_DOWN, CUT)), ((gq_h.at[:, cut_q:3072], 0, D_CAT - CUT),)
+    for p in range(N_PARTS):
         hop(p, last - 1).wait_recv()
         work(p, last, False)
-        cp = pltpu.make_async_copy(bufs[p].at[last], targets[p], out_sem.at[p]); cp.start(); outs.append(cp)
+        for n, (dst, c0, c1) in enumerate(targets[p]):
+            cp = pltpu.make_async_copy(bufs[p].at[last, :, c0:c1], dst, out_sem.at[p + 4 * n])
+            cp.start()
+            outs.append(cp)
     own_small.wait()
     for rc in smalls:
         rc.wait()
     ssum[...] = jnp.sum(smr[...], axis=0)
-    cp = pltpu.make_async_copy(ssum, gs_h, out_sem.at[6]); cp.start(); outs.append(cp)
+    cp = pltpu.make_async_copy(ssum, gs_h, out_sem.at[4])
+    cp.start()
+    outs.append(cp)
     for rc in cross:
         rc.wait_send()
-    for p in range(6):
+    for p in range(N_PARTS):
         @pl.loop(0, last)
         def _(step):
             hop(p, step).wait_send()
     for cp in outs:
         cp.wait()
 
-def grad_shards(mix, dy, nrm, dd, dq, lat_t, du, small):
+
+def grad_shards(mix, dy_all, nrm, dd, dq, lat_t, du, small):
     shapes = [(ROWS[k], RING, w) for k, _, _, w in PARTS]
-    scratch = [pltpu.VMEM((2, TOK, 2048), BF16), pltpu.VMEM((2, TOK, 2048), BF16), pltpu.VMEM((2, TOK, 2048), BF16),
+    scratch = [pltpu.VMEM((GROUP, TOK, 128), BF16), pltpu.VMEM((2, TOK, 2048), BF16), pltpu.VMEM((128, 2048), F32), pltpu.VMEM((2, TOK, 2048), BF16),
                pltpu.VMEM((2, TOK, D_CAT), BF16), pltpu.VMEM((2, 512, TOK), BF16), pltpu.VMEM((2, TOK, D_UP), BF16)]
     scratch += [pltpu.VMEM((RING, r, w), F32) for r, _, w in shapes]
     scratch += [pltpu.VMEM((GROUP, 8, 128), F32), pltpu.VMEM((8, 128), F32)]
     dma = pltpu.SemaphoreType.DMA
-    scratch += [dma((8,)), dma((7,)), dma((7,)), dma((6, RING)), dma((6, RING)), dma((GROUP,)), dma((GROUP,)), dma((7,))]
+    scratch += [dma((7,)), dma((5,)), dma((5,)), dma((N_PARTS, RING)), dma((N_PARTS, RING)), dma((GROUP,)), dma((GROUP,)), dma((GROUP,)), dma((GROUP,)), dma((2,)), dma((8,))]
     return pl.pallas_call(
         grad_kernel,
-        out_shape=(jax.ShapeDtypeStruct((128, 2048), F32), jax.ShapeDtypeStruct((128, D_CAT), F32), jax.ShapeDtypeStruct((32, D_UP), F32), jax.ShapeDtypeStruct((8, 128), F32)),
-        in_specs=[ANY] * 8, out_specs=(ANY,) * 4, scratch_shapes=scratch,
+        out_shape=(jax.ShapeDtypeStruct((128, 2048), F32), jax.ShapeDtypeStruct((128, 3072), F32), jax.ShapeDtypeStruct((128, D_DOWN), F32), jax.ShapeDtypeStruct((32, D_UP), F32), jax.ShapeDtypeStruct((8, 128), F32)),
+        in_specs=[ANY] * 8, out_specs=(ANY,) * 5, scratch_shapes=scratch,
         compiler_params=pltpu.CompilerParams(collective_id=1, has_side_effects=True, vmem_limit_bytes=60 * 1024 * 1024),
         cost_estimate=pl.CostEstimate(flops=8 * 10**9, bytes_accessed=20 * 10**6, transcendentals=0), name='grad_shards',
-    )(mix, dy, nrm, dd, dq, lat_t, du, small)
-
-
-W_SHARDS = ((128, 3072), (128, 576), (32, 4096), (128, 2048))
+    )(mix, dy_all, nrm, dd, dq, lat_t, du, small)
+
+
+W_SHARDS = ((32, 4096),)
 HALF_TOK = TOK // 2
 
 
 def spread_kernel(n_w, *refs):
-    rows_h = refs[0]
-    srcs = refs[1:1 + n_w]
-    got_h = refs[1 + n_w]
-    outs = refs[2 + n_w:2 + 2 * n_w]
-    stage = refs[2 + 2 * n_w:2 + 3 * n_w]
-    own, mate, way0, way1 = refs[2 + 3 * n_w:6 + 3 * n_w]
-    in_sem, own_sem, s_sem, r_sem, ps_sem, pr_sem, h_in, m_s, m_r, hs_sem, hr_sem, out_sem = refs[6 + 3 * n_w:]
+    mask, rows_h = refs[0:2]
+    srcs = refs[2:2 + n_w]
+    got_h = refs[2 + n_w]
+    outs = refs[3 + n_w:3 + 2 * n_w]
+    stage = refs[3 + 2 * n_w:3 + 3 * n_w]
+    own, mate, way0, way1 = refs[3 + 3 * n_w:7 + 3 * n_w]
+    in_sem, own_sem, s_sem, r_sem, ps_sem, pr_sem, h_in, m_s, m_r, hs_sem, hr_sem, out_sem = refs[7 + 3 * n_w:]
     me, core, pos = place()
     partner = me + 1 - 2 * core
     barrier = pltpu.get_barrier_semaphore()
@@ -251,12 +298,15 @@
 
     def fill(way, step, first):
         q = (pos + 7 - step + way * (2 * step + 2)) % RING
+        chip = chip_at(q)
         for c in range(0, HALF_TOK, 48):
             lo = way * HALF_TOK + c
-            part = own[q, lo:lo + 48, :] + mate[q, lo:lo + 48, :]
-            if not first:
-                part = part + ways[way][step, c:c + 48, :]
-            ways[way][step, c:c + 48, :] = part
+            mine, theirs = mask[0, chip, lo:lo + 48, :], mask[1, chip, lo:lo + 48, :]
+            for w in range(0, 2048, 128):
+                part = own[q, lo:lo + 48, w:w + 128] * mine + mate[q, lo:lo + 48, w:w + 128] * theirs
+                if not first:
+                    part = part + ways[way][step, c:c + 48, w:w + 128]
+                ways[way][step, c:c + 48, w:w + 128] = part
 
     kept = []
     for i in range(n_w):
@@ -318,18 +368,116 @@
                 share(i, way, step).wait()
 
 
-def spread(rows, shards):
+def spread(mask, rows, shards):
     dma = pltpu.SemaphoreType.DMA
     n_w = len(shards)
     return pl.pallas_call(
         lambda *refs: spread_kernel(n_w, *refs),
-        out_shape=(jax.ShapeDtypeStruct((TOK, 2048), BF16),) + tuple(jax.ShapeDtypeStruct((GROUP * r, w), BF16) for r, w in W_SHARDS[:n_w]),
-        in_specs=[ANY] * (n_w + 1), out_specs=(ANY,) * (n_w + 1),
-        scratch_shapes=[pltpu.VMEM(s, BF16) for s in W_SHARDS[:n_w]] + [pltpu.VMEM((RING, TOK, 2048), BF16)] * 2 + [pltpu.VMEM((RING, HALF_TOK, 2048), BF16)] * 2
-        + [dma((n_w,)), dma((n_w, 2))] + [dma((n_w, 2, RING)) for _ in range(4)] + [dma((RING,)) for _ in range(3)] + [dma((2, RING)) for _ in range(2)] + [dma((2,))],
+        out_shape=(jax.ShapeDtypeStruct((TOK, 2048), BF16),) + tuple(jax.ShapeDtypeStruct((GROUP * r, w), BF16) for r, w in W_SHARDS),
+        in_specs=[pl.BlockSpec(memory_space=pltpu.VMEM)] + [ANY] * (n_w + 1), out_specs=(ANY,) * (n_w + 1),
+        scratch_shapes=[pltpu.VMEM(s, BF16) for s in W_SHARDS] + [pltpu.VMEM((RING, TOK, 2048), BF16)] * 2 + [pltpu.VMEM((RING, HALF_TOK, 2048), BF16)] * 2
+        + [dma((max(n_w, 1),)), dma((max(n_w, 1), 2))] + [dma((max(n_w, 1), 2, RING)) for _ in range(4)] + [dma((RING,)) for _ in range(3)] + [dma((2, RING)) for _ in range(2)] + [dma((2,))],
         compiler_params=pltpu.CompilerParams(collective_id=2, has_side_effects=True, vmem_limit_bytes=60 * 1024 * 1024),
         cost_estimate=pl.CostEstimate(flops=8 * 10**9, bytes_accessed=27 * 10**6, transcendentals=0), name='spread',
-    )(rows, *shards)
+    )(mask, rows, *shards)
+ROW_BLK = 128
+IN_BLK = 144
+SUB = 48
+PIECE = 16
+IN_SLOTS = 4
+OUT_SLOTS = 4
+
+
+def table_kernel(starts, toks, rows, flags, gain, dy_h, dn_h, h_h, out_h, grad, dy, dn, hh, acc, ob, nil, in_sem, out_sem):
+    n_in = GROUP * TOK // IN_BLK
+    n_out = out_h.shape[0] // ROW_BLK
+
+    def loads(blk):
+        span = pl.ds(pl.multiple_of(blk * IN_BLK, IN_BLK), IN_BLK)
+        slot = blk % IN_SLOTS
+        return [pltpu.make_async_copy(src.at[span, :], dst.at[slot], in_sem.at[i, slot]) for i, (src, dst) in enumerate(((dy_h, dy), (dn_h, dn), (h_h, hh)))]
+    for blk in range(IN_SLOTS - 1):
+        for cp in loads(blk):
+            cp.start()
+
+    @pl.loop(0, n_in)
+    def _(blk):
+        slot = blk % IN_SLOTS
+        for cp in loads(blk):
+            cp.wait()
+
+        @pl.when(blk < n_in - IN_SLOTS + 1)
+        def _():
+            for cp in loads(blk + IN_SLOTS - 1):
+                cp.start()
+
+        @pl.loop(0, IN_BLK // SUB)
+        def _(g):
+            @pl.when(flags[blk * (IN_BLK // SUB) + g] > 0)
+            def _():
+                r0 = pl.multiple_of(g * SUB, PIECE)
+                o0 = pl.multiple_of(blk * IN_BLK + g * SUB, PIECE)
+                pieces = range(0, SUB, PIECE)
+
+                def tile(ref, p, c):
+                    return ref[slot, pl.ds(r0 + p, PIECE), c:c + 128].astype(F32)
+                scale = []
+                for p in pieces:
+                    sq = jnp.zeros((PIECE, 128), F32)
+                    al = jnp.zeros((PIECE, 128), F32)
+                    for c in range(0, 2048, 128):
+                        h = tile(hh, p, c)
+                        sq = sq + h * h
+                        al = al + h * (tile(dn, p, c) * gain[:, c:c + 128])
+                    scale.append((jnp.sum(sq, axis=1, keepdims=True), jnp.sum(al, axis=1, keepdims=True)))
+                for p, (sq, al) in zip(pieces, scale):
+                    inv = lax.rsqrt(sq * (1.0 / 2048) + RMS_EPS)
+                    coef = inv * inv * inv * (al * (1.0 / 2048))
+                    for c in range(0, 2048, 128):
+                        s = tile(dn, p, c) * gain[:, c:c + 128]
+                        grad[pl.ds(o0 + p, PIECE), c:c + 128] = tile(dy, p, c) + inv * s - coef * tile(hh, p, c)
+
+    def store(blk, src):
+        return pltpu.make_async_copy(src, out_h.at[pl.ds(pl.multiple_of(blk * ROW_BLK, ROW_BLK), ROW_BLK), :], out_sem.at[blk % OUT_SLOTS])
+    nil[...] = jnp.zeros_like(nil)
+
+    @pl.loop(0, n_out)
+    def _(blk):
+        first, last = starts[blk], starts[blk + 1]
+        slot = blk % OUT_SLOTS
+
+        @pl.when(blk >= OUT_SLOTS)
+        def _():
+            store(blk - OUT_SLOTS, nil).wait()
+
+        @pl.when(first == last)
+        def _():
+            store(blk, nil).start()
+
+        @pl.when(first < last)
+        def _():
+            acc[...] = jnp.zeros_like(acc)
+
+            @pl.loop(first, last)
+            def _(k):
+                r = rows[k]
+                acc[pl.ds(r, 1), :] += grad[pl.ds(toks[k], 1), :]
+            ob[slot] = acc[...].astype(BF16)
+            store(blk, ob.at[slot]).start()
+    for blk in range(n_out - OUT_SLOTS, n_out):
+        store(blk, nil).wait()
+
+
+def table_grad(starts, toks, rows, flags, gain, dy_all, dn_all, picked, vocab_dev):
+    smem = pl.BlockSpec(memory_space=pltpu.SMEM)
+    dma = pltpu.SemaphoreType.DMA
+    return pl.pallas_call(
+        table_kernel, out_shape=jax.ShapeDtypeStruct((vocab_dev, 2048), BF16),
+        in_specs=[smem] * 4 + [pl.BlockSpec(memory_space=pltpu.VMEM)] + [ANY] * 3, out_specs=ANY,
+        scratch_shapes=[pltpu.VMEM((GROUP * TOK, 2048), F32)] + [pltpu.VMEM((IN_SLOTS, IN_BLK, 2048), BF16)] * 3 + [pltpu.VMEM((ROW_BLK, 2048), F32), pltpu.VMEM((OUT_SLOTS, ROW_BLK, 2048), BF16), pltpu.VMEM((ROW_BLK, 2048), BF16), dma((3, IN_SLOTS)), dma((OUT_SLOTS,))],
+        compiler_params=pltpu.CompilerParams(vmem_limit_bytes=60 * 1024 * 1024),
+        cost_estimate=pl.CostEstimate(flops=10**9, bytes_accessed=80 * 10**6, transcendentals=0), name='table_grad',
+    )(starts, toks, rows, flags, gain, dy_all, dn_all, picked)
 
 
 def small_kernel(src, out, loc_sem, s_sem, r_sem):
@@ -385,9 +533,9 @@
     d_down = jnp.concatenate([d_ckv, d_pe.reshape(tok_count, ROPE_DIM)], axis=1)
     d_normed = lax.dot_general(d_query, w_query, COL_DIMS, preferred_element_type=jnp.float32)
     d_normed = d_normed + lax.dot_general(d_down, w_kv_down, COL_DIMS, preferred_element_type=jnp.float32)
-    d_rows, d_gain = norm_pull(d_normed.astype(jnp.bfloat16))
-    d_rows = d_rows + grad_rows.astype(jnp.float32)
-    return out_f32.astype(jnp.bfloat16), d_rows, normed, mix_rows, latent, d_query, d_down, d_up, d_gain, d_kv_gain
+    d_normed = d_normed.astype(jnp.bfloat16)
+    _, d_gain = norm_pull(d_normed)
+    return out_f32.astype(jnp.bfloat16), d_normed, normed, mix_rows, latent, d_query, d_down, d_up, d_gain, d_kv_gain
 
 
 def solution(mesh):
@@ -402,6 +550,8 @@
         vocab_dev, d_model = emb_table.shape
         tok_count = seq_count * seq_len
         me = lax.axis_index('fsdp')
+        grad_rows = grad_out.reshape(tok_count, d_model)
+        bundle = lax.all_gather(jnp.concatenate([w_query, w_out, w_kv_down], axis=1), 'fsdp', tiled=True)
         fill = lambda rows: jnp.pad(rows, ((0, 0), (0, 128 - rows.shape[1])))
         tile = jnp.concatenate([fill(tok_ids.astype(F32)), norm_gain.astype(F32).reshape(1, 128), fill(kv_gain.astype(F32).reshape(1, 32)), jnp.zeros((3, 128), F32)], axis=0)
         table = small_gather(tile)
@@ -411,16 +561,27 @@
 
         owner = all_ids // vocab_dev
         mine = (owner == me)
-        picked = jnp.where(mine.reshape(-1, 1), jnp.take(emb_table, jnp.where(mine, all_ids - me * vocab_dev, 0).reshape(-1), axis=0), jnp.zeros((), BF16))
-        tok_rows, full_wq, full_kva, full_kvb, full_wo = spread(picked.reshape(GROUP, tok_count, d_model), (w_query, w_kv_down, w_kv_up, w_out))
-        grad_rows = grad_out.reshape(tok_count, d_model)
-        block_out, d_rows, normed, mix, latent, d_query, d_down, d_up, d_gain, d_kv_gain = block_step(
+        local = all_ids - me * vocab_dev
+        keys = lax.sort(jnp.where(mine, local * 8192 + jnp.arange(GROUP * tok_count).reshape(GROUP, tok_count), 2**30).reshape(-1))
+        starts = jnp.sum((mine & (local < ROW_BLK * jnp.arange(vocab_dev // ROW_BLK + 1)[:, None, None])).astype(jnp.int32), axis=(1, 2))
+        flags = jnp.sum(mine.reshape(-1, SUB).astype(jnp.int32), axis=1)
+        picked = jnp.take(emb_table, jnp.where(mine, local, 0).reshape(-1), axis=0, mode='clip')
+        core = me % 2
+        near = lax.dynamic_index_in_dim(owner.reshape(RING, 2, tok_count), core, 1, keepdims=False)
+        mask = jnp.stack([near == me, near == me + 1 - 2 * core]).astype(BF16)
+        mask = jnp.broadcast_to(mask[..., None], (2, RING, tok_count, 128))
+        picked, keys, starts, flags = lax.optimization_barrier((picked, keys, starts, flags))
+        tok_rows, full_kvb = spread(mask, picked.reshape(GROUP, tok_count, d_model), (w_kv_up,))
+        full_wq, full_wo, full_kva = bundle[:, :3072], bundle[:, 3072:5120], bundle[:, 5120:]
+        tok_rows, grad_rows = lax.optimization_barrier((tok_rows, grad_rows))
+        all_dy = lax.all_gather(grad_rows, 'fsdp', tiled=True)
+        block_out, d_normed, normed, mix, latent, d_query, d_down, d_up, d_gain, d_kv_gain = block_step(
             tok_rows.astype(F32), grad_rows, (gain_full, full_wq, full_kva, kv_gain_full, full_kvb, full_wo), seq_count)
+        all_dn = lax.all_gather(d_normed, 'fsdp', tiled=True)
         small = jnp.concatenate([d_gain.reshape(GROUP, 1, 128), jnp.pad(d_kv_gain.reshape(GROUP, 1, 32), ((0, 0), (0, 0), (0, 96))), jnp.zeros((GROUP, 6, 128), F32)], axis=1)
-        g_out, g_cat, g_up, g_small = grad_shards(mix, grad_rows, normed, jnp.pad(d_down, ((0, 0), (0, D_DOWN - d_down.shape[1]))), d_query, latent.T, d_up, small)
-        all_grads = lax.all_gather(d_rows, 'fsdp', tiled=True)
-        seg = jnp.where(mine, all_ids - me * vocab_dev, vocab_dev).reshape(-1)
-        grad_table = jax.ops.segment_sum(all_grads, seg, num_segments=vocab_dev).astype(jnp.bfloat16)
-        return (block_out.reshape(seq_count, seq_len, d_model), grad_table, g_small[0], g_cat[:, D_DOWN:], g_cat[:, :576], g_small[1, :32], g_up, g_out)
+        block_out, mix = lax.optimization_barrier((block_out, mix))
+        g_out, g_query, g_down, g_up, g_small = grad_shards(mix, all_dy, normed, jnp.pad(d_down, ((0, 0), (0, D_DOWN - d_down.shape[1]))), d_query, latent.T, d_up, small)
+        grad_table = table_grad(starts, keys & 8191, (keys >> 13) & (ROW_BLK - 1), flags, gain_full.reshape(1, -1), all_dy, all_dn, picked, vocab_dev)
+        return (block_out.reshape(seq_count, seq_len, d_model), grad_table, g_small[0], g_query, g_down[:, :576], g_small[1, :32], g_up, g_out)
 
     return jax.shard_map(device_step, mesh=mesh, in_specs=(tok_spec, seq_spec, mat_spec, vec_spec, mat_spec, mat_spec, vec_spec, mat_spec, mat_spec), out_specs=(seq_spec, tok_spec, part_vec, tok_spec, tok_spec, part_vec, tok_spec, tok_spec), check_vma=False)

time: 1000 us -> 736 us (0.74)
  Pallas kernels: 686 us -> 524 us
  other arithmetic: 147 us -> 27.6 us
    pallas_call x1, Pallas kernels: 448 us -> 297 us  [grad_shards(): pl.pallas_call(grad_kernel, out_shape=(jax.ShapeDtypeStruct((128, 2048),...]
    scatter-add x1 -> x0, other arithmetic: 79.1 us -> none  [device_step(): jax.ops.segment_sum(all_grads, seg, num_segments=vocab_dev)]
    pallas_call x1, Pallas kernels: 228 us -> 161 us  [spread(): pl.pallas_call(lambda *refs: spread_kernel(n_w, *refs), out_shape=(jax.Sh...]
    pallas_call x0 -> x1, Pallas kernels: none -> 55.8 us  [table_grad(): pl.pallas_call(table_kernel, out_shape=jax.ShapeDtypeStruct((vocab_dev, 2...]
    convert_element_type x1, other arithmetic: 26.6 us -> 0.01 us  [device_step(): mask = jnp.stack([near == me, near == me + 1 - 2 * core]).astype(BF16)]
    select_n x2, other arithmetic: 18.2 us -> 0.09 us  [the longest x1 0.08 us: device_step(): jnp.where(mine, local, 0).reshape(-1)]
    dot_general x3, matrix products: 4.03 us -> 15.8 us  [attend_local(): jnp.einsum('bhst,bthd->bshd', attn_probs, kv_up[..., NOPE_DIM:], preferre...]
    dot_general x1, matrix products: 20 us -> 9.6 us  [block_step(): jnp.dot(normed, w_query, preferred_element_type=jnp.float32)]
  transfers between devices with their start and end apart: 1 -> 3, of which waited for: 0 -> 0; matrix products, arithmetic and copies ran while one was open for 2% -> 24% of each run, Pallas kernels for 45% -> 64%
where the time goes in v2:
time: 736 us; the launch traced here: 726 us
  Pallas kernels  524 us (71%)
  local copies, waits for them, and re-layouts  89.8 us (12%)
  matrix products  69.4 us (9%)
  other arithmetic  27.6 us (4%)
  between operations  15.1 us (2%)
    pallas_call x1, Pallas kernels, grad_shards(): pl.pallas_call(grad_kernel, out_shape=(jax.ShapeDtypeStruct((128, 2048),...  297 us
    pallas_call x1, Pallas kernels, spread(): pl.pallas_call(lambda *refs: spread_kernel(n_w, *refs), out_shape=(jax.Sh...  161 us
    pallas_call x1, Pallas kernels, table_grad(): pl.pallas_call(table_kernel, out_shape=jax.ShapeDtypeStruct((vocab_dev, 2...  55.8 us
    gather x1, local copies, waits for them, and re-layouts, device_step(): jnp.take(emb_table, jnp.where(mine, local, 0).reshape(-1), axis=0, mode='...  46.9 us
    unnamed x105, local copies, waits for them, and re-layouts  17 us
    dot_general x3, matrix products, attend_local(): jnp.einsum('bhst,bthd->bshd', attn_probs, kv_up[..., NOPE_DIM:], preferre...  15.8 us
  transfers between devices with their start and end apart: 3, of which 0 were waited for; matrix products, arithmetic and copies ran while one was open for 24% of the time, Pallas kernels for 64%

profile of v2, /device:TPU:0, one launch (start us, length us, event | category | flops | bytes accessed | tf_op | source)
XLA Modules:
  0.0 726.0 jit_solution(299773709558380891)
XLA Ops:
  8.3 2.5 pad_maximum_fusion
  11.7 10.2 %small_gather.1 = f32[16,8,128]{2,1,0:T(8,128)} custom-call(f32[8,128]{1,0:T(8,128)} %fusion.97.src), custom_call_target="tpu_custom_call" | custom-call | flops 10000000 | bytes 100000 | tf_op jit(solution)/shard_map/small_gather/pallas_call | solution.py:501
  25.1 46.9 %gather_fusion = bf16[4608,2048]{1,0:T(8,128)(2,1)} fusion(bf16[6400,2048]{1,0:T(8,128)(2,1)} %param.11, s32[5120]{0:T(1024)S(1)} %pad_clamp_fusion), kind=kCustom, calls=%fused_computation | custom fusion | bytes 37767168 | tf_op jit(solution)/shard_map/jit(_take)/gather | solution.py:568
  72.0 6.8 sort.14
  79.5 1.7 convert_reduce_fusion.starts
  81.4 1.6 broadcast_in_dim.68.refs_0_
  82.9 160.8 %spread.1 = (bf16[288,2048]{1,0:T(8,128)(2,1)}, bf16[512,4096]{1,0:T(8,128)(2,1)}) custom-call(bf16[2,8,288,128]{3,2,1,0:T(8,128)(2,1)} %broadcast_in_dim.68.refs_0_, bf16[16,288,2048]{2,1,0:T(8,128)(2,1)} %bitcast.118, bf16[32,4096]{1,0:T(8,128)(2,1)} %refs_2_.1), custom_call_target="tpu_custom_call" | custom-call | flops 8000000000 | bytes 27000000 | tf_op jit(solution)/shard_map/spread/pallas_call | solution.py:374
  247.4 1.5 slice_bitcast_fusion.2
  250.3 9.6 %fusion.8 = bf16[288,3072]{1,0:T(8,128)(2,1)} fusion(bf16[288,2048]{1,0:T(8,128)(2,1)S(1)} %fusion.22.nrm_h, bf16[2048,5696]{1,0:T(8,128)(2,1)} %all-gather.4.cloned.1.call-done), kind=kOutput, calls=%fused_computation.10 | convolution fusion | flops 3624763392 | bytes 15532032 | tf_op jit(solution)/shard_map/dot_general | solution.py:520
  259.9 4.0 reshape.396
  265.3 3.2 fusion.58
  268.9 3.7 convolution_convert_fusion
  273.9 6.1 fusion.55
  287.2 13.0 %fusion.33 = (f32[3,16,96]{2,1,0:T(8,128)S(1)}, bf16[3,16,96,96]{2,3,1,0:T(8,128)(2,1)S(1)}) fusion(f32[3,16,96,96]{2,3,1,0:T(8,128)S(1)} %get-tuple-element.84, f32[3,16,96]{2,1,0:T(8,128)S(1)} %multiply_divide_fusion, f32[3,16,96]{2,1,0:T(8,128)S(1)} %get-tuple-element.83, bf16[3,96,16,128]{3,2,1,0:T(8,128)(2,1)S(1)} %get-tuple-element.94, ...), kind=kOutput, calls=%fused_computation.36 | convolution fusion | flops 115895808 | bytes 5068800 | tf_op jit(solution)/shard_map/transpose(jvp(bhst,bthd->bshd))/dot_general | solution.py:51
  302.6 1.3 copy.135
  304.0 2.5 copy.159
  309.0 1.6 reshape.402
  310.6 1.4 convert_multiply_fusion.3
  316.3 1.4 copy.134
  317.7 3.4 reshape.400.dq_h
  321.1 6.1 fusion.78
  328.2 7.2 fusion
  335.5 4.3 fusion.23
  340.5 1.4 shift-right-arithmetic_and_fusion
  342.7 1.8 pad_maximum_fusion.1
  344.5 1.9 copy.156
  346.5 2.0 fusion.53
  349.0 1.3 copy.197
  350.3 7.1 fusion.16
  358.9 297.1 %grad_shards.1 = (f32[128,2048]{1,0:T(8,128)}, f32[128,3072]{1,0:T(8,128)}, f32[128,640]{1,0:T(8,128)}, f32[32,4096]{1,0:T(8,128)}, f32[8,128]{1,0:T(8,128)}) custom-call(bf16[288,2048]{1,0:T(8,128)(2,1)} %bitcast.130, bf16[4608,2048]{1,0:T(8,128)(2,1)} %all-gather.6.cloned.1.call-done.dy_h, bf16[288,2048]{1,0:T(8,128)(2,1)} %copy-done.14, ...), custom_call_target="tpu_custom_call" | custom-call | flops 8000000000 | bytes 20000000 | tf_op jit(solution)/shard_map/grad_shards/pallas_call | solution.py:227
  656.0 1.8 copy.140
  660.2 55.8 %table_grad.1 = bf16[6400,2048]{1,0:T(8,128)(2,1)} custom-call(s32[51]{0:T(128)} %convert_reduce_fusion.starts, s32[4608]{0:T(1024)} %get-tuple-element.109.toks, s32[4608]{0:T(1024)} %get-tuple-element.108.rows, s32[96]{0:T(128)} %convert_reduce_fusion.1.flags, f32[1,2048]{1,0:T(1,128)} %get-tuple-element.101.gain, ...), custom_call_target="tpu_custom_call" | custom-call | flops 1000000000 | bytes 80000000 | tf_op jit(solution)/shard_map/table_grad/pallas_call | solution.py:474
  (195 shorter events, 39.7 us)
Async XLA Ops:
  7.2 3.7 copy-start.43
  7.2 3.8 copy-start.45
  7.2 3.8 copy-start.46
  7.2 242.1 %all-gather.4.cloned.1.call-start = ((), (), s32[]{:S(2)}) async-start(), calls=%async_computation | async-start | bytes 25067520 | tf_op jit(solution)/shard_map/all_gather | solution.py:554
  10.8 348.0 %all-gather.6.cloned.1.call-start = ((), (), s32[]{:S(2)}) async-start(), calls=%async_computation.1 | async-start | bytes 20054016 | tf_op jit(solution)/shard_map/all_gather | solution.py:577
  243.7 3.4 copy-start.2
  243.8 416.4 %all-gather.8.cloned.1.call-start = ((), (), s32[]{:S(2)}) async-start(), calls=%async_computation.2 | async-start | bytes 20054016 | tf_op jit(solution)/shard_map/all_gather | solution.py:580
  244.1 4.8 copy-start.20
  244.1 4.8 copy-start.23
  268.6 4.0 copy-start.7
  268.9 3.7 copy-start.39
  268.9 3.7 copy-start.37
  280.8 2.5 copy-start.26
  283.3 3.3 copy-start.5
  283.4 3.9 copy-start.16
  286.7 19.8 %copy-start.31 = (f32[3,16,96]{2,1,0:T(8,128)}, f32[3,16,96]{2,1,0:T(8,128)S(1)}, u32[]{:S(2)}) copy-start(f32[3,16,96]{2,1,0:T(8,128)S(1)} %get-tuple-element.83) | copy-start | bytes 55300
  286.7 27.1 %copy-start = (f32[3,16,96,96]{2,3,1,0:T(8,128)}, f32[3,16,96,96]{2,3,1,0:T(8,128)S(1)}, u32[]{:S(2)}) copy-start(f32[3,16,96,96]{2,3,1,0:T(8,128)S(1)} %get-tuple-element.84) | copy-start | bytes 5308420
  287.2 19.3 %copy-start.29 = (f32[3,16,96]{2,1,0:T(8,128)}, f32[3,16,96]{2,1,0:T(8,128)S(1)}, u32[]{:S(2)}) copy-start(f32[3,16,96]{2,1,0:T(8,128)S(1)} %fusion.50) | copy-start | bytes 55300
  300.3 6.2 copy-start.17
  304.0 2.5 copy-start.34
  317.7 3.4 copy-start.8
  317.7 3.4 copy-start.38
  321.1 6.1 copy-start.40
  321.1 7.1 copy-start.9
  328.2 7.3 %copy-start.11 = (bf16[288,512]{0,1:T(8,128)(2,1)}, bf16[288,512]{0,1:T(8,128)(2,1)S(1)}, u32[]{:S(2)}) copy-start(bf16[288,512]{0,1:T(8,128)(2,1)S(1)} %get-tuple-element.96) | copy-start | bytes 884740
  328.2 7.3 %copy-start.3 = (bf16[288,2048]{1,0:T(8,128)(2,1)S(1)}, bf16[288,2048]{1,0:T(8,128)(2,1)}, u32[]{:S(2)}) copy-start(bf16[288,2048]{1,0:T(8,128)(2,1)} %get-tuple-element.28) | copy-start | bytes 3538948
  328.2 7.3 %copy-start.33 = (bf16[288,64]{0,1:T(8,128)(2,1)S(1)}, bf16[288,64]{0,1:T(8,128)(2,1)}, u32[]{:S(2)}) copy-start(bf16[288,64]{0,1:T(8,128)(2,1)} %reshape.402) | copy-start | bytes 110596
  328.2 7.3 %copy-start.42 = (f32[288]{0:T(512)S(1)}, f32[288]{0:T(512)}, u32[]{:S(2)}) copy-start(f32[288]{0:T(512)} %copy-done.41) | copy-start | bytes 3460
  339.9 6.6 copy-start.1
  350.3 7.1 copy-start.12
  350.3 7.9 %copy-start.44 = (f32[8]{0:T(128)S(1)}, f32[8]{0:T(128)}, u32[]{:S(2)}) copy-start(f32[8]{0:T(128)} %pad.58.clone) | copy-start | bytes 100
  660.2 55.8 %copy-start.10 = (f32[128,3072]{1,0:T(8,128)S(1)}, f32[128,3072]{1,0:T(8,128)}, u32[]{:S(2)}) copy-start(f32[128,3072]{1,0:T(8,128)} %get-tuple-element.133) | copy-start | bytes 4718596
  (18 other events, 24.0 us)
Sparse Core Ops, SparseCore 0:
  11.0 168.3 all-gather.3
  243.9 98.7 all-gather.5
  344.9 175.4 all-gather.7

commit v3 on v2

--- a/solution.py
+++ b/solution.py
@@ -81,8 +81,9 @@
 
 TOK = 288
 D_OUT, D_CAT, D_UP, D_DOWN = 2048, 3712, 4096, 640
+WO_COL = 3072
 CUT = 1792
-PARTS = (('u', 0, 0, 2048), ('u', 1, 2048, 2048), ('n', 0, 0, CUT), ('n', 1, CUT, D_CAT - CUT))
+PARTS = (('u', 0, 0, 2048), ('u', 1, 2048, 2048), ('n', 0, 0, 896), ('n', 1, 1792, 1024), ('n', 0, 896, 896), ('n', 1, 2816, 896))
 N_PARTS = len(PARTS)
 ROWS = {'n': 128, 'u': 32}
 
@@ -90,8 +91,8 @@
     step = 512
     return [(c, min(step, width - c)) for c in range(0, width, step)]
 
-def grad_kernel(mix_h, dy_h, nrm_h, dd_h, dq_h, lat_h, du_h, sm_h, go_h, gq_h, gd_h, gu_h, gs_h,
-                mix, dy, go, nrm, cat, lat, du, b0, b1, b2, b3, smr, ssum, loc_sem, xs_sem, xr_sem, s_sem, r_sem, ms_sem, mr_sem, cs_sem, cr_sem, dy_sem, out_sem):
+def grad_kernel(mix_h, dy_h, nrm_h, dd_h, dq_h, lat_h, du_h, sm_h, h0_h, wo_h, y_h, go_h, gq_h, gd_h, gu_h, gs_h,
+                mix, dy, go, nrm, cat, lat, du, b0, b1, b2, b3, b4, b5, mixf, h0, wo, yv, smr, ssum, loc_sem, xs_sem, xr_sem, s_sem, r_sem, ms_sem, mr_sem, cs_sem, cr_sem, dy_sem, y_sem, out_sem):
     me, core, pos = place()
     partner = me + 1 - 2 * core
     meet_all(me)
@@ -114,7 +115,13 @@
         rc = pltpu.make_async_remote_copy(sm_h.at[peer], smr.at[i], ms_sem.at[i], mr_sem.at[i], device_id={'fsdp': peer}, device_id_type=MESH)
         rc.start()
         smalls.append(rc)
-    bufs = (b0, b1, b2, b3)
+    for i, (src, dst) in enumerate(((mix_h, mixf), (h0_h, h0))):
+        pltpu.make_async_copy(src, dst, y_sem.at[2 + i]).start()
+
+    def wo_load(t):
+        return pltpu.make_async_copy(wo_h.at[:, pl.ds(pl.multiple_of(WO_COL + t * 512, 512), 512)], wo.at[t % 2], y_sem.at[t % 2])
+    wo_load(0).start()
+    bufs = (b0, b1, b2, b3, b4, b5)
     peers = (at_pos(pos + 1, core), at_pos(pos + 7, core))
     left_ops = {'n': (nrm, cat), 'u': (lat, du)}
 
@@ -130,49 +137,46 @@
         return pltpu.make_async_remote_copy(bufs[p].at[step], bufs[p].at[step + 1], s_sem.at[p, step], r_sem.at[p, step + 1],
                                             device_id={'fsdp': peers[PARTS[p][1]]}, device_id_type=MESH)
 
-    def work(p, step, first):
+    def work(p, step):
         kind, way, c0, width = PARTS[p]
         chip = chip_at((pos + 7 - step + way * (2 * step + 2)) % RING)
         lhs_ref, rhs_ref = left_ops[kind]
-        if kind == 'u':
-            row = pl.multiple_of(chip * 64 + core * 32, 32)
-            lhs = [lhs_ref[b, pl.ds(row, 32), :] for b in range(2)]
-            dims = (((1,), (0,)), ((), ()))
-        else:
-            col = pl.multiple_of(chip * 256 + core * 128, 128)
-            lhs = [lhs_ref[b, :, pl.ds(col, 128)] for b in range(2)]
-            dims = (((0,), (0,)), ((), ()))
+        rows = ROWS[kind]
+        row = pl.multiple_of((chip * 2 + core) * rows, rows)
+        lhs = [lhs_ref[b, pl.ds(row, rows), :] for b in range(2)]
         for c, w in col_tiles(width):
-            part = sum(lax.dot_general(lhs[b], rhs_ref[b, :, c0 + c:c0 + c + w], dims, preferred_element_type=F32) for b in range(2))
-            if first:
-                bufs[p][step, :, c:c + w] = part
-            else:
-                bufs[p][step, :, c:c + w] = bufs[p][step, :, c:c + w] + part
-
-    need = {'u': (0, 1), 'n': (2, 3, 4)}
-    for p in range(N_PARTS):
-        if PARTS[p][1] == 0:
-            for i in need[PARTS[p][0]]:
-                local[i].wait()
-                cross[i].wait_recv()
-        work(p, 0, True)
-        hop(p, 0).start()
+            part = sum(jnp.dot(lhs[b], rhs_ref[b, :, c0 + c:c0 + c + w], preferred_element_type=F32) for b in range(2))
+            bufs[p][step, :, c:c + w] = bufs[p][step, :, c:c + w] + part
+
     for i in range(1, GROUP):
         mix_send(i).start()
     dy_load(0).start()
-    own_mix.wait()
-    for i in range(1, GROUP):
-        mix_send(i).wait()
     go[...] = jnp.zeros_like(go)
-
-    @pl.loop(1, RING - 1)
+    for p in range(N_PARTS):
+        bufs[p][0] = jnp.zeros(bufs[p].shape[1:], F32)
+    for i in range(5):
+        local[i].wait()
+        cross[i].wait_recv()
+
+    @pl.loop(0, RING)
     def _(step):
         for p in range(N_PARTS):
-            hop(p, step - 1).wait_recv()
-            work(p, step, False)
-            hop(p, step).start()
-
-        @pl.when(step < 5)
+            @pl.when(step > 0)
+            def _():
+                hop(p, step - 1).wait_recv()
+            work(p, step)
+
+            @pl.when(step < RING - 1)
+            def _():
+                hop(p, step).start()
+
+        @pl.when(step == 0)
+        def _():
+            own_mix.wait()
+            for i in range(1, GROUP):
+                mix_send(i).wait()
+
+        @pl.when((step > 0) & (step < 5))
         def _():
             @pl.loop(0, 4)
             def _(j):
@@ -182,28 +186,44 @@
                 @pl.when(blk < GROUP - 1)
                 def _():
                     dy_load(blk + 1).start()
-                for c, w in col_tiles(D_OUT):
+                for c, w in col_tiles(2048):
                     go[:, c:c + w] += lax.dot_general(mix[blk], dy[blk % 2, :, c:c + w], (((0,), (0,)), ((), ())), preferred_element_type=F32)
+
+        @pl.when(step == 5)
+        def _():
+            for i, (src, dst) in enumerate(((mix_h, mixf), (h0_h, h0))):
+                pltpu.make_async_copy(src, dst, y_sem.at[2 + i]).wait()
+
+            @pl.loop(0, 4)
+            def _(t):
+                wo_load(t).wait()
+
+                @pl.when(t < 3)
+                def _():
+                    wo_load(t + 1).start()
+                here = pl.ds(pl.multiple_of(t * 512, 512), 512)
+                yv[:, here] = (h0[:, here].astype(F32) + jnp.dot(mixf[...], wo[t % 2], preferred_element_type=F32)).astype(BF16)
 
     last = RING - 1
     outs = []
-    cp = pltpu.make_async_copy(go, go_h, out_sem.at[7])
+    cp = pltpu.make_async_copy(go, go_h, out_sem.at[6])
     cp.start()
     outs.append(cp)
-    cut_q = CUT - D_DOWN
-    targets = ((gu_h.at[:, 0:2048], 0, 2048),), ((gu_h.at[:, 2048:4096], 0, 2048),), ((gd_h, 0, D_DOWN), (gq_h.at[:, 0:cut_q], D_DOWN, CUT)), ((gq_h.at[:, cut_q:3072], 0, D_CAT - CUT),)
+    cp = pltpu.make_async_copy(yv, y_h, out_sem.at[9])
+    cp.start()
+    outs.append(cp)
+    targets = (((gu_h.at[:, 0:2048], 0, 2048),), ((gu_h.at[:, 2048:4096], 0, 2048),), ((gd_h, 0, 640), (gq_h.at[:, 0:256], 640, 896)),
+               ((gq_h.at[:, 1152:2176], 0, 1024),), ((gq_h.at[:, 256:1152], 0, 896),), ((gq_h.at[:, 2176:3072], 0, 896),))
     for p in range(N_PARTS):
-        hop(p, last - 1).wait_recv()
-        work(p, last, False)
         for n, (dst, c0, c1) in enumerate(targets[p]):
-            cp = pltpu.make_async_copy(bufs[p].at[last, :, c0:c1], dst, out_sem.at[p + 4 * n])
+            cp = pltpu.make_async_copy(bufs[p].at[last, :, c0:c1], dst, out_sem.at[p + 6 * n])
             cp.start()
             outs.append(cp)
     own_small.wait()
     for rc in smalls:
         rc.wait()
     ssum[...] = jnp.sum(smr[...], axis=0)
-    cp = pltpu.make_async_copy(ssum, gs_h, out_sem.at[4])
+    cp = pltpu.make_async_copy(ssum, gs_h, out_sem.at[7])
     cp.start()
     outs.append(cp)
     for rc in cross:
@@ -216,21 +236,22 @@
         cp.wait()
 
 
-def grad_shards(mix, dy_all, nrm, dd, dq, lat_t, du, small):
+def grad_shards(mix, dy_all, nrm_t, dd, dq, lat_t, du, small, rows, weights):
     shapes = [(ROWS[k], RING, w) for k, _, _, w in PARTS]
-    scratch = [pltpu.VMEM((GROUP, TOK, 128), BF16), pltpu.VMEM((2, TOK, 2048), BF16), pltpu.VMEM((128, 2048), F32), pltpu.VMEM((2, TOK, 2048), BF16),
+    scratch = [pltpu.VMEM((GROUP, TOK, 128), BF16), pltpu.VMEM((2, TOK, 2048), BF16), pltpu.VMEM((128, 2048), F32), pltpu.VMEM((2, 2048, TOK), BF16),
                pltpu.VMEM((2, TOK, D_CAT), BF16), pltpu.VMEM((2, 512, TOK), BF16), pltpu.VMEM((2, TOK, D_UP), BF16)]
     scratch += [pltpu.VMEM((RING, r, w), F32) for r, _, w in shapes]
+    scratch += [pltpu.VMEM((TOK, 2048), BF16), pltpu.VMEM((TOK, 2048), BF16), pltpu.VMEM((2, 2048, 512), BF16), pltpu.VMEM((TOK, 2048), BF16)]
     scratch += [pltpu.VMEM((GROUP, 8, 128), F32), pltpu.VMEM((8, 128), F32)]
     dma = pltpu.SemaphoreType.DMA
-    scratch += [dma((7,)), dma((5,)), dma((5,)), dma((N_PARTS, RING)), dma((N_PARTS, RING)), dma((GROUP,)), dma((GROUP,)), dma((GROUP,)), dma((GROUP,)), dma((2,)), dma((8,))]
+    scratch += [dma((7,)), dma((5,)), dma((5,)), dma((N_PARTS, RING)), dma((N_PARTS, RING)), dma((GROUP,)), dma((GROUP,)), dma((GROUP,)), dma((GROUP,)), dma((2,)), dma((4,)), dma((10,))]
     return pl.pallas_call(
         grad_kernel,
-        out_shape=(jax.ShapeDtypeStruct((128, 2048), F32), jax.ShapeDtypeStruct((128, 3072), F32), jax.ShapeDtypeStruct((128, D_DOWN), F32), jax.ShapeDtypeStruct((32, D_UP), F32), jax.ShapeDtypeStruct((8, 128), F32)),
-        in_specs=[ANY] * 8, out_specs=(ANY,) * 5, scratch_shapes=scratch,
+        out_shape=(jax.ShapeDtypeStruct((TOK, 2048), BF16), jax.ShapeDtypeStruct((128, 2048), F32), jax.ShapeDtypeStruct((128, 3072), F32), jax.ShapeDtypeStruct((128, D_DOWN), F32), jax.ShapeDtypeStruct((32, D_UP), F32), jax.ShapeDtypeStruct((8, 128), F32)),
+        in_specs=[ANY] * 10, out_specs=(ANY,) * 6, scratch_shapes=scratch,
         compiler_params=pltpu.CompilerParams(collective_id=1, has_side_effects=True, vmem_limit_bytes=60 * 1024 * 1024),
         cost_estimate=pl.CostEstimate(flops=8 * 10**9, bytes_accessed=20 * 10**6, transcendentals=0), name='grad_shards',
-    )(mix, dy_all, nrm, dd, dq, lat_t, du, small)
+    )(mix, dy_all, nrm_t, dd, dq, lat_t, du, small, rows, weights)
 
 
 W_SHARDS = ((32, 4096),)
@@ -384,6 +405,7 @@
 IN_BLK = 144
 SUB = 48
 PIECE = 16
+UNROLL = 4
 IN_SLOTS = 4
 OUT_SLOTS = 4
 
@@ -458,10 +480,18 @@
         def _():
             acc[...] = jnp.zeros_like(acc)
 
-            @pl.loop(first, last)
+            def add(k):
+                acc[pl.ds(rows[k], 1), :] += grad[pl.ds(toks[k], 1), :]
+            quads = (last - first) // UNROLL
+
+            @pl.loop(0, quads)
+            def _(i):
+                for j in range(UNROLL):
+                    add(first + i * UNROLL + j)
+
+            @pl.loop(first + quads * UNROLL, last)
             def _(k):
-                r = rows[k]
-                acc[pl.ds(r, 1), :] += grad[pl.ds(toks[k], 1), :]
+                add(k)
             ob[slot] = acc[...].astype(BF16)
             store(blk, ob.at[slot]).start()
     for blk in range(n_out - OUT_SLOTS, n_out):
@@ -523,7 +553,6 @@
     kv_up = jnp.dot(latent, w_kv_up, preferred_element_type=jnp.float32).astype(jnp.bfloat16)
     attn_mix, attn_pull = jax.vjp(attend_local, q_proj.reshape(seq_count, seq_len, -1, NOPE_DIM + ROPE_DIM), kv_down[:, kv_rank:].reshape(seq_count, seq_len, ROPE_DIM), kv_up.reshape(seq_count, seq_len, -1, NOPE_DIM + VALUE_DIM))
     mix_rows = attn_mix.reshape(tok_count, -1)
-    out_f32 = rows_f32 + jnp.dot(mix_rows, w_out, preferred_element_type=jnp.float32)
     d_mix = lax.dot_general(grad_rows, w_out, COL_DIMS, preferred_element_type=jnp.float32).astype(jnp.bfloat16)
     d_query, d_pe, d_up = attn_pull(d_mix.reshape(attn_mix.shape))
     d_query = d_query.reshape(tok_count, -1)
@@ -535,7 +564,7 @@
     d_normed = d_normed + lax.dot_general(d_down, w_kv_down, COL_DIMS, preferred_element_type=jnp.float32)
     d_normed = d_normed.astype(jnp.bfloat16)
     _, d_gain = norm_pull(d_normed)
-    return out_f32.astype(jnp.bfloat16), d_normed, normed, mix_rows, latent, d_query, d_down, d_up, d_gain, d_kv_gain
+    return d_normed, normed, mix_rows, latent, d_query, d_down, d_up, d_gain, d_kv_gain
 
 
 def solution(mesh):
@@ -562,7 +591,8 @@
         owner = all_ids // vocab_dev
         mine = (owner == me)
         local = all_ids - me * vocab_dev
-        keys = lax.sort(jnp.where(mine, local * 8192 + jnp.arange(GROUP * tok_count).reshape(GROUP, tok_count), 2**30).reshape(-1))
+        stamp = jnp.arange(GROUP * tok_count).reshape(GROUP, tok_count) * ROW_BLK
+        keys = lax.sort(jnp.where(mine, (local // ROW_BLK) * 2**20 + stamp + local % ROW_BLK, 2**30).reshape(-1))
         starts = jnp.sum((mine & (local < ROW_BLK * jnp.arange(vocab_dev // ROW_BLK + 1)[:, None, None])).astype(jnp.int32), axis=(1, 2))
         flags = jnp.sum(mine.reshape(-1, SUB).astype(jnp.int32), axis=1)
         picked = jnp.take(emb_table, jnp.where(mine, local, 0).reshape(-1), axis=0, mode='clip')
@@ -575,13 +605,12 @@
         full_wq, full_wo, full_kva = bundle[:, :3072], bundle[:, 3072:5120], bundle[:, 5120:]
         tok_rows, grad_rows = lax.optimization_barrier((tok_rows, grad_rows))
         all_dy = lax.all_gather(grad_rows, 'fsdp', tiled=True)
-        block_out, d_normed, normed, mix, latent, d_query, d_down, d_up, d_gain, d_kv_gain = block_step(
+        d_normed, normed, mix, latent, d_query, d_down, d_up, d_gain, d_kv_gain = block_step(
             tok_rows.astype(F32), grad_rows, (gain_full, full_wq, full_kva, kv_gain_full, full_kvb, full_wo), seq_count)
         all_dn = lax.all_gather(d_normed, 'fsdp', tiled=True)
         small = jnp.concatenate([d_gain.reshape(GROUP, 1, 128), jnp.pad(d_kv_gain.reshape(GROUP, 1, 32), ((0, 0), (0, 0), (0, 96))), jnp.zeros((GROUP, 6, 128), F32)], axis=1)
-        block_out, mix = lax.optimization_barrier((block_out, mix))
-        g_out, g_query, g_down, g_up, g_small = grad_shards(mix, all_dy, normed, jnp.pad(d_down, ((0, 0), (0, D_DOWN - d_down.shape[1]))), d_query, latent.T, d_up, small)
-        grad_table = table_grad(starts, keys & 8191, (keys >> 13) & (ROW_BLK - 1), flags, gain_full.reshape(1, -1), all_dy, all_dn, picked, vocab_dev)
+        block_out, g_out, g_query, g_down, g_up, g_small = grad_shards(mix, all_dy, normed.T, jnp.pad(d_down, ((0, 0), (0, D_DOWN - d_down.shape[1]))), d_query, latent.T, d_up, small, tok_rows, bundle)
+        grad_table = table_grad(starts, (keys >> 7) & 8191, keys & (ROW_BLK - 1), flags, gain_full.reshape(1, -1), all_dy, all_dn, picked, vocab_dev)
         return (block_out.reshape(seq_count, seq_len, d_model), grad_table, g_small[0], g_query, g_down[:, :576], g_small[1, :32], g_up, g_out)
 
     return jax.shard_map(device_step, mesh=mesh, in_specs=(tok_spec, seq_spec, mat_spec, vec_spec, mat_spec, mat_spec, vec_spec, mat_spec, mat_spec), out_specs=(seq_spec, tok_spec, part_vec, tok_spec, tok_spec, part_vec, tok_spec, tok_spec), check_vma=False)

time: 736 us -> 720 us (0.978)
  matrix products: 69.4 us -> 47 us
    dot_general x3, matrix products: 15.8 us -> 6.34 us  [attend_local(): jnp.einsum('bhst,bthd->bshd', attn_probs, kv_up[..., NOPE_DIM:], preferre...]
    pallas_call x1, Pallas kernels: 55.8 us -> 47.2 us  [table_grad(): pl.pallas_call(table_kernel, out_shape=jax.ShapeDtypeStruct((vocab_dev, 2...]
    unnamed x105 -> x120, local copies, waits for them, and re-layouts: 17 us -> 17.4 us
  transfers between devices with their start and end apart: 3 -> 3, of which waited for: 0 -> 1; matrix products, arithmetic and copies ran while one was open for 24% -> 22% of each run, Pallas kernels for 64% -> 67%
where the time goes in v3:
time: 720 us; the launch traced here: 710 us
  Pallas kernels  522 us (72%)
  local copies, waits for them, and re-layouts  93.3 us (13%)
  matrix products  47 us (7%)
  other arithmetic  27.2 us (4%)
  between operations  15.2 us (2%)
    pallas_call x1, Pallas kernels, grad_shards(): pl.pallas_call(grad_kernel, out_shape=(jax.ShapeDtypeStruct((TOK, 2048),...  304 us
    pallas_call x1, Pallas kernels, spread(): pl.pallas_call(lambda *refs: spread_kernel(n_w, *refs), out_shape=(jax.Sh...  161 us
    pallas_call x1, Pallas kernels, table_grad(): pl.pallas_call(table_kernel, out_shape=jax.ShapeDtypeStruct((vocab_dev, 2...  47.2 us
    gather x1, local copies, waits for them, and re-layouts, device_step(): jnp.take(emb_table, jnp.where(mine, local, 0).reshape(-1), axis=0, mode='...  46.9 us
    unnamed x120, local copies, waits for them, and re-layouts  17.4 us
  transfers between devices with their start and end apart: 3, of which 1 were waited for; matrix products, arithmetic and copies ran while one was open for 22% of the time, Pallas kernels for 67%

profile of v3, /device:TPU:0, one launch (start us, length us, event | category | flops | bytes accessed | tf_op | source)
XLA Modules:
  0.0 709.9 jit_solution(15504944358066532886)
XLA Ops:
  8.3 2.5 pad_maximum_fusion
  11.7 10.2 %small_gather.1 = f32[16,8,128]{2,1,0:T(8,128)} custom-call(f32[8,128]{1,0:T(8,128)} %fusion.98.src), custom_call_target="tpu_custom_call" | custom-call | flops 10000000 | bytes 100000 | tf_op jit(solution)/shard_map/small_gather/pallas_call | solution.py:531
  25.1 46.9 %gather_fusion = bf16[4608,2048]{1,0:T(8,128)(2,1)} fusion(bf16[6400,2048]{1,0:T(8,128)(2,1)} %param.11, s32[5120]{0:T(1024)S(1)} %pad_clamp_fusion), kind=kCustom, calls=%fused_computation | custom fusion | bytes 37767168 | tf_op jit(solution)/shard_map/jit(_take)/gather | solution.py:598
  72.1 6.8 sort.14
  79.6 1.6 convert_reduce_fusion.starts
  81.4 1.6 broadcast_in_dim.68.refs_0_
  82.9 160.8 %spread.1 = (bf16[288,2048]{1,0:T(8,128)(2,1)}, bf16[512,4096]{1,0:T(8,128)(2,1)}) custom-call(bf16[2,8,288,128]{3,2,1,0:T(8,128)(2,1)} %broadcast_in_dim.68.refs_0_, bf16[16,288,2048]{2,1,0:T(8,128)(2,1)} %bitcast.117, bf16[32,4096]{1,0:T(8,128)(2,1)} %refs_2_.1), custom_call_target="tpu_custom_call" | custom-call | flops 8000000000 | bytes 27000000 | tf_op jit(solution)/shard_map/spread/pallas_call | solution.py:395
  247.1 1.6 fusion.17
  248.7 1.4 slice_bitcast_fusion.2
  250.2 8.7 %fusion.6 = bf16[288,3072]{1,0:T(8,128)(2,1)S(1)} fusion(bf16[2048,5696]{1,0:T(8,128)(2,1)} %all-gather.4.cloned.1.call-done.wo_h, bf16[288,2048]{1,0:T(8,128)(2,1)S(1)} %copy-done, f32[2048]{0:T(1024)S(1)} %bitcast.133, f32[288]{0:T(512)S(1)} %add_rsqrt_fusion), kind=kOutput, calls=%fused_computation.8 | convolution fusion | flops 3627122688 | bytes 15541376 | tf_op jit(solution)/shard_map/dot_general | solution.py:550
  258.8 3.5 reshape.393
  262.4 1.6 slice.87
  265.6 3.3 fusion.51
  269.1 1.6 convolution_convert_fusion
  270.7 2.2 copy.162
  273.0 6.4 fusion.48
  287.0 1.5 fusion.26
  293.8 2.8 copy.142
  296.6 5.0 reshape.398.dq_h
  303.8 2.8 fusion.47
  308.7 1.4 copy.136
  312.8 3.1 fusion.71
  316.9 7.3 %fusion = f32[288,2048]{1,0:T(8,128)S(1)} fusion(bf16[288,3072]{1,0:T(8,128)(2,1)S(1)} %copy-done.6, bf16[2048,5696]{1,0:T(8,128)(2,1)} %all-gather.4.cloned.1.call-done.wo_h), kind=kOutput, calls=%fused_computation.1 | convolution fusion | flops 3623878656 | bytes 16711680 | tf_op jit(solution)/shard_map/dot_general | solution.py:563
  324.3 4.1 fusion.11
  328.4 1.4 broadcast_and_fusion
  329.8 2.0 fusion.46
  332.3 1.3 copy.201
  334.4 1.5 copy.143.nrm_h
  337.8 4.9 all-gather.6.cloned.1.call-done.dy_h
  342.7 304.1 %grad_shards.1 = (bf16[288,2048]{1,0:T(8,128)(2,1)}, f32[128,2048]{1,0:T(8,128)}, f32[128,3072]{1,0:T(8,128)}, f32[128,640]{1,0:T(8,128)}, f32[32,4096]{1,0:T(8,128)}, /*index=5*/f32[8,128]{1,0:T(8,128)}) custom-call(bf16[288,2048]{1,0:T(8,128)(2,1)} %bitcast.123, bf16[4608,2048]{1,0:T(8,128)(2,1)} %all-gather.6.cloned.1.call-done.dy_h, ...), custom_call_target="tpu_custom_call" | custom-call | flops 8000000000 | bytes 20000000 | tf_op jit(solution)/shard_map/grad_shards/pallas_call | solution.py:248
  646.8 1.8 copy.145
  651.0 47.2 %table_grad.1 = bf16[6400,2048]{1,0:T(8,128)(2,1)} custom-call(s32[51]{0:T(128)} %convert_reduce_fusion.starts, s32[4608]{0:T(1024)} %get-tuple-element.106.toks, s32[4608]{0:T(1024)} %get-tuple-element.105.rows, s32[96]{0:T(128)} %convert_reduce_fusion.1.flags, f32[1,2048]{1,0:T(1,128)} %get-tuple-element.99.gain, ...), custom_call_target="tpu_custom_call" | custom-call | flops 1000000000 | bytes 80000000 | tf_op jit(solution)/shard_map/table_grad/pallas_call | solution.py:504
  (210 shorter events, 41.9 us)
Async XLA Ops:
  7.2 3.7 copy-start.51
  7.2 3.8 copy-start.52
  7.2 3.8 copy-start.53
  7.2 242.9 %all-gather.4.cloned.1.call-start = ((), (), s32[]{:S(2)}) async-start(), calls=%async_computation | async-start | bytes 25067520 | tf_op jit(solution)/shard_map/all_gather | solution.py:583
  10.8 331.9 %all-gather.6.cloned.1.call-start = ((), (), s32[]{:S(2)}) async-start(), calls=%async_computation.1 | async-start | bytes 20054016 | tf_op jit(solution)/shard_map/all_gather | solution.py:607
  243.7 6.4 copy-start
  243.8 407.2 %all-gather.8.cloned.1.call-start = ((), (), s32[]{:S(2)}) async-start(), calls=%async_computation.2 | async-start | bytes 20054016 | tf_op jit(solution)/shard_map/all_gather | solution.py:610
  245.0 5.1 copy-start.23
  245.0 5.1 copy-start.26
  248.7 10.1 %copy-start.47 = (f32[288]{0:T(512)}, f32[288]{0:T(512)S(1)}, u32[]{:S(2)}) copy-start(f32[288]{0:T(512)S(1)} %add_rsqrt_fusion) | copy-start | bytes 3460
  250.1 8.7 %copy-start.38 = (f32[16,1,128]{2,1,0:T(1,128)}, f32[16,1,128]{2,1,0:T(1,128)S(1)}, u32[]{:S(2)}) copy-start(f32[16,1,128]{2,1,0:T(1,128)S(1)} %get-tuple-element.100) | copy-start | bytes 24580
  262.4 3.2 copy-start.39
  262.4 3.2 copy-start.48
  265.6 3.5 copy-start.10
  268.9 3.9 copy-start.12
  279.7 7.3 %copy-start.17 = (bf16[36,8,16,128]{3,2,1,0:T(8,128)(2,1)}, bf16[36,8,16,128]{3,2,1,0:T(8,128)(2,1)S(1)}, u32[]{:S(2)}) copy-start(bf16[36,8,16,128]{3,2,1,0:T(8,128)(2,1)S(1)} %copy.163) | copy-start | bytes 3538948
  283.6 3.5 copy-start.19
  286.4 5.6 copy-start.4
  286.4 5.6 copy-start.33
  287.0 5.1 copy-start.31
  288.5 3.5 copy-start.20
  288.5 3.5 copy-start.41
  303.8 3.4 copy-start.21
  303.8 3.4 copy-start.32
  303.8 3.4 copy-start.34
  303.8 3.4 copy-start.42
  311.2 4.7 copy-start.1
  312.8 3.1 copy-start.46
  312.8 4.1 copy-start.6
  316.9 7.3 %copy-start.15 = (bf16[288,512]{0,1:T(8,128)(2,1)}, bf16[288,512]{0,1:T(8,128)(2,1)S(1)}, u32[]{:S(2)}) copy-start(bf16[288,512]{0,1:T(8,128)(2,1)S(1)} %get-tuple-element.94) | copy-start | bytes 884740
  316.9 7.3 %copy-start.35 = (bf16[288,64]{0,1:T(8,128)(2,1)S(1)}, bf16[288,64]{0,1:T(8,128)(2,1)}, u32[]{:S(2)}) copy-start(bf16[288,64]{0,1:T(8,128)(2,1)} %reshape.397) | copy-start | bytes 110596
  651.0 47.2 %copy-start.18 = (bf16[288,2048]{1,0:T(8,128)(2,1)S(1)}, bf16[288,2048]{1,0:T(8,128)(2,1)}, u32[]{:S(2)}) copy-start(bf16[288,2048]{1,0:T(8,128)(2,1)} %get-tuple-element.30) | copy-start | bytes 3538948
  (25 other events, 45.9 us)
Sparse Core Ops, SparseCore 0:
  11.0 168.3 all-gather.3
  243.9 98.7 all-gather.5
  344.3 195.8 all-gather.7

commit v4 on v3

--- a/solution.py
+++ b/solution.py
@@ -91,7 +91,7 @@
     step = 512
     return [(c, min(step, width - c)) for c in range(0, width, step)]
 
-def grad_kernel(mix_h, dy_h, nrm_h, dd_h, dq_h, lat_h, du_h, sm_h, h0_h, wo_h, y_h, go_h, gq_h, gd_h, gu_h, gs_h,
+def grad_kernel(mix_h, dy_h, nrm_h, dd_h, dq_h, lat_h, du_h, sm_h, h0_h, wo_h, wl_h, y_h, go_h, gq_h, gd_h, gu_h, gs_h,
                 mix, dy, go, nrm, cat, lat, du, b0, b1, b2, b3, b4, b5, mixf, h0, wo, yv, smr, ssum, loc_sem, xs_sem, xr_sem, s_sem, r_sem, ms_sem, mr_sem, cs_sem, cr_sem, dy_sem, y_sem, out_sem):
     me, core, pos = place()
     partner = me + 1 - 2 * core
@@ -120,6 +120,9 @@
 
     def wo_load(t):
         return pltpu.make_async_copy(wo_h.at[:, pl.ds(pl.multiple_of(WO_COL + t * 512, 512), 512)], wo.at[t % 2], y_sem.at[t % 2])
+
+    def wo_last():
+        return pltpu.make_async_copy(wl_h, wo.at[1], y_sem.at[1])
     wo_load(0).start()
     bufs = (b0, b1, b2, b3, b4, b5)
     peers = (at_pos(pos + 1, core), at_pos(pos + 7, core))
@@ -196,11 +199,21 @@
 
             @pl.loop(0, 4)
             def _(t):
-                wo_load(t).wait()
-
                 @pl.when(t < 3)
                 def _():
+                    wo_load(t).wait()
+
+                @pl.when(t == 3)
+                def _():
+                    wo_last().wait()
+
+                @pl.when(t < 2)
+                def _():
                     wo_load(t + 1).start()
+
+                @pl.when(t == 2)
+                def _():
+                    wo_last().start()
                 here = pl.ds(pl.multiple_of(t * 512, 512), 512)
                 yv[:, here] = (h0[:, here].astype(F32) + jnp.dot(mixf[...], wo[t % 2], preferred_element_type=F32)).astype(BF16)
 
@@ -236,7 +249,7 @@
         cp.wait()
 
 
-def grad_shards(mix, dy_all, nrm_t, dd, dq, lat_t, du, small, rows, weights):
+def grad_shards(mix, dy_all, nrm_t, dd, dq, lat_t, du, small, rows, weights, last_cols):
     shapes = [(ROWS[k], RING, w) for k, _, _, w in PARTS]
     scratch = [pltpu.VMEM((GROUP, TOK, 128), BF16), pltpu.VMEM((2, TOK, 2048), BF16), pltpu.VMEM((128, 2048), F32), pltpu.VMEM((2, 2048, TOK), BF16),
                pltpu.VMEM((2, TOK, D_CAT), BF16), pltpu.VMEM((2, 512, TOK), BF16), pltpu.VMEM((2, TOK, D_UP), BF16)]
@@ -248,13 +261,13 @@
     return pl.pallas_call(
         grad_kernel,
         out_shape=(jax.ShapeDtypeStruct((TOK, 2048), BF16), jax.ShapeDtypeStruct((128, 2048), F32), jax.ShapeDtypeStruct((128, 3072), F32), jax.ShapeDtypeStruct((128, D_DOWN), F32), jax.ShapeDtypeStruct((32, D_UP), F32), jax.ShapeDtypeStruct((8, 128), F32)),
-        in_specs=[ANY] * 10, out_specs=(ANY,) * 6, scratch_shapes=scratch,
+        in_specs=[ANY] * 11, out_specs=(ANY,) * 6, scratch_shapes=scratch,
         compiler_params=pltpu.CompilerParams(collective_id=1, has_side_effects=True, vmem_limit_bytes=60 * 1024 * 1024),
         cost_estimate=pl.CostEstimate(flops=8 * 10**9, bytes_accessed=20 * 10**6, transcendentals=0), name='grad_shards',
-    )(mix, dy_all, nrm_t, dd, dq, lat_t, du, small, rows, weights)
-
-
-W_SHARDS = ((32, 4096),)
+    )(mix, dy_all, nrm_t, dd, dq, lat_t, du, small, rows, weights, last_cols)
+
+
+W_SHARDS = ((32, 4096), (128, 576), (128, 512))
 HALF_TOK = TOK // 2
 
 
@@ -265,14 +278,16 @@
     outs = refs[3 + n_w:3 + 2 * n_w]
     stage = refs[3 + 2 * n_w:3 + 3 * n_w]
     own, mate, way0, way1 = refs[3 + 3 * n_w:7 + 3 * n_w]
-    in_sem, own_sem, s_sem, r_sem, ps_sem, pr_sem, h_in, m_s, m_r, hs_sem, hr_sem, out_sem = refs[7 + 3 * n_w:]
+    in_sem, own_sem, s_sem, r_sem, ps_sem, pr_sem, os_sem, or_sem, xs_sem, xr_sem, ts_sem, tr_sem, h_in, m_s, m_r, hs_sem, hr_sem, out_sem = refs[7 + 3 * n_w:]
     me, core, pos = place()
+    twin = lax.axis_index('dp')
     partner = me + 1 - 2 * core
     barrier = pltpu.get_barrier_semaphore()
     peers = (at_pos(pos + 1, core), at_pos(pos + 7, core))
     for peer in peers + (partner,):
         pl.semaphore_signal(barrier, inc=1, device_id={'fsdp': peer}, device_id_type=MESH)
-    pl.semaphore_wait(barrier, 3)
+    pl.semaphore_signal(barrier, inc=1, device_id={'dp': 1 - twin}, device_id_type=MESH)
+    pl.semaphore_wait(barrier, 4)
     loads = []
     for i in range(n_w):
         cp = pltpu.make_async_copy(srcs[i], stage[i], in_sem.at[i])
@@ -289,27 +304,44 @@
         row_share((pos + j) % RING).start()
         row_load((pos + j) % RING).start()
 
-    def where(i, way, source):
+    def where(i, way, source, side):
         rows = W_SHARDS[i][0]
-        half = rows // 2
-        return outs[i].at[pl.ds(pl.multiple_of(source * rows + way * half, half), half), :]
+        part = rows // 4
+        return outs[i].at[pl.ds(pl.multiple_of(source * rows + side * 2 * part + way * part, part), part), :]
+
+    def whole(i):
+        rows = W_SHARDS[i][0]
+        return outs[i].at[pl.ds(pl.multiple_of(me * rows, rows), rows), :]
 
     def origin(way, step):
         return at_pos(pos + 8 - step + way * 2 * step, core)
 
     def hop(i, way, step, src=None):
-        spot = where(i, way, origin(way, step))
+        spot = where(i, way, origin(way, step), twin)
         return pltpu.make_async_remote_copy(spot if src is None else src, spot, s_sem.at[i, way, step], r_sem.at[i, way, step + 1],
                                             device_id={'fsdp': peers[way]}, device_id_type=MESH)
 
     def arrive(i, way, step):
-        spot = where(i, way, origin(way, step))
+        spot = where(i, way, origin(way, step), twin)
         return pltpu.make_async_remote_copy(spot, spot, s_sem.at[i, way, step], r_sem.at[i, way, step],
                                             device_id={'fsdp': peers[way]}, device_id_type=MESH)
 
-    def share(i, way, step, src=None):
-        spot = where(i, way, origin(way, step))
-        return pltpu.make_async_remote_copy(spot if src is None else src, spot, ps_sem.at[i, way, step], pr_sem.at[i, way, step],
+    def share(i, way, step):
+        spot = where(i, way, origin(way, step), twin)
+        return pltpu.make_async_remote_copy(spot, spot, ps_sem.at[i, way, step], pr_sem.at[i, way, step],
+                                            device_id={'fsdp': partner}, device_id_type=MESH)
+
+    def share_own(i):
+        return pltpu.make_async_remote_copy(stage[i], whole(i), os_sem.at[i], or_sem.at[i], device_id={'fsdp': partner}, device_id_type=MESH)
+
+    def to_twin(i, way, step):
+        spot = where(i, way, origin(way, step), twin)
+        return pltpu.make_async_remote_copy(spot, spot, xs_sem.at[i, way, step], xr_sem.at[i, way, step],
+                                            device_id={'dp': 1 - twin}, device_id_type=MESH)
+
+    def share_twin(i, way, step):
+        spot = where(i, way, origin(way, step), 1 - twin)
+        return pltpu.make_async_remote_copy(spot, spot, ts_sem.at[i, way, step], tr_sem.at[i, way, step],
                                             device_id={'fsdp': partner}, device_id_type=MESH)
     ways = (way0, way1)
 
@@ -332,14 +364,13 @@
     kept = []
     for i in range(n_w):
         loads[i].wait()
-        half = W_SHARDS[i][0] // 2
+        part = W_SHARDS[i][0] // 4
         for way in range(2):
-            src = stage[i].at[way * half:(way + 1) * half, :]
-            hop(i, way, 0, src).start()
-            share(i, way, 0, src).start()
-            cp = pltpu.make_async_copy(src, where(i, way, me), own_sem.at[i, way])
-            cp.start()
-            kept.append(cp)
+            hop(i, way, 0, stage[i].at[pl.ds(pl.multiple_of(twin * 2 * part + way * part, part), part), :]).start()
+        share_own(i).start()
+        cp = pltpu.make_async_copy(stage[i], whole(i), own_sem.at[i])
+        cp.start()
+        kept.append(cp)
     for j in (7, 1, 6, 2, 5, 3, 4, 0):
         row_load((pos + j) % RING).wait()
         row_share((pos + j) % RING).wait_recv()
@@ -358,6 +389,7 @@
                 def _():
                     hop(i, way, step).start()
                 share(i, way, step).start()
+                to_twin(i, way, step).start()
         for way in range(2):
             row_hop(way, step - 1).wait_recv()
             fill(way, step, False)
@@ -366,6 +398,17 @@
             def _():
                 row_hop(way, step).start()
 
+        @pl.when(step > 1)
+        def _():
+            for i in range(n_w):
+                for way in range(2):
+                    to_twin(i, way, step - 1).wait_recv()
+                    share_twin(i, way, step - 1).start()
+
+    for i in range(n_w):
+        for way in range(2):
+            to_twin(i, way, RING - 1).wait_recv()
+            share_twin(i, way, RING - 1).start()
     for way in range(2):
         cp = pltpu.make_async_copy(ways[way].at[RING - 1], got_h.at[way * HALF_TOK:(way + 1) * HALF_TOK, :], out_sem.at[way])
         cp.start()
@@ -386,7 +429,14 @@
                 @pl.when(step < RING - 1)
                 def _():
                     hop(i, way, step).wait_send()
-                share(i, way, step).wait()
+
+                @pl.when(step > 0)
+                def _():
+                    share(i, way, step).wait()
+                    to_twin(i, way, step).wait_send()
+                    share_twin(i, way, step).wait()
+    for i in range(n_w):
+        share_own(i).wait()
 
 
 def spread(mask, rows, shards):
@@ -397,7 +447,7 @@
         out_shape=(jax.ShapeDtypeStruct((TOK, 2048), BF16),) + tuple(jax.ShapeDtypeStruct((GROUP * r, w), BF16) for r, w in W_SHARDS),
         in_specs=[pl.BlockSpec(memory_space=pltpu.VMEM)] + [ANY] * (n_w + 1), out_specs=(ANY,) * (n_w + 1),
         scratch_shapes=[pltpu.VMEM(s, BF16) for s in W_SHARDS] + [pltpu.VMEM((RING, TOK, 2048), BF16)] * 2 + [pltpu.VMEM((RING, HALF_TOK, 2048), BF16)] * 2
-        + [dma((max(n_w, 1),)), dma((max(n_w, 1), 2))] + [dma((max(n_w, 1), 2, RING)) for _ in range(4)] + [dma((RING,)) for _ in range(3)] + [dma((2, RING)) for _ in range(2)] + [dma((2,))],
+        + [dma((n_w,)), dma((n_w,))] + [dma((n_w, 2, RING))] * 4 + [dma((n_w,))] * 2 + [dma((n_w, 2, RING))] * 4 + [dma((RING,)) for _ in range(3)] + [dma((2, RING)) for _ in range(2)] + [dma((2,))],
         compiler_params=pltpu.CompilerParams(collective_id=2, has_side_effects=True, vmem_limit_bytes=60 * 1024 * 1024),
         cost_estimate=pl.CostEstimate(flops=8 * 10**9, bytes_accessed=27 * 10**6, transcendentals=0), name='spread',
     )(mask, rows, *shards)
@@ -553,7 +603,8 @@
     kv_up = jnp.dot(latent, w_kv_up, preferred_element_type=jnp.float32).astype(jnp.bfloat16)
     attn_mix, attn_pull = jax.vjp(attend_local, q_proj.reshape(seq_count, seq_len, -1, NOPE_DIM + ROPE_DIM), kv_down[:, kv_rank:].reshape(seq_count, seq_len, ROPE_DIM), kv_up.reshape(seq_count, seq_len, -1, NOPE_DIM + VALUE_DIM))
     mix_rows = attn_mix.reshape(tok_count, -1)
-    d_mix = lax.dot_general(grad_rows, w_out, COL_DIMS, preferred_element_type=jnp.float32).astype(jnp.bfloat16)
+    d_mix = lax.dot_general(grad_rows[:, :1536], w_out[0], COL_DIMS, preferred_element_type=jnp.float32)
+    d_mix = (d_mix + lax.dot_general(grad_rows[:, 1536:], w_out[1], COL_DIMS, preferred_element_type=jnp.float32)).astype(jnp.bfloat16)
     d_query, d_pe, d_up = attn_pull(d_mix.reshape(attn_mix.shape))
     d_query = d_query.reshape(tok_count, -1)
     d_up = d_up.reshape(tok_count, -1)
@@ -580,7 +631,7 @@
         tok_count = seq_count * seq_len
         me = lax.axis_index('fsdp')
         grad_rows = grad_out.reshape(tok_count, d_model)
-        bundle = lax.all_gather(jnp.concatenate([w_query, w_out, w_kv_down], axis=1), 'fsdp', tiled=True)
+        bundle = lax.all_gather(jnp.concatenate([w_query, w_out[:, :1536]], axis=1), 'fsdp', tiled=True)
         fill = lambda rows: jnp.pad(rows, ((0, 0), (0, 128 - rows.shape[1])))
         tile = jnp.concatenate([fill(tok_ids.astype(F32)), norm_gain.astype(F32).reshape(1, 128), fill(kv_gain.astype(F32).reshape(1, 32)), jnp.zeros((3, 128), F32)], axis=0)
         table = small_gather(tile)
@@ -601,15 +652,15 @@
         mask = jnp.stack([near == me, near == me + 1 - 2 * core]).astype(BF16)
         mask = jnp.broadcast_to(mask[..., None], (2, RING, tok_count, 128))
         picked, keys, starts, flags = lax.optimization_barrier((picked, keys, starts, flags))
-        tok_rows, full_kvb = spread(mask, picked.reshape(GROUP, tok_count, d_model), (w_kv_up,))
-        full_wq, full_wo, full_kva = bundle[:, :3072], bundle[:, 3072:5120], bundle[:, 5120:]
+        tok_rows, full_kvb, full_kva, wo_last = spread(mask, picked.reshape(GROUP, tok_count, d_model), (w_kv_up, w_kv_down, w_out[:, 1536:]))
+        full_wq, full_wo = bundle[:, :3072], (bundle[:, 3072:], wo_last)
         tok_rows, grad_rows = lax.optimization_barrier((tok_rows, grad_rows))
         all_dy = lax.all_gather(grad_rows, 'fsdp', tiled=True)
         d_normed, normed, mix, latent, d_query, d_down, d_up, d_gain, d_kv_gain = block_step(
             tok_rows.astype(F32), grad_rows, (gain_full, full_wq, full_kva, kv_gain_full, full_kvb, full_wo), seq_count)
         all_dn = lax.all_gather(d_normed, 'fsdp', tiled=True)
         small = jnp.concatenate([d_gain.reshape(GROUP, 1, 128), jnp.pad(d_kv_gain.reshape(GROUP, 1, 32), ((0, 0), (0, 0), (0, 96))), jnp.zeros((GROUP, 6, 128), F32)], axis=1)
-        block_out, g_out, g_query, g_down, g_up, g_small = grad_shards(mix, all_dy, normed.T, jnp.pad(d_down, ((0, 0), (0, D_DOWN - d_down.shape[1]))), d_query, latent.T, d_up, small, tok_rows, bundle)
+        block_out, g_out, g_query, g_down, g_up, g_small = grad_shards(mix, all_dy, normed.T, jnp.pad(d_down, ((0, 0), (0, D_DOWN - d_down.shape[1]))), d_query, latent.T, d_up, small, tok_rows, bundle, wo_last)
         grad_table = table_grad(starts, (keys >> 7) & 8191, keys & (ROW_BLK - 1), flags, gain_full.reshape(1, -1), all_dy, all_dn, picked, vocab_dev)
         return (block_out.reshape(seq_count, seq_len, d_model), grad_table, g_small[0], g_query, g_down[:, :576], g_small[1, :32], g_up, g_out)
 

time: 720 us -> 704 us (0.978)
  Pallas kernels: 522 us -> 502 us
    pallas_call x1, Pallas kernels: 161 us -> 141 us  [spread(): pl.pallas_call(lambda *refs: spread_kernel(n_w, *refs), out_shape=(jax.Sh...]
    unnamed x120 -> x116, local copies, waits for them, and re-layouts: 17.4 us -> 16.7 us
  transfers between devices with their start and end apart: 3 -> 3, of which waited for: 1 -> 0; matrix products, arithmetic and copies ran while one was open for 22% -> 23% of each run, Pallas kernels for 67% -> 66%
where the time goes in v4:
time: 704 us; the launch traced here: 693 us
  Pallas kernels  502 us (71%)
  local copies, waits for them, and re-layouts  99.1 us (14%)
  matrix products  46.2 us (7%)
  other arithmetic  30.6 us (4%)
  between operations  15.1 us (2%)
    pallas_call x1, Pallas kernels, grad_shards(): pl.pallas_call(grad_kernel, out_shape=(jax.ShapeDtypeStruct((TOK, 2048),...  304 us
    pallas_call x1, Pallas kernels, spread(): pl.pallas_call(lambda *refs: spread_kernel(n_w, *refs), out_shape=(jax.Sh...  141 us
    gather x1, local copies, waits for them, and re-layouts, device_step(): jnp.take(emb_table, jnp.where(mine, local, 0).reshape(-1), axis=0, mode='...  46.9 us
    pallas_call x1, Pallas kernels, table_grad(): pl.pallas_call(table_kernel, out_shape=jax.ShapeDtypeStruct((vocab_dev, 2...  46.7 us
    unnamed x116, local copies, waits for them, and re-layouts  16.7 us
  transfers between devices with their start and end apart: 3, of which 0 were waited for; matrix products, arithmetic and copies ran while one was open for 23% of the time, Pallas kernels for 66%

profile of v4, /device:TPU:0, one launch (start us, length us, event | category | flops | bytes accessed | tf_op | source)
XLA Modules:
  0.0 693.0 jit_solution(16464411340507692285)
XLA Ops:
  8.3 2.2 pad_maximum_fusion
  11.4 10.2 %small_gather.1 = f32[16,8,128]{2,1,0:T(8,128)} custom-call(f32[8,128]{1,0:T(8,128)} %fusion.90.src), custom_call_target="tpu_custom_call" | custom-call | flops 10000000 | bytes 100000 | tf_op jit(solution)/shard_map/small_gather/pallas_call | solution.py:581
  24.6 1.6 slice.67.refs_4_
  26.4 46.9 %gather_fusion = bf16[4608,2048]{1,0:T(8,128)(2,1)} fusion(bf16[6400,2048]{1,0:T(8,128)(2,1)} %param.11, s32[5120]{0:T(1024)S(1)} %pad_clamp_fusion), kind=kCustom, calls=%fused_computation | custom fusion | bytes 37767168 | tf_op jit(solution)/shard_map/jit(_take)/gather | solution.py:649
  73.4 6.8 sort.14
  80.9 1.7 convert_reduce_fusion.starts
  83.6 1.6 broadcast_in_dim.68.refs_0_
  85.1 140.8 %spread.1 = (bf16[288,2048]{1,0:T(8,128)(2,1)}, bf16[512,4096]{1,0:T(8,128)(2,1)}, bf16[2048,576]{1,0:T(8,128)(2,1)}, bf16[2048,512]{1,0:T(8,128)(2,1)}) custom-call(bf16[2,8,288,128]{3,2,1,0:T(8,128)(2,1)} %broadcast_in_dim.68.refs_0_, bf16[16,288,2048]{2,1,0:T(8,128)(2,1)} %bitcast.119, bf16[32,4096]{1,0:T(8,128)(2,1)} %refs_2_.1, ...), custom_call_target="tpu_custom_call" | custom-call | flops 8000000000 | bytes 27000000 | tf_op jit(solution)/shard_map/spread/pallas_call | solution.py:445
  227.1 1.6 fusion.15
  230.1 3.3 convolution_convert_fusion.7
  234.2 1.6 convolution_convert_fusion
  237.2 1.7 reshape.404
  238.9 1.6 copy.126
  241.2 1.5 copy.131
  242.7 1.5 copy.130
  245.6 1.6 fusion.74
  247.2 1.8 fusion.100
  249.0 9.8 %fusion.6 = bf16[288,3072]{1,0:T(8,128)(2,1)} fusion(bf16[2048,4608]{1,0:T(8,128)(2,1)} %all-gather.4.cloned.1.call-done.wo_h, bf16[288,2048]{1,0:T(8,128)(2,1)S(1)} %copy-done, f32[2048]{0:T(1024)} %bitcast.137, f32[288]{0:T(512)} %copy-done.45), kind=kOutput, calls=%fused_computation.8 | convolution fusion | flops 3627122688 | bytes 15542272 | tf_op jit(solution)/shard_map/dot_general | solution.py:600
  258.8 4.2 reshape.393
  264.2 5.3 fusion.4
  275.7 1.6 copy-done.20
  284.2 2.7 copy.142
  286.9 4.8 reshape.398.dq_h
  293.9 2.8 fusion.42
  302.9 3.1 fusion.62
  307.1 7.4 %fusion = f32[288,2048]{1,0:T(8,128)S(1)} fusion(bf16[288,3072]{1,0:T(8,128)(2,1)S(1)} %copy-done.5, bf16[2048,4608]{1,0:T(8,128)(2,1)} %all-gather.4.cloned.1.call-done.wo_h), kind=kOutput, calls=%fused_computation.1 | convolution fusion | flops 3623878656 | bytes 16711680 | tf_op jit(solution)/shard_map/dot_general | solution.py:614
  314.5 2.3 fusion.12
  318.3 2.0 fusion.41
  322.9 1.5 copy.143.nrm_h
  326.3 304.0 %grad_shards.1 = (bf16[288,2048]{1,0:T(8,128)(2,1)}, f32[128,2048]{1,0:T(8,128)}, f32[128,3072]{1,0:T(8,128)}, f32[128,640]{1,0:T(8,128)}, f32[32,4096]{1,0:T(8,128)}, /*index=5*/f32[8,128]{1,0:T(8,128)}) custom-call(bf16[288,2048]{1,0:T(8,128)(2,1)} %bitcast.125, bf16[4608,2048]{1,0:T(8,128)(2,1)} %all-gather.6.cloned.1.call-done.dy_h, ...), custom_call_target="tpu_custom_call" | custom-call | flops 8000000000 | bytes 20000000 | tf_op jit(solution)/shard_map/grad_shards/pallas_call | solution.py:261
  630.3 1.8 copy.145
  634.5 46.7 %table_grad.1 = bf16[6400,2048]{1,0:T(8,128)(2,1)} custom-call(s32[51]{0:T(128)} %convert_reduce_fusion.starts, s32[4608]{0:T(1024)} %get-tuple-element.110.toks, s32[4608]{0:T(1024)} %get-tuple-element.109.rows, s32[96]{0:T(128)} %convert_reduce_fusion.1.flags, f32[1,2048]{1,0:T(1,128)} %get-tuple-element.103.gain, ...), custom_call_target="tpu_custom_call" | custom-call | flops 1000000000 | bytes 80000000 | tf_op jit(solution)/shard_map/table_grad/pallas_call | solution.py:554
  (209 shorter events, 49.8 us)
Async XLA Ops:
  7.2 3.4 copy-start.48
  7.2 3.5 copy-start.49
  7.2 3.5 copy-start.50
  7.2 241.8 %all-gather.4.cloned.1.call-start = ((), (), s32[]{:S(2)}) async-start(), calls=%async_computation | async-start | bytes 20054016 | tf_op jit(solution)/shard_map/all_gather | solution.py:634
  10.5 315.8 %all-gather.6.cloned.1.call-start = ((), (), s32[]{:S(2)}) async-start(), calls=%async_computation.1 | async-start | bytes 20054016 | tf_op jit(solution)/shard_map/all_gather | solution.py:658
  26.4 56.3 %copy-start.35 = (bf16[128,576]{0,1:T(8,128)(2,1)S(1)}, bf16[128,576]{0,1:T(8,128)(2,1)}, u32[]{:S(2)}) copy-start(bf16[128,576]{0,1:T(8,128)(2,1)} %param.14) | copy-start | bytes 442372
  225.9 4.2 copy-start
  226.0 408.6 %all-gather.8.cloned.1.call-start = ((), (), s32[]{:S(2)}) async-start(), calls=%async_computation.2 | async-start | bytes 20054016 | tf_op jit(solution)/shard_map/all_gather | solution.py:661
  230.1 3.4 copy-start.37
  230.1 4.1 copy-start.10
  233.5 3.1 copy-start.12
  264.2 9.5 %copy-start.7 = (bf16[3,96,16,128]{3,2,1,0:T(8,128)(2,1)}, bf16[3,96,16,128]{3,2,1,0:T(8,128)(2,1)S(1)}, u32[]{:S(2)}) copy-start(bf16[3,96,16,128]{3,2,1,0:T(8,128)(2,1)S(1)} %slice.93) | copy-start | bytes 3538948
  264.2 5.3 copy-start.4
  270.6 5.1 copy-start.18
  275.2 7.0 %copy-start.2 = (f32[3,16,96,96]{2,3,1,0:T(8,128)}, f32[3,16,96,96]{2,3,1,0:T(8,128)S(1)}, u32[]{:S(2)}) copy-start(f32[3,16,96,96]{2,3,1,0:T(8,128)S(1)} %get-tuple-element.86) | copy-start | bytes 5308420
  275.2 7.0 %copy-start.31 = (f32[3,16,96]{2,1,0:T(8,128)}, f32[3,16,96]{2,1,0:T(8,128)S(1)}, u32[]{:S(2)}) copy-start(f32[3,16,96]{2,1,0:T(8,128)S(1)} %get-tuple-element.85) | copy-start | bytes 55300
  275.7 6.4 copy-start.29
  278.6 3.5 copy-start.21
  278.6 3.5 copy-start.39
  293.9 3.1 copy-start.8
  293.9 3.4 copy-start.22
  293.9 3.4 copy-start.30
  293.9 3.4 copy-start.32
  293.9 3.4 copy-start.40
  301.3 4.7 copy-start.1
  302.9 3.1 copy-start.44
  302.9 4.1 copy-start.5
  307.0 7.4 %copy-start.16 = (bf16[288,512]{0,1:T(8,128)(2,1)}, bf16[288,512]{0,1:T(8,128)(2,1)S(1)}, u32[]{:S(2)}) copy-start(bf16[288,512]{0,1:T(8,128)(2,1)S(1)} %get-tuple-element.98) | copy-start | bytes 884740
  307.1 7.4 %copy-start.33 = (bf16[288,64]{0,1:T(8,128)(2,1)S(1)}, bf16[288,64]{0,1:T(8,128)(2,1)}, u32[]{:S(2)}) copy-start(bf16[288,64]{0,1:T(8,128)(2,1)} %reshape.397) | copy-start | bytes 110596
  307.1 7.4 %copy-start.51 = (bf16[2048,576]{1,0:T(8,128)(2,1)S(1)}, bf16[2048,576]{1,0:T(8,128)(2,1)}, u32[]{:S(2)}) copy-start(bf16[2048,576]{1,0:T(8,128)(2,1)} %get-tuple-element.30) | copy-start | bytes 7077892
  634.5 46.7 %copy-start.19 = (bf16[288,2048]{1,0:T(8,128)(2,1)S(1)}, bf16[288,2048]{1,0:T(8,128)(2,1)}, u32[]{:S(2)}) copy-start(bf16[288,2048]{1,0:T(8,128)(2,1)} %get-tuple-element.34) | copy-start | bytes 3538948
  681.3 3.0 copy-start.24
  (23 other events, 38.7 us)
Sparse Core Ops, SparseCore 0:
  10.6 121.4 all-gather.3
  226.1 98.7 all-gather.5
  326.5 197.2 all-gather.7

commit v5 on v4

--- a/solution.py
+++ b/solution.py
@@ -83,7 +83,7 @@
 D_OUT, D_CAT, D_UP, D_DOWN = 2048, 3712, 4096, 640
 WO_COL = 3072
 CUT = 1792
-PARTS = (('u', 0, 0, 2048), ('u', 1, 2048, 2048), ('n', 0, 0, 896), ('n', 1, 1792, 1024), ('n', 0, 896, 896), ('n', 1, 2816, 896))
+PARTS = (('u', 0, 0, 2304), ('u', 1, 2304, 1792), ('n', 0, 0, 896), ('n', 1, 1792, 1024), ('n', 0, 896, 896), ('n', 1, 2816, 896))
 N_PARTS = len(PARTS)
 ROWS = {'n': 128, 'u': 32}
 
@@ -157,13 +157,18 @@
     go[...] = jnp.zeros_like(go)
     for p in range(N_PARTS):
         bufs[p][0] = jnp.zeros(bufs[p].shape[1:], F32)
-    for i in range(5):
-        local[i].wait()
-        cross[i].wait_recv()
+    first_use = {0: (0, 1), 2: (2, 3, 4)}
 
     @pl.loop(0, RING)
     def _(step):
         for p in range(N_PARTS):
+            if p in first_use:
+                @pl.when(step == 0)
+                def _():
+                    for i in first_use[p]:
+                        local[i].wait()
+                        cross[i].wait_recv()
+
             @pl.when(step > 0)
             def _():
                 hop(p, step - 1).wait_recv()
@@ -225,7 +230,7 @@
     cp = pltpu.make_async_copy(yv, y_h, out_sem.at[9])
     cp.start()
     outs.append(cp)
-    targets = (((gu_h.at[:, 0:2048], 0, 2048),), ((gu_h.at[:, 2048:4096], 0, 2048),), ((gd_h, 0, 640), (gq_h.at[:, 0:256], 640, 896)),
+    targets = (((gu_h.at[:, 0:2304], 0, 2304),), ((gu_h.at[:, 2304:4096], 0, 1792),), ((gd_h, 0, 640), (gq_h.at[:, 0:256], 640, 896)),
                ((gq_h.at[:, 1152:2176], 0, 1024),), ((gq_h.at[:, 256:1152], 0, 896),), ((gq_h.at[:, 2176:3072], 0, 896),))
     for p in range(N_PARTS):
         for n, (dst, c0, c1) in enumerate(targets[p]):
@@ -460,7 +465,16 @@
 OUT_SLOTS = 4
 
 
-def table_kernel(starts, toks, rows, flags, gain, dy_h, dn_h, h_h, out_h, grad, dy, dn, hh, acc, ob, nil, in_sem, out_sem):
+def table_kernel(starts, toks, rows, flags, gain, small, dy_h, dn_h, h_h, *refs):
+    passed, out_h, given, gain_out, kv_out = refs[0:5], refs[5], refs[6:11], refs[11], refs[12]
+    grad, dy, dn, hh, acc, ob, nil, in_sem, out_sem = refs[13:22]
+    hold, cut, ride_in, ride_out = refs[22:27], refs[27], refs[28], refs[29]
+    boards = [pltpu.make_async_copy(src, dst, ride_in.at[i]) for i, (src, dst) in enumerate(zip(passed, hold))]
+    leaves = [pltpu.make_async_copy(cut if i == 2 else src, dst, ride_out.at[i]) for i, (src, dst) in enumerate(zip(hold, given))]
+    for cp in boards:
+        cp.start()
+    gain_out[...] = small[0:1, :]
+    kv_out[...] = small[1:2, 0:32]
     n_in = GROUP * TOK // IN_BLK
     n_out = out_h.shape[0] // ROW_BLK
 
@@ -509,6 +523,12 @@
                         s = tile(dn, p, c) * gain[:, c:c + 128]
                         grad[pl.ds(o0 + p, PIECE), c:c + 128] = tile(dy, p, c) + inv * s - coef * tile(hh, p, c)
 
+    for cp in boards:
+        cp.wait()
+    cut[...] = hold[2][...].T[0:576, :]
+    for cp in leaves:
+        cp.start()
+
     def store(blk, src):
         return pltpu.make_async_copy(src, out_h.at[pl.ds(pl.multiple_of(blk * ROW_BLK, ROW_BLK), ROW_BLK), :], out_sem.at[blk % OUT_SLOTS])
     nil[...] = jnp.zeros_like(nil)
@@ -546,18 +566,25 @@
             store(blk, ob.at[slot]).start()
     for blk in range(n_out - OUT_SLOTS, n_out):
         store(blk, nil).wait()
-
-
-def table_grad(starts, toks, rows, flags, gain, dy_all, dn_all, picked, vocab_dev):
+    for cp in leaves:
+        cp.wait()
+
+
+def table_grad(starts, toks, rows, flags, gain, small, dy_all, dn_all, picked, vocab_dev, passed):
     smem = pl.BlockSpec(memory_space=pltpu.SMEM)
+    vmem = pl.BlockSpec(memory_space=pltpu.VMEM)
     dma = pltpu.SemaphoreType.DMA
+    shapes = [jax.ShapeDtypeStruct((vocab_dev, 2048), BF16)] + [jax.ShapeDtypeStruct((576, 128) if i == 2 else p.shape, p.dtype) for i, p in enumerate(passed)]
+    shapes += [jax.ShapeDtypeStruct((1, 128), F32), jax.ShapeDtypeStruct((1, 32), F32)]
     return pl.pallas_call(
-        table_kernel, out_shape=jax.ShapeDtypeStruct((vocab_dev, 2048), BF16),
-        in_specs=[smem] * 4 + [pl.BlockSpec(memory_space=pltpu.VMEM)] + [ANY] * 3, out_specs=ANY,
-        scratch_shapes=[pltpu.VMEM((GROUP * TOK, 2048), F32)] + [pltpu.VMEM((IN_SLOTS, IN_BLK, 2048), BF16)] * 3 + [pltpu.VMEM((ROW_BLK, 2048), F32), pltpu.VMEM((OUT_SLOTS, ROW_BLK, 2048), BF16), pltpu.VMEM((ROW_BLK, 2048), BF16), dma((3, IN_SLOTS)), dma((OUT_SLOTS,))],
-        compiler_params=pltpu.CompilerParams(vmem_limit_bytes=60 * 1024 * 1024),
-        cost_estimate=pl.CostEstimate(flops=10**9, bytes_accessed=80 * 10**6, transcendentals=0), name='table_grad',
-    )(starts, toks, rows, flags, gain, dy_all, dn_all, picked)
+        table_kernel, out_shape=tuple(shapes),
+        in_specs=[smem] * 4 + [vmem] * 2 + [ANY] * 8, out_specs=(ANY,) * 6 + (vmem,) * 2,
+        scratch_shapes=[pltpu.VMEM((GROUP * TOK, 2048), F32)] + [pltpu.VMEM((IN_SLOTS, IN_BLK, 2048), BF16)] * 3
+        + [pltpu.VMEM((ROW_BLK, 2048), F32), pltpu.VMEM((OUT_SLOTS, ROW_BLK, 2048), BF16), pltpu.VMEM((ROW_BLK, 2048), BF16), dma((3, IN_SLOTS)), dma((OUT_SLOTS,))]
+        + [pltpu.VMEM(p.shape, p.dtype) for p in passed] + [pltpu.VMEM((576, 128), F32), dma((5,)), dma((5,))],
+        compiler_params=pltpu.CompilerParams(vmem_limit_bytes=63 * 1024 * 1024),
+        cost_estimate=pl.CostEstimate(flops=10**9, bytes_accessed=90 * 10**6, transcendentals=0), name='table_grad',
+    )(starts, toks, rows, flags, gain, small, dy_all, dn_all, picked, *passed)
 
 
 def small_kernel(src, out, loc_sem, s_sem, r_sem):
@@ -651,7 +678,7 @@
         near = lax.dynamic_index_in_dim(owner.reshape(RING, 2, tok_count), core, 1, keepdims=False)
         mask = jnp.stack([near == me, near == me + 1 - 2 * core]).astype(BF16)
         mask = jnp.broadcast_to(mask[..., None], (2, RING, tok_count, 128))
-        picked, keys, starts, flags = lax.optimization_barrier((picked, keys, starts, flags))
+        picked, keys, starts, flags, w_kv_down = lax.optimization_barrier((picked, keys, starts, flags, w_kv_down))
         tok_rows, full_kvb, full_kva, wo_last = spread(mask, picked.reshape(GROUP, tok_count, d_model), (w_kv_up, w_kv_down, w_out[:, 1536:]))
         full_wq, full_wo = bundle[:, :3072], (bundle[:, 3072:], wo_last)
         tok_rows, grad_rows = lax.optimization_barrier((tok_rows, grad_rows))
@@ -661,7 +688,9 @@
         all_dn = lax.all_gather(d_normed, 'fsdp', tiled=True)
         small = jnp.concatenate([d_gain.reshape(GROUP, 1, 128), jnp.pad(d_kv_gain.reshape(GROUP, 1, 32), ((0, 0), (0, 0), (0, 96))), jnp.zeros((GROUP, 6, 128), F32)], axis=1)
         block_out, g_out, g_query, g_down, g_up, g_small = grad_shards(mix, all_dy, normed.T, jnp.pad(d_down, ((0, 0), (0, D_DOWN - d_down.shape[1]))), d_query, latent.T, d_up, small, tok_rows, bundle, wo_last)
-        grad_table = table_grad(starts, (keys >> 7) & 8191, keys & (ROW_BLK - 1), flags, gain_full.reshape(1, -1), all_dy, all_dn, picked, vocab_dev)
-        return (block_out.reshape(seq_count, seq_len, d_model), grad_table, g_small[0], g_query, g_down[:, :576], g_small[1, :32], g_up, g_out)
+        grad_table, block_out, g_query, g_down, g_up, g_out, g_gain, g_kv_gain = table_grad(
+            starts, (keys >> 7) & 8191, keys & (ROW_BLK - 1), flags, gain_full.reshape(1, -1), g_small, all_dy, all_dn, picked, vocab_dev,
+            (block_out, g_query, g_down, g_up, g_out))
+        return (block_out.reshape(seq_count, seq_len, d_model), grad_table, g_gain.reshape(-1), g_query, g_down.T, g_kv_gain.reshape(-1), g_up, g_out)
 
     return jax.shard_map(device_step, mesh=mesh, in_specs=(tok_spec, seq_spec, mat_spec, vec_spec, mat_spec, mat_spec, vec_spec, mat_spec, mat_spec), out_specs=(seq_spec, tok_spec, part_vec, tok_spec, tok_spec, part_vec, tok_spec, tok_spec), check_vma=False)

time: 704 us -> 690 us (0.980)
  local copies, waits for them, and re-layouts: 99.1 us -> 89.3 us
    unnamed x116 -> x106, local copies, waits for them, and re-layouts: 16.7 us -> 10.3 us
  transfers between devices with their start and end apart: 3 -> 3, of which waited for: 0 -> 1; matrix products, arithmetic and copies ran while one was open for 23% -> 23% of each run, Pallas kernels for 66% -> 66%
where the time goes in v5:
time: 690 us; the launch traced here: 681 us
  Pallas kernels  500 us (72%)
  local copies, waits for them, and re-layouts  89.3 us (13%)
  matrix products  47.9 us (7%)
  other arithmetic  28.1 us (4%)
  between operations  15.2 us (2%)
    pallas_call x1, Pallas kernels, grad_shards(): pl.pallas_call(grad_kernel, out_shape=(jax.ShapeDtypeStruct((TOK, 2048),...  299 us
    pallas_call x1, Pallas kernels, spread(): pl.pallas_call(lambda *refs: spread_kernel(n_w, *refs), out_shape=(jax.Sh...  141 us
    pallas_call x1, Pallas kernels, table_grad(): pl.pallas_call(table_kernel, out_shape=tuple(shapes), in_specs=[smem] * 4...  49.5 us
    gather x1, local copies, waits for them, and re-layouts, device_step(): jnp.take(emb_table, jnp.where(mine, local, 0).reshape(-1), axis=0, mode='...  46.9 us
  transfers between devices with their start and end apart: 3, of which 1 were waited for; matrix products, arithmetic and copies ran while one was open for 23% of the time, Pallas kernels for 66%

profile of v5, /device:TPU:0, one launch (start us, length us, event | category | flops | bytes accessed | tf_op | source)
XLA Modules:
  0.0 680.5 jit_solution(16418209806651523571)
XLA Ops:
  8.3 2.2 pad_maximum_fusion
  11.4 10.2 %small_gather.1 = f32[16,8,128]{2,1,0:T(8,128)} custom-call(f32[8,128]{1,0:T(8,128)} %fusion.90.src), custom_call_target="tpu_custom_call" | custom-call | flops 10000000 | bytes 100000 | tf_op jit(solution)/shard_map/small_gather/pallas_call | solution.py:608
  24.6 1.6 slice.59.refs_4_
  26.3 6.8 %sort.14 = (s32[4608]{0:T(1024)}, s32[4608]{0:T(1024)}) sort(s32[4608]{0:T(1024)S(1)} %fusion.83, s32[4608]{0:T(1024)S(1)} %iota.41), dimensions={0}, to_apply=%region_0.1 | sort | flops 59904 | bytes 73728 | tf_op jit(solution)/shard_map/sort | solution.py:673
  33.3 46.9 %gather_fusion = bf16[4608,2048]{1,0:T(8,128)(2,1)} fusion(bf16[6400,2048]{1,0:T(8,128)(2,1)} %param.11, s32[5120]{0:T(1024)S(1)} %pad_clamp_fusion), kind=kCustom, calls=%fused_computation | custom fusion | bytes 37767168 | tf_op jit(solution)/shard_map/jit(_take)/gather | solution.py:676
  80.8 1.7 convert_reduce_fusion.starts
  83.5 1.6 broadcast_in_dim.69.refs_0_
  85.0 140.9 %spread.1 = (bf16[288,2048]{1,0:T(8,128)(2,1)}, bf16[512,4096]{1,0:T(8,128)(2,1)}, bf16[2048,576]{1,0:T(8,128)(2,1)}, bf16[2048,512]{1,0:T(8,128)(2,1)}) custom-call(bf16[2,8,288,128]{3,2,1,0:T(8,128)(2,1)} %broadcast_in_dim.69.refs_0_, bf16[16,288,2048]{2,1,0:T(8,128)(2,1)} %bitcast.117, bf16[32,4096]{1,0:T(8,128)(2,1)} %refs_2_.1, ...), custom_call_target="tpu_custom_call" | custom-call | flops 8000000000 | bytes 27000000 | tf_op jit(solution)/shard_map/spread/pallas_call | solution.py:450
  228.6 1.6 fusion.15
  230.2 1.4 fusion.102
  231.6 3.2 convolution_convert_fusion.7
  235.2 3.7 convolution_convert_fusion
  240.9 1.8 fusion.100
  242.8 9.7 %fusion.6 = bf16[288,3072]{1,0:T(8,128)(2,1)} fusion(bf16[2048,4608]{1,0:T(8,128)(2,1)} %all-gather.4.cloned.1.call-done.wo_h, bf16[288,2048]{1,0:T(8,128)(2,1)S(1)} %copy-done, f32[2048]{0:T(1024)S(1)} %bitcast.133, f32[288]{0:T(512)S(1)} %add_rsqrt_fusion), kind=kOutput, calls=%fused_computation.8 | convolution fusion | flops 3627122688 | bytes 15541376 | tf_op jit(solution)/shard_map/dot_general | solution.py:627
  252.5 4.2 reshape.399
  257.9 4.9 fusion.4
  269.1 1.6 copy-done.15
  274.4 1.3 copy.132
  275.7 2.7 copy.160
  281.2 1.6 reshape.403
  282.7 1.4 convert_multiply_fusion.1
  288.8 2.7 copy.138
  291.6 5.0 reshape.404.dq_h
  296.6 5.4 fusion.62
  303.1 7.4 %fusion = f32[288,2048]{1,0:T(8,128)S(1)} fusion(bf16[288,3072]{1,0:T(8,128)(2,1)S(1)} %copy-done.6, bf16[2048,4608]{1,0:T(8,128)(2,1)} %all-gather.4.cloned.1.call-done.wo_h), kind=kOutput, calls=%fused_computation.1 | convolution fusion | flops 3623878656 | bytes 16711680 | tf_op jit(solution)/shard_map/dot_general | solution.py:641
  310.5 2.3 fusion.12
  313.5 1.3 broadcast_and_fusion
  314.8 2.0 fusion.41
  317.4 1.3 copy.196
  321.7 1.5 copy.139.nrm_h
  324.9 299.0 %grad_shards.1 = (bf16[288,2048]{1,0:T(8,128)(2,1)}, f32[128,2048]{1,0:T(8,128)}, f32[128,3072]{1,0:T(8,128)}, f32[128,640]{1,0:T(8,128)}, f32[32,4096]{1,0:T(8,128)}, /*index=5*/f32[8,128]{1,0:T(8,128)}) custom-call(bf16[288,2048]{1,0:T(8,128)(2,1)} %bitcast.123, bf16[4608,2048]{1,0:T(8,128)(2,1)} %all-gather.6.cloned.1.call-done.dy_h, ...), custom_call_target="tpu_custom_call" | custom-call | flops 8000000000 | bytes 20000000 | tf_op jit(solution)/shard_map/grad_shards/pallas_call | solution.py:266
  624.0 49.5 %table_grad.1 = (bf16[6400,2048]{1,0:T(8,128)(2,1)}, bf16[288,2048]{1,0:T(8,128)(2,1)}, f32[128,3072]{1,0:T(8,128)}, f32[576,128]{1,0:T(8,128)}, f32[32,4096]{1,...) custom-call(s32[51]{0:T(128)} %convert_reduce_fusion.starts, s32[4608]{0:T(1024)} %get-tuple-element.88.toks, ...), custom_call_target="tpu_custom_call" | custom-call | flops 1000000000 | bytes 90000000 | tf_op jit(solution)/shard_map/table_grad/pallas_call | solution.py:579
  (198 shorter events, 36.5 us)
Async XLA Ops:
  7.2 3.4 copy-start.45
  7.2 3.5 copy-start.47
  7.2 3.5 copy-start.48
  7.2 235.5 %all-gather.4.cloned.1.call-start = ((), (), s32[]{:S(2)}) async-start(), calls=%async_computation | async-start | bytes 20054016 | tf_op jit(solution)/shard_map/all_gather | solution.py:661
  10.5 314.4 %all-gather.6.cloned.1.call-start = ((), (), s32[]{:S(2)}) async-start(), calls=%async_computation.1 | async-start | bytes 20054016 | tf_op jit(solution)/shard_map/all_gather | solution.py:685
  33.3 49.3 %copy-start.32 = (bf16[128,576]{0,1:T(8,128)(2,1)S(1)}, bf16[128,576]{0,1:T(8,128)(2,1)}, u32[]{:S(2)}) copy-start(bf16[128,576]{0,1:T(8,128)(2,1)} %param.14) | copy-start | bytes 442372
  225.9 5.7 copy-start
  226.0 398.0 %all-gather.8.cloned.1.call-start = ((), (), s32[]{:S(2)}) async-start(), calls=%async_computation.2 | async-start | bytes 20054016 | tf_op jit(solution)/shard_map/all_gather | solution.py:688
  226.2 14.1 %copy-start.18 = (f32[96,64]{0,1:T(8,128)}, f32[96,64]{0,1:T(8,128)S(1)}, u32[]{:S(2)}) copy-start(f32[96,64]{0,1:T(8,128)S(1)} %get-tuple-element.90) | copy-start | bytes 73732
  226.2 14.1 %copy-start.20 = (f32[96,64]{0,1:T(8,128)}, f32[96,64]{0,1:T(8,128)S(1)}, u32[]{:S(2)}) copy-start(f32[96,64]{0,1:T(8,128)S(1)} %get-tuple-element.89) | copy-start | bytes 73732
  230.2 12.6 %copy-start.43 = (f32[288]{0:T(512)}, f32[288]{0:T(512)S(1)}, u32[]{:S(2)}) copy-start(f32[288]{0:T(512)S(1)} %add_rsqrt_fusion) | copy-start | bytes 3460
  231.6 11.1 %copy-start.34 = (f32[16,1,128]{2,1,0:T(1,128)}, f32[16,1,128]{2,1,0:T(1,128)S(1)}, u32[]{:S(2)}) copy-start(f32[16,1,128]{2,1,0:T(1,128)S(1)} %get-tuple-element.81) | copy-start | bytes 24580
  234.8 4.0 copy-start.9
  235.1 3.7 copy-start.41
  235.1 3.7 copy-start.39
  257.9 5.0 copy-start.5
  268.5 4.2 copy-start.2
  268.6 9.9 %copy-start.28 = (f32[3,16,96]{2,1,0:T(8,128)}, f32[3,16,96]{2,1,0:T(8,128)S(1)}, u32[]{:S(2)}) copy-start(f32[3,16,96]{2,1,0:T(8,128)S(1)} %get-tuple-element.63) | copy-start | bytes 55300
  269.1 9.3 %copy-start.26 = (f32[3,16,96]{2,1,0:T(8,128)}, f32[3,16,96]{2,1,0:T(8,128)S(1)}, u32[]{:S(2)}) copy-start(f32[3,16,96]{2,1,0:T(8,128)S(1)} %fusion.38) | copy-start | bytes 55300
  272.0 6.5 copy-start.16
  275.7 2.7 copy-start.33
  291.6 5.0 copy-start.1
  291.6 5.0 copy-start.40
  296.5 5.5 copy-start.42
  296.5 5.5 copy-start.10
  296.5 6.5 copy-start.6
  303.1 7.4 %copy-start.12 = (bf16[288,512]{0,1:T(8,128)(2,1)}, bf16[288,512]{0,1:T(8,128)(2,1)S(1)}, u32[]{:S(2)}) copy-start(bf16[288,512]{0,1:T(8,128)(2,1)S(1)} %get-tuple-element.76) | copy-start | bytes 884740
  303.1 7.4 %copy-start.30 = (bf16[288,64]{0,1:T(8,128)(2,1)S(1)}, bf16[288,64]{0,1:T(8,128)(2,1)}, u32[]{:S(2)}) copy-start(bf16[288,64]{0,1:T(8,128)(2,1)} %reshape.403) | copy-start | bytes 110596
  303.1 7.4 %copy-start.49 = (bf16[2048,576]{1,0:T(8,128)(2,1)S(1)}, bf16[2048,576]{1,0:T(8,128)(2,1)}, u32[]{:S(2)}) copy-start(bf16[2048,576]{1,0:T(8,128)(2,1)} %get-tuple-element.43) | copy-start | bytes 7077892
  310.5 4.3 copy-start.4
  317.4 3.0 copy-start.7
  317.4 3.0 copy-start.35
  (21 other events, 33.8 us)
Sparse Core Ops, SparseCore 0:
  10.6 121.5 all-gather.3
  226.1 98.7 all-gather.5
  326.5 195.8 all-gather.7

commit v6 on v5

--- a/solution.py
+++ b/solution.py
@@ -80,6 +80,8 @@
     pl.semaphore_wait(barrier, GROUP - 1)
 
 TOK = 288
+IN_BLK = 144
+PIECE = 16
 D_OUT, D_CAT, D_UP, D_DOWN = 2048, 3712, 4096, 640
 WO_COL = 3072
 CUT = 1792
@@ -91,8 +93,8 @@
     step = 512
     return [(c, min(step, width - c)) for c in range(0, width, step)]
 
-def grad_kernel(mix_h, dy_h, nrm_h, dd_h, dq_h, lat_h, du_h, sm_h, h0_h, wo_h, wl_h, y_h, go_h, gq_h, gd_h, gu_h, gs_h,
-                mix, dy, go, nrm, cat, lat, du, b0, b1, b2, b3, b4, b5, mixf, h0, wo, yv, smr, ssum, loc_sem, xs_sem, xr_sem, s_sem, r_sem, ms_sem, mr_sem, cs_sem, cr_sem, dy_sem, y_sem, out_sem):
+def grad_kernel(mix_h, dy_h, nrm_h, dd_h, dq_h, lat_h, du_h, sm_h, h0_h, wo_h, wl_h, dn_h, h_h, gain, y_h, dn_all, grad_h, go_h, gq_h, gd_h, gu_h, gs_h,
+                mix, dy, go, nrm, cat, lat, du, b0, b1, b2, b3, b4, b5, mixf, h0, wo, yv, own_dn, fdn, fdy, fh, fo, smr, ssum, loc_sem, xs_sem, xr_sem, s_sem, r_sem, ms_sem, mr_sem, cs_sem, cr_sem, dy_sem, y_sem, ns_sem, nr_sem, np_sem, nq_sem, f_sem, fo_sem, out_sem):
     me, core, pos = place()
     partner = me + 1 - 2 * core
     meet_all(me)
@@ -105,6 +107,85 @@
         rc = pltpu.make_async_remote_copy(src, dst.at[core], xs_sem.at[i], xr_sem.at[i], device_id={'fsdp': partner}, device_id_type=MESH)
         rc.start()
         cross.append(rc)
+    peers = (at_pos(pos + 1, core), at_pos(pos + 7, core))
+
+    def unit(dev, way):
+        return pl.ds(pl.multiple_of(dev * TOK + way * IN_BLK, PIECE), IN_BLK)
+
+    def origin(way, step):
+        return at_pos(pos + 8 - step + way * 2 * step, core)
+
+    def dn_hop(way, step, src=None):
+        spot = dn_all.at[unit(origin(way, step), way), :]
+        return pltpu.make_async_remote_copy(spot if src is None else src, spot, ns_sem.at[way, step], nr_sem.at[way, step + 1],
+                                            device_id={'fsdp': peers[way]}, device_id_type=MESH)
+
+    def dn_arrive(way, step):
+        spot = dn_all.at[unit(origin(way, step), way), :]
+        return pltpu.make_async_remote_copy(spot, spot, ns_sem.at[way, step], nr_sem.at[way, step],
+                                            device_id={'fsdp': peers[way]}, device_id_type=MESH)
+
+    def dn_share(way, step, src=None):
+        spot = dn_all.at[unit(origin(way, step), way), :]
+        return pltpu.make_async_remote_copy(spot if src is None else src, spot, np_sem.at[way, step], nq_sem.at[way, step],
+                                            device_id={'fsdp': partner}, device_id_type=MESH)
+    own_load = pltpu.make_async_copy(dn_h, own_dn, f_sem.at[0, 0])
+    own_load.start()
+    own_load.wait()
+    for way in range(2):
+        src = own_dn.at[way * IN_BLK:(way + 1) * IN_BLK, :]
+        dn_hop(way, 0, src).start()
+        dn_share(way, 0, src).start()
+        pltpu.make_async_copy(src, dn_all.at[unit(me, way), :], fo_sem.at[way]).start()
+
+    def row_grads(step):
+        jobs = [(at_pos(pos + 8 - step + way * 2 * step, c), way) for way in range(2) for c in (core, 1 - core)]
+
+        def fetch(slot):
+            dev, way = jobs[slot]
+            return [pltpu.make_async_copy(src.at[unit(dev, way), :], dst.at[slot], f_sem.at[i, slot])
+                    for i, (src, dst) in enumerate(((dn_all, fdn), (dy_h, fdy), (h_h, fh)))]
+
+        def put(slot):
+            dev, way = jobs[slot]
+            return pltpu.make_async_copy(fo.at[slot % 2], grad_h.at[unit(dev, way), :], fo_sem.at[slot % 2])
+        for way in range(2):
+            dn_share(way, step).wait_recv()
+        for slot in range(4):
+            for cp in fetch(slot):
+                cp.start()
+
+        for slot in range(4):
+            for cp in fetch(slot):
+                cp.wait()
+            if slot >= 2:
+                put(slot - 2).wait()
+
+            @pl.loop(0, IN_BLK // 48)
+            def _(g):
+                r0 = pl.multiple_of(g * 48, PIECE)
+
+                def tile(ref, p, c):
+                    return ref[slot, pl.ds(r0 + p, PIECE), c:c + 128].astype(F32)
+                scale = []
+                for p in range(0, 48, PIECE):
+                    sq = jnp.zeros((PIECE, 128), F32)
+                    al = jnp.zeros((PIECE, 128), F32)
+                    for c in range(0, 2048, 128):
+                        h = tile(fh, p, c)
+                        sq = sq + h * h
+                        al = al + h * (tile(fdn, p, c) * gain[:, c:c + 128])
+                    scale.append((jnp.sum(sq, axis=1, keepdims=True), jnp.sum(al, axis=1, keepdims=True)))
+                for p, (sq, al) in zip(range(0, 48, PIECE), scale):
+                    inv = lax.rsqrt(sq * (1.0 / 2048) + RMS_EPS)
+                    coef = inv * inv * inv * (al * (1.0 / 2048))
+                    for c in range(0, 2048, 128):
+                        s = tile(fdn, p, c) * gain[:, c:c + 128]
+                        fo[slot % 2, pl.ds(r0 + p, PIECE), c:c + 128] = tile(fdy, p, c) + inv * s - coef * tile(fh, p, c)
+            put(slot).start()
+        put(2).wait()
+        put(3).wait()
+
     own_small = pltpu.make_async_copy(sm_h.at[me], smr.at[0], loc_sem.at[5])
     own_small.start()
     own_mix = pltpu.make_async_copy(mix_h.at[:, pl.ds(pl.multiple_of(me * 128, 128), 128)], mix.at[me], loc_sem.at[6])
@@ -125,7 +206,6 @@
         return pltpu.make_async_copy(wl_h, wo.at[1], y_sem.at[1])
     wo_load(0).start()
     bufs = (b0, b1, b2, b3, b4, b5)
-    peers = (at_pos(pos + 1, core), at_pos(pos + 7, core))
     left_ops = {'n': (nrm, cat), 'u': (lat, du)}
 
     def mix_send(i):
@@ -159,8 +239,25 @@
         bufs[p][0] = jnp.zeros(bufs[p].shape[1:], F32)
     first_use = {0: (0, 1), 2: (2, 3, 4)}
 
+    for way in range(2):
+        pltpu.make_async_copy(own_dn.at[way * IN_BLK:(way + 1) * IN_BLK, :], dn_all.at[unit(me, way), :], fo_sem.at[way]).wait()
+
     @pl.loop(0, RING)
     def _(step):
+        @pl.when(step > 0)
+        def _():
+            for way in range(2):
+                dn_arrive(way, step).wait_recv()
+
+                @pl.when(step < RING - 1)
+                def _():
+                    dn_hop(way, step).start()
+                dn_share(way, step).start()
+
+            @pl.loop(step - 1, step + step // (RING - 1))
+            def _(done):
+                row_grads(done)
+
         for p in range(N_PARTS):
             if p in first_use:
                 @pl.when(step == 0)
@@ -250,26 +347,36 @@
         @pl.loop(0, last)
         def _(step):
             hop(p, step).wait_send()
+
+    @pl.loop(0, RING)
+    def _(step):
+        for way in range(2):
+            dn_share(way, step).wait_send()
+
+            @pl.when(step < last)
+            def _():
+                dn_hop(way, step).wait_send()
     for cp in outs:
         cp.wait()
 
 
-def grad_shards(mix, dy_all, nrm_t, dd, dq, lat_t, du, small, rows, weights, last_cols):
+def grad_shards(mix, dy_all, nrm_t, dd, dq, lat_t, du, small, rows, weights, last_cols, dn, picked, gain):
     shapes = [(ROWS[k], RING, w) for k, _, _, w in PARTS]
     scratch = [pltpu.VMEM((GROUP, TOK, 128), BF16), pltpu.VMEM((2, TOK, 2048), BF16), pltpu.VMEM((128, 2048), F32), pltpu.VMEM((2, 2048, TOK), BF16),
                pltpu.VMEM((2, TOK, D_CAT), BF16), pltpu.VMEM((2, 512, TOK), BF16), pltpu.VMEM((2, TOK, D_UP), BF16)]
     scratch += [pltpu.VMEM((RING, r, w), F32) for r, _, w in shapes]
     scratch += [pltpu.VMEM((TOK, 2048), BF16), pltpu.VMEM((TOK, 2048), BF16), pltpu.VMEM((2, 2048, 512), BF16), pltpu.VMEM((TOK, 2048), BF16)]
+    scratch += [pltpu.VMEM((TOK, 2048), BF16)] + [pltpu.VMEM((4, IN_BLK, 2048), BF16)] * 3 + [pltpu.VMEM((2, IN_BLK, 2048), F32)]
     scratch += [pltpu.VMEM((GROUP, 8, 128), F32), pltpu.VMEM((8, 128), F32)]
     dma = pltpu.SemaphoreType.DMA
-    scratch += [dma((7,)), dma((5,)), dma((5,)), dma((N_PARTS, RING)), dma((N_PARTS, RING)), dma((GROUP,)), dma((GROUP,)), dma((GROUP,)), dma((GROUP,)), dma((2,)), dma((4,)), dma((10,))]
+    scratch += [dma((7,)), dma((5,)), dma((5,)), dma((N_PARTS, RING)), dma((N_PARTS, RING)), dma((GROUP,)), dma((GROUP,)), dma((GROUP,)), dma((GROUP,)), dma((2,)), dma((4,)), dma((2, RING)), dma((2, RING)), dma((2, RING)), dma((2, RING)), dma((3, 4)), dma((2,)), dma((10,))]
     return pl.pallas_call(
         grad_kernel,
-        out_shape=(jax.ShapeDtypeStruct((TOK, 2048), BF16), jax.ShapeDtypeStruct((128, 2048), F32), jax.ShapeDtypeStruct((128, 3072), F32), jax.ShapeDtypeStruct((128, D_DOWN), F32), jax.ShapeDtypeStruct((32, D_UP), F32), jax.ShapeDtypeStruct((8, 128), F32)),
-        in_specs=[ANY] * 11, out_specs=(ANY,) * 6, scratch_shapes=scratch,
-        compiler_params=pltpu.CompilerParams(collective_id=1, has_side_effects=True, vmem_limit_bytes=60 * 1024 * 1024),
+        out_shape=(jax.ShapeDtypeStruct((TOK, 2048), BF16), jax.ShapeDtypeStruct((GROUP * TOK, 2048), BF16), jax.ShapeDtypeStruct((GROUP * TOK, 2048), F32), jax.ShapeDtypeStruct((128, 2048), F32), jax.ShapeDtypeStruct((128, 3072), F32), jax.ShapeDtypeStruct((128, D_DOWN), F32), jax.ShapeDtypeStruct((32, D_UP), F32), jax.ShapeDtypeStruct((8, 128), F32)),
+        in_specs=[ANY] * 13 + [pl.BlockSpec(memory_space=pltpu.VMEM)], out_specs=(ANY,) * 8, scratch_shapes=scratch,
+        compiler_params=pltpu.CompilerParams(collective_id=1, has_side_effects=True, vmem_limit_bytes=63 * 1024 * 1024),
         cost_estimate=pl.CostEstimate(flops=8 * 10**9, bytes_accessed=20 * 10**6, transcendentals=0), name='grad_shards',
-    )(mix, dy_all, nrm_t, dd, dq, lat_t, du, small, rows, weights, last_cols)
+    )(mix, dy_all, nrm_t, dd, dq, lat_t, du, small, rows, weights, last_cols, dn, picked, gain)
 
 
 W_SHARDS = ((32, 4096), (128, 576), (128, 512))
@@ -457,72 +564,40 @@
         cost_estimate=pl.CostEstimate(flops=8 * 10**9, bytes_accessed=27 * 10**6, transcendentals=0), name='spread',
     )(mask, rows, *shards)
 ROW_BLK = 128
-IN_BLK = 144
-SUB = 48
-PIECE = 16
+SUB = 144
 UNROLL = 4
-IN_SLOTS = 4
 OUT_SLOTS = 4
 
 
-def table_kernel(starts, toks, rows, flags, gain, small, dy_h, dn_h, h_h, *refs):
+def table_kernel(starts, toks, rows, flags, small, grad_h, *refs):
     passed, out_h, given, gain_out, kv_out = refs[0:5], refs[5], refs[6:11], refs[11], refs[12]
-    grad, dy, dn, hh, acc, ob, nil, in_sem, out_sem = refs[13:22]
-    hold, cut, ride_in, ride_out = refs[22:27], refs[27], refs[28], refs[29]
+    grad, acc, ob, nil, in_sem, out_sem = refs[13:19]
+    hold, cut, ride_in, ride_out = refs[19:24], refs[24], refs[25], refs[26]
     boards = [pltpu.make_async_copy(src, dst, ride_in.at[i]) for i, (src, dst) in enumerate(zip(passed, hold))]
     leaves = [pltpu.make_async_copy(cut if i == 2 else src, dst, ride_out.at[i]) for i, (src, dst) in enumerate(zip(hold, given))]
     for cp in boards:
         cp.start()
     gain_out[...] = small[0:1, :]
     kv_out[...] = small[1:2, 0:32]
-    n_in = GROUP * TOK // IN_BLK
+    n_in = GROUP * TOK // SUB
     n_out = out_h.shape[0] // ROW_BLK
 
-    def loads(blk):
-        span = pl.ds(pl.multiple_of(blk * IN_BLK, IN_BLK), IN_BLK)
-        slot = blk % IN_SLOTS
-        return [pltpu.make_async_copy(src.at[span, :], dst.at[slot], in_sem.at[i, slot]) for i, (src, dst) in enumerate(((dy_h, dy), (dn_h, dn), (h_h, hh)))]
-    for blk in range(IN_SLOTS - 1):
-        for cp in loads(blk):
-            cp.start()
+    def load(blk):
+        span = pl.ds(pl.multiple_of(blk * SUB, SUB), SUB)
+        return pltpu.make_async_copy(grad_h.at[span, :], grad.at[span, :], in_sem)
 
     @pl.loop(0, n_in)
     def _(blk):
-        slot = blk % IN_SLOTS
-        for cp in loads(blk):
-            cp.wait()
-
-        @pl.when(blk < n_in - IN_SLOTS + 1)
-        def _():
-            for cp in loads(blk + IN_SLOTS - 1):
-                cp.start()
-
-        @pl.loop(0, IN_BLK // SUB)
-        def _(g):
-            @pl.when(flags[blk * (IN_BLK // SUB) + g] > 0)
-            def _():
-                r0 = pl.multiple_of(g * SUB, PIECE)
-                o0 = pl.multiple_of(blk * IN_BLK + g * SUB, PIECE)
-                pieces = range(0, SUB, PIECE)
-
-                def tile(ref, p, c):
-                    return ref[slot, pl.ds(r0 + p, PIECE), c:c + 128].astype(F32)
-                scale = []
-                for p in pieces:
-                    sq = jnp.zeros((PIECE, 128), F32)
-                    al = jnp.zeros((PIECE, 128), F32)
-                    for c in range(0, 2048, 128):
-                        h = tile(hh, p, c)
-                        sq = sq + h * h
-                        al = al + h * (tile(dn, p, c) * gain[:, c:c + 128])
-                    scale.append((jnp.sum(sq, axis=1, keepdims=True), jnp.sum(al, axis=1, keepdims=True)))
-                for p, (sq, al) in zip(pieces, scale):
-                    inv = lax.rsqrt(sq * (1.0 / 2048) + RMS_EPS)
-                    coef = inv * inv * inv * (al * (1.0 / 2048))
-                    for c in range(0, 2048, 128):
-                        s = tile(dn, p, c) * gain[:, c:c + 128]
-                        grad[pl.ds(o0 + p, PIECE), c:c + 128] = tile(dy, p, c) + inv * s - coef * tile(hh, p, c)
-
+        @pl.when(flags[blk] > 0)
+        def _():
+            load(blk).start()
+    nil[...] = jnp.zeros_like(nil)
+
+    @pl.loop(0, n_in)
+    def _(blk):
+        @pl.when(flags[blk] > 0)
+        def _():
+            load(blk).wait()
     for cp in boards:
         cp.wait()
     cut[...] = hold[2][...].T[0:576, :]
@@ -531,8 +606,6 @@
 
     def store(blk, src):
         return pltpu.make_async_copy(src, out_h.at[pl.ds(pl.multiple_of(blk * ROW_BLK, ROW_BLK), ROW_BLK), :], out_sem.at[blk % OUT_SLOTS])
-    nil[...] = jnp.zeros_like(nil)
-
     @pl.loop(0, n_out)
     def _(blk):
         first, last = starts[blk], starts[blk + 1]
@@ -570,7 +643,7 @@
         cp.wait()
 
 
-def table_grad(starts, toks, rows, flags, gain, small, dy_all, dn_all, picked, vocab_dev, passed):
+def table_grad(starts, toks, rows, flags, small, row_grads, vocab_dev, passed):
     smem = pl.BlockSpec(memory_space=pltpu.SMEM)
     vmem = pl.BlockSpec(memory_space=pltpu.VMEM)
     dma = pltpu.SemaphoreType.DMA
@@ -578,13 +651,13 @@
     shapes += [jax.ShapeDtypeStruct((1, 128), F32), jax.ShapeDtypeStruct((1, 32), F32)]
     return pl.pallas_call(
         table_kernel, out_shape=tuple(shapes),
-        in_specs=[smem] * 4 + [vmem] * 2 + [ANY] * 8, out_specs=(ANY,) * 6 + (vmem,) * 2,
-        scratch_shapes=[pltpu.VMEM((GROUP * TOK, 2048), F32)] + [pltpu.VMEM((IN_SLOTS, IN_BLK, 2048), BF16)] * 3
-        + [pltpu.VMEM((ROW_BLK, 2048), F32), pltpu.VMEM((OUT_SLOTS, ROW_BLK, 2048), BF16), pltpu.VMEM((ROW_BLK, 2048), BF16), dma((3, IN_SLOTS)), dma((OUT_SLOTS,))]
+        in_specs=[smem] * 4 + [vmem] + [ANY] * 6, out_specs=(ANY,) * 6 + (vmem,) * 2,
+        scratch_shapes=[pltpu.VMEM((GROUP * TOK, 2048), F32)]
+        + [pltpu.VMEM((ROW_BLK, 2048), F32), pltpu.VMEM((OUT_SLOTS, ROW_BLK, 2048), BF16), pltpu.VMEM((ROW_BLK, 2048), BF16), dma, dma((OUT_SLOTS,))]
         + [pltpu.VMEM(p.shape, p.dtype) for p in passed] + [pltpu.VMEM((576, 128), F32), dma((5,)), dma((5,))],
         compiler_params=pltpu.CompilerParams(vmem_limit_bytes=63 * 1024 * 1024),
         cost_estimate=pl.CostEstimate(flops=10**9, bytes_accessed=90 * 10**6, transcendentals=0), name='table_grad',
-    )(starts, toks, rows, flags, gain, small, dy_all, dn_all, picked, *passed)
+    )(starts, toks, rows, flags, small, row_grads, *passed)
 
 
 def small_kernel(src, out, loc_sem, s_sem, r_sem):
@@ -685,11 +758,10 @@
         all_dy = lax.all_gather(grad_rows, 'fsdp', tiled=True)
         d_normed, normed, mix, latent, d_query, d_down, d_up, d_gain, d_kv_gain = block_step(
             tok_rows.astype(F32), grad_rows, (gain_full, full_wq, full_kva, kv_gain_full, full_kvb, full_wo), seq_count)
-        all_dn = lax.all_gather(d_normed, 'fsdp', tiled=True)
         small = jnp.concatenate([d_gain.reshape(GROUP, 1, 128), jnp.pad(d_kv_gain.reshape(GROUP, 1, 32), ((0, 0), (0, 0), (0, 96))), jnp.zeros((GROUP, 6, 128), F32)], axis=1)
-        block_out, g_out, g_query, g_down, g_up, g_small = grad_shards(mix, all_dy, normed.T, jnp.pad(d_down, ((0, 0), (0, D_DOWN - d_down.shape[1]))), d_query, latent.T, d_up, small, tok_rows, bundle, wo_last)
+        block_out, _, row_grads, g_out, g_query, g_down, g_up, g_small = grad_shards(mix, all_dy, normed.T, jnp.pad(d_down, ((0, 0), (0, D_DOWN - d_down.shape[1]))), d_query, latent.T, d_up, small, tok_rows, bundle, wo_last, d_normed, picked, gain_full.reshape(1, -1))
         grad_table, block_out, g_query, g_down, g_up, g_out, g_gain, g_kv_gain = table_grad(
-            starts, (keys >> 7) & 8191, keys & (ROW_BLK - 1), flags, gain_full.reshape(1, -1), g_small, all_dy, all_dn, picked, vocab_dev,
+            starts, (keys >> 7) & 8191, keys & (ROW_BLK - 1), flags, g_small, row_grads, vocab_dev,
             (block_out, g_query, g_down, g_up, g_out))
         return (block_out.reshape(seq_count, seq_len, d_model), grad_table, g_gain.reshape(-1), g_query, g_down.T, g_kv_gain.reshape(-1), g_up, g_out)
 

time: 690 us -> 684 us (level)
  Pallas kernels: 500 us -> 493 us
    pallas_call x1, Pallas kernels: 49.5 us -> 37.9 us  [table_grad(): pl.pallas_call(table_kernel, out_shape=tuple(shapes), in_specs=[smem] * 4...]
  transfers between devices with their start and end apart: 3 -> 2, of which waited for: 1 -> 1; matrix products, arithmetic and copies ran while one was open for 23% -> 23% of each run, Pallas kernels for 66% -> 22%
where the time goes in v6:
time: 684 us; the launch traced here: 674 us
  Pallas kernels  493 us (72%)
  local copies, waits for them, and re-layouts  88.7 us (13%)
  matrix products  47.6 us (7%)
  other arithmetic  27.4 us (4%)
  between operations  15.4 us (2%)
    pallas_call x1, Pallas kernels, grad_shards(): pl.pallas_call(grad_kernel, out_shape=(jax.ShapeDtypeStruct((TOK, 2048),...  304 us
    pallas_call x1, Pallas kernels, spread(): pl.pallas_call(lambda *refs: spread_kernel(n_w, *refs), out_shape=(jax.Sh...  141 us
    gather x1, local copies, waits for them, and re-layouts, device_step(): jnp.take(emb_table, jnp.where(mine, local, 0).reshape(-1), axis=0, mode='...  46.9 us
    pallas_call x1, Pallas kernels, table_grad(): pl.pallas_call(table_kernel, out_shape=tuple(shapes), in_specs=[smem] * 4...  37.9 us
  transfers between devices with their start and end apart: 2, of which 1 were waited for; matrix products, arithmetic and copies ran while one was open for 23% of the time, Pallas kernels for 22%

profile of v6, /device:TPU:0, one launch (start us, length us, event | category | flops | bytes accessed | tf_op | source)
XLA Modules:
  0.0 674.4 jit_solution(7805909785939410172)
XLA Ops:
  8.3 2.2 pad_maximum_fusion
  11.4 10.2 %small_gather.1 = f32[16,8,128]{2,1,0:T(8,128)} custom-call(f32[8,128]{1,0:T(8,128)} %fusion.90.src), custom_call_target="tpu_custom_call" | custom-call | flops 10000000 | bytes 100000 | tf_op jit(solution)/shard_map/small_gather/pallas_call | solution.py:681
  24.6 1.6 slice.58.refs_4_
  26.4 46.9 %gather_fusion = bf16[4608,2048]{1,0:T(8,128)(2,1)} fusion(bf16[6400,2048]{1,0:T(8,128)(2,1)} %param.11, s32[5120]{0:T(1024)S(1)} %pad_clamp_fusion), kind=kCustom, calls=%fused_computation | custom fusion | bytes 37767168 | tf_op jit(solution)/shard_map/jit(_take)/gather | solution.py:749
  73.4 6.7 sort.14
  80.7 1.7 convert_reduce_fusion.starts
  83.4 1.6 broadcast_in_dim.69.refs_0_
  85.0 141.0 %spread.1 = (bf16[288,2048]{1,0:T(8,128)(2,1)}, bf16[512,4096]{1,0:T(8,128)(2,1)}, bf16[2048,576]{1,0:T(8,128)(2,1)}, bf16[2048,512]{1,0:T(8,128)(2,1)}) custom-call(bf16[2,8,288,128]{3,2,1,0:T(8,128)(2,1)} %broadcast_in_dim.69.refs_0_, bf16[16,288,2048]{2,1,0:T(8,128)(2,1)} %bitcast.117, bf16[32,4096]{1,0:T(8,128)(2,1)} %refs_2_.1, ...), custom_call_target="tpu_custom_call" | custom-call | flops 8000000000 | bytes 27000000 | tf_op jit(solution)/shard_map/spread/pallas_call | solution.py:557
  227.6 1.6 fusion.15
  229.2 1.4 slice_bitcast_fusion
  230.7 3.2 convolution_convert_fusion.7
  235.1 3.7 convolution_convert_fusion
  242.6 10.2 %fusion.6 = bf16[288,3072]{1,0:T(8,128)(2,1)} fusion(bf16[2048,4608]{1,0:T(8,128)(2,1)} %all-gather.3.cloned.1.call-done.wo_h, bf16[288,2048]{1,0:T(8,128)(2,1)S(1)} %copy-done, f32[2048]{0:T(1024)} %bitcast.133, f32[288]{0:T(512)} %copy-done.38), kind=kOutput, calls=%fused_computation.8 | convolution fusion | flops 3627122688 | bytes 15542272 | tf_op jit(solution)/shard_map/dot_general | solution.py:700
  252.8 5.2 reshape.399
  258.0 1.6 slice.86
  260.3 4.9 fusion.4
  271.2 1.3 fusion.24
  274.9 1.4 copy.132
  276.3 2.8 copy.160
  281.7 1.6 reshape.403
  283.3 1.4 convert_multiply_fusion.1
  289.4 2.9 copy.138
  292.3 4.8 reshape.404.dq_h
  297.2 5.4 fusion.62
  302.7 1.7 fusion.71
  305.3 7.7 %fusion = f32[288,2048]{1,0:T(8,128)S(1)} fusion(bf16[288,3072]{1,0:T(8,128)(2,1)} %reshape.404.dq_h, bf16[2048,4608]{1,0:T(8,128)(2,1)} %all-gather.3.cloned.1.call-done.wo_h), kind=kOutput, calls=%fused_computation.1 | convolution fusion | flops 3623878656 | bytes 16711680 | tf_op jit(solution)/shard_map/dot_general | solution.py:714
  315.5 1.5 copy.139.nrm_h
  317.7 2.0 fusion.41
  320.2 1.3 copy.196
  323.0 1.9 all-gather.5.cloned.1.call-done.dy_h
  324.9 304.3 %grad_shards.1 = (bf16[288,2048]{1,0:T(8,128)(2,1)}, bf16[4608,2048]{1,0:T(8,128)(2,1)}, f32[4608,2048]{1,0:T(8,128)}, f32[128,2048]{1,0:T(8,128)}, f32[128,3072...) custom-call(bf16[288,2048]{1,0:T(8,128)(2,1)} %bitcast.124, ...), custom_call_target="tpu_custom_call" | custom-call | flops 8000000000 | bytes 20000000 | tf_op jit(solution)/shard_map/grad_shards/pallas_call | solution.py:373
  629.2 37.9 %table_grad.1 = (bf16[6400,2048]{1,0:T(8,128)(2,1)}, bf16[288,2048]{1,0:T(8,128)(2,1)}, f32[128,3072]{1,0:T(8,128)}, f32[576,128]{1,0:T(8,128)}, f32[32,4096]{1,...) custom-call(s32[51]{0:T(128)} %convert_reduce_fusion.starts, s32[4608]{0:T(1024)} %get-tuple-element.90.toks, ...), custom_call_target="tpu_custom_call" | custom-call | flops 1000000000 | bytes 90000000 | tf_op jit(solution)/shard_map/table_grad/pallas_call | solution.py:652
  (185 shorter events, 35.3 us)
Async XLA Ops:
  7.2 3.4 copy-start.40
  7.2 3.5 copy-start.42
  7.2 3.5 copy-start.43
  7.2 235.4 %all-gather.3.cloned.1.call-start = ((), (), s32[]{:S(2)}) async-start(), calls=%async_computation | async-start | bytes 20054016 | tf_op jit(solution)/shard_map/all_gather | solution.py:734
  10.5 314.4 %all-gather.5.cloned.1.call-start = ((), (), s32[]{:S(2)}) async-start(), calls=%async_computation.1 | async-start | bytes 20054016 | tf_op jit(solution)/shard_map/all_gather | solution.py:758
  26.4 56.1 %copy-start.27 = (bf16[128,576]{0,1:T(8,128)(2,1)S(1)}, bf16[128,576]{0,1:T(8,128)(2,1)}, u32[]{:S(2)}) copy-start(bf16[128,576]{0,1:T(8,128)(2,1)} %param.14) | copy-start | bytes 442372
  226.0 4.7 copy-start
  226.2 15.3 %copy-start.14 = (f32[96,64]{0,1:T(8,128)}, f32[96,64]{0,1:T(8,128)S(1)}, u32[]{:S(2)}) copy-start(f32[96,64]{0,1:T(8,128)S(1)} %get-tuple-element.92) | copy-start | bytes 73732
  226.2 15.3 %copy-start.16 = (f32[96,64]{0,1:T(8,128)}, f32[96,64]{0,1:T(8,128)S(1)}, u32[]{:S(2)}) copy-start(f32[96,64]{0,1:T(8,128)S(1)} %get-tuple-element.91) | copy-start | bytes 73732
  230.6 3.2 copy-start.29
  233.9 5.0 copy-start.7
  235.0 62.2 %copy-start.33 = (f32[512]{0:T(512)}, f32[512]{0:T(512)S(1)}, u32[]{:S(2)}) copy-start(f32[512]{0:T(512)S(1)} %mul.256) | copy-start | bytes 6148
  235.1 3.7 copy-start.36
  235.1 3.7 copy-start.34
  242.5 28.7 %copy-start.11 = (bf16[3,96,16,128]{3,2,1,0:T(8,128)(2,1)}, bf16[3,96,16,128]{3,2,1,0:T(8,128)(2,1)S(1)}, u32[]{:S(2)}) copy-start(bf16[3,96,16,128]{3,2,1,0:T(8,128)(2,1)S(1)} %get-tuple-element.74) | copy-start | bytes 3538948
  257.9 2.0 copy-start.1
  257.9 2.3 copy-start.9
  260.3 5.0 copy-start.5
  270.7 2.6 copy-start.2
  270.7 8.4 %copy-start.24 = (f32[3,16,96]{2,1,0:T(8,128)}, f32[3,16,96]{2,1,0:T(8,128)S(1)}, u32[]{:S(2)}) copy-start(f32[3,16,96]{2,1,0:T(8,128)S(1)} %get-tuple-element.65) | copy-start | bytes 55300
  271.2 7.9 %copy-start.22 = (f32[3,16,96]{2,1,0:T(8,128)}, f32[3,16,96]{2,1,0:T(8,128)S(1)}, u32[]{:S(2)}) copy-start(f32[3,16,96]{2,1,0:T(8,128)S(1)} %fusion.38) | copy-start | bytes 55300
  272.5 6.5 copy-start.12
  276.3 2.8 copy-start.28
  285.6 2.0 copy-start.13
  285.6 2.0 copy-start.23
  292.3 4.8 copy-start.8
  292.3 4.8 copy-start.35
  297.2 5.5 copy-start.37
  297.2 7.2 %copy-start.26 = (bf16[288,64]{0,1:T(8,128)(2,1)S(1)}, bf16[288,64]{0,1:T(8,128)(2,1)}, u32[]{:S(2)}) copy-start(bf16[288,64]{0,1:T(8,128)(2,1)} %reshape.403) | copy-start | bytes 110596
  305.3 7.8 %copy-start.44 = (bf16[2048,576]{1,0:T(8,128)(2,1)S(1)}, bf16[2048,576]{1,0:T(8,128)(2,1)}, u32[]{:S(2)}) copy-start(bf16[2048,576]{1,0:T(8,128)(2,1)} %get-tuple-element.44) | copy-start | bytes 7077892
  315.5 2.2 copy-start.4
  319.8 2.6 copy-start.41
  (15 other events, 19.0 us)
Sparse Core Ops, SparseCore 0:
  10.6 121.6 all-gather.2
  226.1 98.7 all-gather.4

commit v7 on v6

--- a/solution.py
+++ b/solution.py
@@ -84,6 +84,7 @@
 PIECE = 16
 D_OUT, D_CAT, D_UP, D_DOWN = 2048, 3712, 4096, 640
 WO_COL = 3072
+WO_CUT = 1152
 CUT = 1792
 PARTS = (('u', 0, 0, 2304), ('u', 1, 2304, 1792), ('n', 0, 0, 896), ('n', 1, 1792, 1024), ('n', 0, 896, 896), ('n', 1, 2816, 896))
 N_PARTS = len(PARTS)
@@ -94,7 +95,7 @@
     return [(c, min(step, width - c)) for c in range(0, width, step)]
 
 def grad_kernel(mix_h, dy_h, nrm_h, dd_h, dq_h, lat_h, du_h, sm_h, h0_h, wo_h, wl_h, dn_h, h_h, gain, y_h, dn_all, grad_h, go_h, gq_h, gd_h, gu_h, gs_h,
-                mix, dy, go, nrm, cat, lat, du, b0, b1, b2, b3, b4, b5, mixf, h0, wo, yv, own_dn, fdn, fdy, fh, fo, smr, ssum, loc_sem, xs_sem, xr_sem, s_sem, r_sem, ms_sem, mr_sem, cs_sem, cr_sem, dy_sem, y_sem, ns_sem, nr_sem, np_sem, nq_sem, f_sem, fo_sem, out_sem):
+                mix, dy, go, nrm, cat, lat, du, b0, b1, b2, b3, b4, b5, mixf, h0, wo, yacc, yv, own_dn, fdn, fdy, fh, fo, smr, ssum, loc_sem, xs_sem, xr_sem, s_sem, r_sem, ms_sem, mr_sem, cs_sem, cr_sem, dy_sem, y_sem, ns_sem, nr_sem, np_sem, nq_sem, f_sem, fo_sem, out_sem):
     me, core, pos = place()
     partner = me + 1 - 2 * core
     meet_all(me)
@@ -197,14 +198,14 @@
         rc.start()
         smalls.append(rc)
     for i, (src, dst) in enumerate(((mix_h, mixf), (h0_h, h0))):
-        pltpu.make_async_copy(src, dst, y_sem.at[2 + i]).start()
+        pltpu.make_async_copy(src, dst, y_sem.at[2, i]).start()
 
     def wo_load(t):
-        return pltpu.make_async_copy(wo_h.at[:, pl.ds(pl.multiple_of(WO_COL + t * 512, 512), 512)], wo.at[t % 2], y_sem.at[t % 2])
-
-    def wo_last():
-        return pltpu.make_async_copy(wl_h, wo.at[1], y_sem.at[1])
-    wo_load(0).start()
+        span = pl.ds(pl.multiple_of(t * 256, 256), 256)
+        return [pltpu.make_async_copy(src, dst, y_sem.at[i, t % 2]) for i, (src, dst) in enumerate((
+            (wo_h.at[span, WO_COL:WO_COL + WO_CUT], wo.at[t % 2, :, 0:WO_CUT]), (wl_h.at[span, :], wo.at[t % 2, :, WO_CUT:2048])))]
+    for cp in wo_load(0):
+        cp.start()
     bufs = (b0, b1, b2, b3, b4, b5)
     left_ops = {'n': (nrm, cat), 'u': (lat, du)}
 
@@ -297,27 +298,25 @@
         @pl.when(step == 5)
         def _():
             for i, (src, dst) in enumerate(((mix_h, mixf), (h0_h, h0))):
-                pltpu.make_async_copy(src, dst, y_sem.at[2 + i]).wait()
-
-            @pl.loop(0, 4)
+                pltpu.make_async_copy(src, dst, y_sem.at[2, i]).wait()
+
+            yacc[...] = h0[...].astype(F32)
+
+            @pl.loop(0, 8)
             def _(t):
-                @pl.when(t < 3)
+                for cp in wo_load(t):
+                    cp.wait()
+
+                @pl.when(t < 7)
                 def _():
-                    wo_load(t).wait()
-
-                @pl.when(t == 3)
-                def _():
-                    wo_last().wait()
-
-                @pl.when(t < 2)
-                def _():
-                    wo_load(t + 1).start()
-
-                @pl.when(t == 2)
-                def _():
-                    wo_last().start()
-                here = pl.ds(pl.multiple_of(t * 512, 512), 512)
-                yv[:, here] = (h0[:, here].astype(F32) + jnp.dot(mixf[...], wo[t % 2], preferred_element_type=F32)).astype(BF16)
+                    for cp in wo_load(t + 1):
+                        cp.start()
+
+                @pl.loop(0, 4)
+                def _(j):
+                    here = pl.ds(pl.multiple_of(j * 512, 512), 512)
+                    yacc[:, here] += jnp.dot(mixf[:, pl.ds(pl.multiple_of(t * 256, 256), 256)], wo[t % 2, :, here], preferred_element_type=F32)
+            yv[...] = yacc[...].astype(BF16)
 
     last = RING - 1
     outs = []
@@ -365,11 +364,11 @@
     scratch = [pltpu.VMEM((GROUP, TOK, 128), BF16), pltpu.VMEM((2, TOK, 2048), BF16), pltpu.VMEM((128, 2048), F32), pltpu.VMEM((2, 2048, TOK), BF16),
                pltpu.VMEM((2, TOK, D_CAT), BF16), pltpu.VMEM((2, 512, TOK), BF16), pltpu.VMEM((2, TOK, D_UP), BF16)]
     scratch += [pltpu.VMEM((RING, r, w), F32) for r, _, w in shapes]
-    scratch += [pltpu.VMEM((TOK, 2048), BF16), pltpu.VMEM((TOK, 2048), BF16), pltpu.VMEM((2, 2048, 512), BF16), pltpu.VMEM((TOK, 2048), BF16)]
+    scratch += [pltpu.VMEM((TOK, 2048), BF16), pltpu.VMEM((TOK, 2048), BF16), pltpu.VMEM((2, 256, 2048), BF16), pltpu.VMEM((TOK, 2048), F32), pltpu.VMEM((TOK, 2048), BF16)]
     scratch += [pltpu.VMEM((TOK, 2048), BF16)] + [pltpu.VMEM((4, IN_BLK, 2048), BF16)] * 3 + [pltpu.VMEM((2, IN_BLK, 2048), F32)]
     scratch += [pltpu.VMEM((GROUP, 8, 128), F32), pltpu.VMEM((8, 128), F32)]
     dma = pltpu.SemaphoreType.DMA
-    scratch += [dma((7,)), dma((5,)), dma((5,)), dma((N_PARTS, RING)), dma((N_PARTS, RING)), dma((GROUP,)), dma((GROUP,)), dma((GROUP,)), dma((GROUP,)), dma((2,)), dma((4,)), dma((2, RING)), dma((2, RING)), dma((2, RING)), dma((2, RING)), dma((3, 4)), dma((2,)), dma((10,))]
+    scratch += [dma((7,)), dma((5,)), dma((5,)), dma((N_PARTS, RING)), dma((N_PARTS, RING)), dma((GROUP,)), dma((GROUP,)), dma((GROUP,)), dma((GROUP,)), dma((2,)), dma((3, 2)), dma((2, RING)), dma((2, RING)), dma((2, RING)), dma((2, RING)), dma((3, 4)), dma((2,)), dma((10,))]
     return pl.pallas_call(
         grad_kernel,
         out_shape=(jax.ShapeDtypeStruct((TOK, 2048), BF16), jax.ShapeDtypeStruct((GROUP * TOK, 2048), BF16), jax.ShapeDtypeStruct((GROUP * TOK, 2048), F32), jax.ShapeDtypeStruct((128, 2048), F32), jax.ShapeDtypeStruct((128, 3072), F32), jax.ShapeDtypeStruct((128, D_DOWN), F32), jax.ShapeDtypeStruct((32, D_UP), F32), jax.ShapeDtypeStruct((8, 128), F32)),
@@ -379,7 +378,7 @@
     )(mix, dy_all, nrm_t, dd, dq, lat_t, du, small, rows, weights, last_cols, dn, picked, gain)
 
 
-W_SHARDS = ((32, 4096), (128, 576), (128, 512))
+W_SHARDS = ((32, 4096), (128, 576), (128, 896))
 HALF_TOK = TOK // 2
 
 
@@ -563,7 +562,7 @@
         compiler_params=pltpu.CompilerParams(collective_id=2, has_side_effects=True, vmem_limit_bytes=60 * 1024 * 1024),
         cost_estimate=pl.CostEstimate(flops=8 * 10**9, bytes_accessed=27 * 10**6, transcendentals=0), name='spread',
     )(mask, rows, *shards)
-ROW_BLK = 128
+ROW_BLK = 256
 SUB = 144
 UNROLL = 4
 OUT_SLOTS = 4
@@ -592,6 +591,7 @@
         def _():
             load(blk).start()
     nil[...] = jnp.zeros_like(nil)
+    acc[...] = jnp.zeros_like(acc)
 
     @pl.loop(0, n_in)
     def _(blk):
@@ -621,8 +621,6 @@
 
         @pl.when(first < last)
         def _():
-            acc[...] = jnp.zeros_like(acc)
-
             def add(k):
                 acc[pl.ds(rows[k], 1), :] += grad[pl.ds(toks[k], 1), :]
             quads = (last - first) // UNROLL
@@ -635,7 +633,11 @@
             @pl.loop(first + quads * UNROLL, last)
             def _(k):
                 add(k)
-            ob[slot] = acc[...].astype(BF16)
+            @pl.loop(0, ROW_BLK // 32)
+            def _(r):
+                here = pl.ds(pl.multiple_of(r * 32, 32), 32)
+                ob[slot, here, :] = acc[here, :].astype(BF16)
+                acc[here, :] = jnp.zeros((32, 2048), F32)
             store(blk, ob.at[slot]).start()
     for blk in range(n_out - OUT_SLOTS, n_out):
         store(blk, nil).wait()
@@ -703,8 +705,8 @@
     kv_up = jnp.dot(latent, w_kv_up, preferred_element_type=jnp.float32).astype(jnp.bfloat16)
     attn_mix, attn_pull = jax.vjp(attend_local, q_proj.reshape(seq_count, seq_len, -1, NOPE_DIM + ROPE_DIM), kv_down[:, kv_rank:].reshape(seq_count, seq_len, ROPE_DIM), kv_up.reshape(seq_count, seq_len, -1, NOPE_DIM + VALUE_DIM))
     mix_rows = attn_mix.reshape(tok_count, -1)
-    d_mix = lax.dot_general(grad_rows[:, :1536], w_out[0], COL_DIMS, preferred_element_type=jnp.float32)
-    d_mix = (d_mix + lax.dot_general(grad_rows[:, 1536:], w_out[1], COL_DIMS, preferred_element_type=jnp.float32)).astype(jnp.bfloat16)
+    d_mix = lax.dot_general(grad_rows[:, :WO_CUT], w_out[0], COL_DIMS, preferred_element_type=jnp.float32)
+    d_mix = (d_mix + lax.dot_general(grad_rows[:, WO_CUT:], w_out[1], COL_DIMS, preferred_element_type=jnp.float32)).astype(jnp.bfloat16)
     d_query, d_pe, d_up = attn_pull(d_mix.reshape(attn_mix.shape))
     d_query = d_query.reshape(tok_count, -1)
     d_up = d_up.reshape(tok_count, -1)
@@ -731,7 +733,7 @@
         tok_count = seq_count * seq_len
         me = lax.axis_index('fsdp')
         grad_rows = grad_out.reshape(tok_count, d_model)
-        bundle = lax.all_gather(jnp.concatenate([w_query, w_out[:, :1536]], axis=1), 'fsdp', tiled=True)
+        bundle = lax.all_gather(jnp.concatenate([w_query, w_out[:, :WO_CUT]], axis=1), 'fsdp', tiled=True)
         fill = lambda rows: jnp.pad(rows, ((0, 0), (0, 128 - rows.shape[1])))
         tile = jnp.concatenate([fill(tok_ids.astype(F32)), norm_gain.astype(F32).reshape(1, 128), fill(kv_gain.astype(F32).reshape(1, 32)), jnp.zeros((3, 128), F32)], axis=0)
         table = small_gather(tile)
@@ -743,7 +745,7 @@
         mine = (owner == me)
         local = all_ids - me * vocab_dev
         stamp = jnp.arange(GROUP * tok_count).reshape(GROUP, tok_count) * ROW_BLK
-        keys = lax.sort(jnp.where(mine, (local // ROW_BLK) * 2**20 + stamp + local % ROW_BLK, 2**30).reshape(-1))
+        keys = lax.sort(jnp.where(mine, (local // ROW_BLK) * (8192 * ROW_BLK) + stamp + local % ROW_BLK, 2**30).reshape(-1))
         starts = jnp.sum((mine & (local < ROW_BLK * jnp.arange(vocab_dev // ROW_BLK + 1)[:, None, None])).astype(jnp.int32), axis=(1, 2))
         flags = jnp.sum(mine.reshape(-1, SUB).astype(jnp.int32), axis=1)
         picked = jnp.take(emb_table, jnp.where(mine, local, 0).reshape(-1), axis=0, mode='clip')
@@ -752,7 +754,7 @@
         mask = jnp.stack([near == me, near == me + 1 - 2 * core]).astype(BF16)
         mask = jnp.broadcast_to(mask[..., None], (2, RING, tok_count, 128))
         picked, keys, starts, flags, w_kv_down = lax.optimization_barrier((picked, keys, starts, flags, w_kv_down))
-        tok_rows, full_kvb, full_kva, wo_last = spread(mask, picked.reshape(GROUP, tok_count, d_model), (w_kv_up, w_kv_down, w_out[:, 1536:]))
+        tok_rows, full_kvb, full_kva, wo_last = spread(mask, picked.reshape(GROUP, tok_count, d_model), (w_kv_up, w_kv_down, w_out[:, WO_CUT:]))
         full_wq, full_wo = bundle[:, :3072], (bundle[:, 3072:], wo_last)
         tok_rows, grad_rows = lax.optimization_barrier((tok_rows, grad_rows))
         all_dy = lax.all_gather(grad_rows, 'fsdp', tiled=True)
@@ -761,7 +763,7 @@
         small = jnp.concatenate([d_gain.reshape(GROUP, 1, 128), jnp.pad(d_kv_gain.reshape(GROUP, 1, 32), ((0, 0), (0, 0), (0, 96))), jnp.zeros((GROUP, 6, 128), F32)], axis=1)
         block_out, _, row_grads, g_out, g_query, g_down, g_up, g_small = grad_shards(mix, all_dy, normed.T, jnp.pad(d_down, ((0, 0), (0, D_DOWN - d_down.shape[1]))), d_query, latent.T, d_up, small, tok_rows, bundle, wo_last, d_normed, picked, gain_full.reshape(1, -1))
         grad_table, block_out, g_query, g_down, g_up, g_out, g_gain, g_kv_gain = table_grad(
-            starts, (keys >> 7) & 8191, keys & (ROW_BLK - 1), flags, g_small, row_grads, vocab_dev,
+            starts, (keys // ROW_BLK) & 8191, keys & (ROW_BLK - 1), flags, g_small, row_grads, vocab_dev,
             (block_out, g_query, g_down, g_up, g_out))
         return (block_out.reshape(seq_count, seq_len, d_model), grad_table, g_gain.reshape(-1), g_query, g_down.T, g_kv_gain.reshape(-1), g_up, g_out)
 

time: 684 us -> 680 us (level)
  no operation moved by 1% of the time
where the time goes in v7:
time: 680 us; the launch traced here: 670 us
  Pallas kernels  489 us (72%)
  local copies, waits for them, and re-layouts  88.5 us (13%)
  matrix products  47.4 us (7%)
  other arithmetic  26.8 us (4%)
  between operations  15.4 us (2%)
    pallas_call x1, Pallas kernels, grad_shards(): pl.pallas_call(grad_kernel, out_shape=(jax.ShapeDtypeStruct((TOK, 2048),...  304 us
    pallas_call x1, Pallas kernels, spread(): pl.pallas_call(lambda *refs: spread_kernel(n_w, *refs), out_shape=(jax.Sh...  138 us
    gather x1, local copies, waits for them, and re-layouts, device_step(): jnp.take(emb_table, jnp.where(mine, local, 0).reshape(-1), axis=0, mode='...  46.9 us
    pallas_call x1, Pallas kernels, table_grad(): pl.pallas_call(table_kernel, out_shape=tuple(shapes), in_specs=[smem] * 4...  36.9 us
  transfers between devices with their start and end apart: 2, of which 1 were waited for; matrix products, arithmetic and copies ran while one was open for 23% of the time, Pallas kernels for 22%

profile of v7, /device:TPU:0, one launch (start us, length us, event | category | flops | bytes accessed | tf_op | source)
XLA Modules:
  0.0 669.8 jit_solution(6019882683654113269)
XLA Ops:
  8.2 2.2 pad_maximum_fusion
  11.3 10.2 %small_gather.1 = f32[16,8,128]{2,1,0:T(8,128)} custom-call(f32[8,128]{1,0:T(8,128)} %fusion.93.src), custom_call_target="tpu_custom_call" | custom-call | flops 10000000 | bytes 100000 | tf_op jit(solution)/shard_map/small_gather/pallas_call | solution.py:683
  24.6 1.6 slice.58.refs_4_
  26.4 46.9 %gather_fusion = bf16[4608,2048]{1,0:T(8,128)(2,1)} fusion(bf16[6400,2048]{1,0:T(8,128)(2,1)} %param.11, s32[5120]{0:T(1024)S(1)} %pad_clamp_fusion), kind=kCustom, calls=%fused_computation | custom fusion | bytes 37767168 | tf_op jit(solution)/shard_map/jit(_take)/gather | solution.py:751
  73.4 6.7 sort.14
  82.9 1.6 broadcast_in_dim.69.refs_0_
  84.5 137.8 %spread.1 = (bf16[288,2048]{1,0:T(8,128)(2,1)}, bf16[512,4096]{1,0:T(8,128)(2,1)}, bf16[2048,576]{1,0:T(8,128)(2,1)}, bf16[2048,896]{1,0:T(8,128)(2,1)}) custom-call(bf16[2,8,288,128]{3,2,1,0:T(8,128)(2,1)} %broadcast_in_dim.69.refs_0_, bf16[16,288,2048]{2,1,0:T(8,128)(2,1)} %bitcast.117, bf16[32,4096]{1,0:T(8,128)(2,1)} %refs_2_.1, ...), custom_call_target="tpu_custom_call" | custom-call | flops 8000000000 | bytes 27000000 | tf_op jit(solution)/shard_map/spread/pallas_call | solution.py:556
  224.0 1.6 fusion.15
  225.6 1.4 slice_bitcast_fusion
  227.0 3.2 convolution_convert_fusion.7
  231.5 3.7 convolution_convert_fusion
  238.9 10.2 %fusion.6 = bf16[288,3072]{1,0:T(8,128)(2,1)} fusion(bf16[2048,4224]{1,0:T(8,128)(2,1)} %all-gather.3.cloned.1.call-done.wo_h, bf16[288,2048]{1,0:T(8,128)(2,1)S(1)} %copy-done, f32[2048]{0:T(1024)} %bitcast.133, f32[288]{0:T(512)} %copy-done.38), kind=kOutput, calls=%fused_computation.8 | convolution fusion | flops 3627122688 | bytes 15542272 | tf_op jit(solution)/shard_map/dot_general | solution.py:702
  249.1 5.1 reshape.399
  254.3 1.6 slice.86
  256.6 4.2 fusion.4
  260.8 1.4 fusion.43
  267.4 1.3 fusion.24
  271.0 1.4 copy.132
  272.4 2.7 copy.160
  277.8 1.6 reshape.403
  279.4 1.4 convert_multiply_fusion.1
  285.5 2.8 copy.138
  288.3 4.8 reshape.404.dq_h
  293.1 5.4 fusion.61
  298.6 1.7 fusion.71
  301.3 7.7 %fusion = f32[288,2048]{1,0:T(8,128)S(1)} fusion(bf16[288,3072]{1,0:T(8,128)(2,1)} %reshape.404.dq_h, bf16[2048,4224]{1,0:T(8,128)(2,1)} %all-gather.3.cloned.1.call-done.wo_h), kind=kOutput, calls=%fused_computation.1 | convolution fusion | flops 3623878656 | bytes 16711680 | tf_op jit(solution)/shard_map/dot_general | solution.py:716
  311.5 1.5 copy.139.nrm_h
  313.7 2.0 fusion.41
  316.2 1.3 copy.196
  319.0 2.3 all-gather.5.cloned.1.call-done.dy_h
  321.3 304.3 %grad_shards.1 = (bf16[288,2048]{1,0:T(8,128)(2,1)}, bf16[4608,2048]{1,0:T(8,128)(2,1)}, f32[4608,2048]{1,0:T(8,128)}, f32[128,2048]{1,0:T(8,128)}, f32[128,3072...) custom-call(bf16[288,2048]{1,0:T(8,128)(2,1)} %bitcast.124, ...), custom_call_target="tpu_custom_call" | custom-call | flops 8000000000 | bytes 20000000 | tf_op jit(solution)/shard_map/grad_shards/pallas_call | solution.py:372
  625.6 36.9 %table_grad.1 = (bf16[6400,2048]{1,0:T(8,128)(2,1)}, bf16[288,2048]{1,0:T(8,128)(2,1)}, f32[128,3072]{1,0:T(8,128)}, f32[576,128]{1,0:T(8,128)}, f32[32,4096]{1,...) custom-call(s32[26]{0:T(128)} %convert_reduce_fusion.starts, s32[4608]{0:T(1024)} %get-tuple-element.90.toks, ...), custom_call_target="tpu_custom_call" | custom-call | flops 1000000000 | bytes 90000000 | tf_op jit(solution)/shard_map/table_grad/pallas_call | solution.py:654
  (185 shorter events, 35.7 us)
Async XLA Ops:
  7.2 3.3 copy-start.40
  7.2 3.4 copy-start.42
  7.2 3.4 copy-start.43
  7.2 231.7 %all-gather.3.cloned.1.call-start = ((), (), s32[]{:S(2)}) async-start(), calls=%async_computation | async-start | bytes 18382848 | tf_op jit(solution)/shard_map/all_gather | solution.py:736
  10.4 310.9 %all-gather.5.cloned.1.call-start = ((), (), s32[]{:S(2)}) async-start(), calls=%async_computation.1 | async-start | bytes 20054016 | tf_op jit(solution)/shard_map/all_gather | solution.py:760
  26.4 55.6 %copy-start.27 = (bf16[128,576]{0,1:T(8,128)(2,1)S(1)}, bf16[128,576]{0,1:T(8,128)(2,1)}, u32[]{:S(2)}) copy-start(bf16[128,576]{0,1:T(8,128)(2,1)} %param.14) | copy-start | bytes 442372
  222.3 4.7 copy-start
  222.5 15.3 %copy-start.14 = (f32[96,64]{0,1:T(8,128)}, f32[96,64]{0,1:T(8,128)S(1)}, u32[]{:S(2)}) copy-start(f32[96,64]{0,1:T(8,128)S(1)} %get-tuple-element.92) | copy-start | bytes 73732
  222.5 15.3 %copy-start.16 = (f32[96,64]{0,1:T(8,128)}, f32[96,64]{0,1:T(8,128)S(1)}, u32[]{:S(2)}) copy-start(f32[96,64]{0,1:T(8,128)S(1)} %get-tuple-element.91) | copy-start | bytes 73732
  227.0 3.2 copy-start.29
  230.2 5.0 copy-start.7
  231.4 61.8 %copy-start.33 = (f32[512]{0:T(512)}, f32[512]{0:T(512)S(1)}, u32[]{:S(2)}) copy-start(f32[512]{0:T(512)S(1)} %mul.252) | copy-start | bytes 6148
  231.5 3.7 copy-start.36
  231.5 3.7 copy-start.34
  238.9 28.5 %copy-start.11 = (bf16[3,96,16,128]{3,2,1,0:T(8,128)(2,1)}, bf16[3,96,16,128]{3,2,1,0:T(8,128)(2,1)S(1)}, u32[]{:S(2)}) copy-start(bf16[3,96,16,128]{3,2,1,0:T(8,128)(2,1)S(1)} %get-tuple-element.74) | copy-start | bytes 3538948
  254.3 2.0 copy-start.1
  254.3 2.3 copy-start.10
  256.6 4.2 copy-start.6
  266.8 2.6 copy-start.2
  266.8 8.3 %copy-start.24 = (f32[3,16,96]{2,1,0:T(8,128)}, f32[3,16,96]{2,1,0:T(8,128)S(1)}, u32[]{:S(2)}) copy-start(f32[3,16,96]{2,1,0:T(8,128)S(1)} %get-tuple-element.65) | copy-start | bytes 55300
  267.3 7.8 %copy-start.22 = (f32[3,16,96]{2,1,0:T(8,128)}, f32[3,16,96]{2,1,0:T(8,128)S(1)}, u32[]{:S(2)}) copy-start(f32[3,16,96]{2,1,0:T(8,128)S(1)} %fusion.38) | copy-start | bytes 55300
  268.7 6.5 copy-start.12
  272.4 2.8 copy-start.28
  281.7 2.0 copy-start.13
  281.7 2.0 copy-start.23
  288.3 4.8 copy-start.8
  288.3 4.8 copy-start.35
  293.1 5.5 copy-start.37
  293.1 7.2 %copy-start.26 = (bf16[288,64]{0,1:T(8,128)(2,1)S(1)}, bf16[288,64]{0,1:T(8,128)(2,1)}, u32[]{:S(2)}) copy-start(bf16[288,64]{0,1:T(8,128)(2,1)} %reshape.403) | copy-start | bytes 110596
  301.3 7.8 %copy-start.44 = (bf16[2048,576]{1,0:T(8,128)(2,1)S(1)}, bf16[2048,576]{1,0:T(8,128)(2,1)}, u32[]{:S(2)}) copy-start(bf16[2048,576]{1,0:T(8,128)(2,1)} %get-tuple-element.44) | copy-start | bytes 7077892
  311.5 2.2 copy-start.4
  315.8 2.6 copy-start.41
  (15 other events, 19.0 us)
Sparse Core Ops, SparseCore 0:
  10.6 107.2 all-gather.2
  222.5 98.7 all-gather.4

commit v8 on v7

--- a/solution.py
+++ b/solution.py
@@ -562,90 +562,81 @@
         compiler_params=pltpu.CompilerParams(collective_id=2, has_side_effects=True, vmem_limit_bytes=60 * 1024 * 1024),
         cost_estimate=pl.CostEstimate(flops=8 * 10**9, bytes_accessed=27 * 10**6, transcendentals=0), name='spread',
     )(mask, rows, *shards)
-ROW_BLK = 256
-SUB = 144
+ROW_BLK = 64
+SUB = 72
 UNROLL = 4
-OUT_SLOTS = 4
-
-
-def table_kernel(starts, toks, rows, flags, small, grad_h, *refs):
+IN_SLOTS = 6
+OUT_SLOTS = 8
+
+
+def table_kernel(starts, toks, rows, small, grad_h, *refs):
     passed, out_h, given, gain_out, kv_out = refs[0:5], refs[5], refs[6:11], refs[11], refs[12]
-    grad, acc, ob, nil, in_sem, out_sem = refs[13:19]
-    hold, cut, ride_in, ride_out = refs[19:24], refs[24], refs[25], refs[26]
+    acc, grad, ob, in_sem, out_sem = refs[13:18]
+    hold, cut, ride_in, ride_out = refs[18:23], refs[23], refs[24], refs[25]
+    n_in = GROUP * TOK // SUB
+    n_out = out_h.shape[0] // ROW_BLK
+
+    def load(blk):
+        return pltpu.make_async_copy(grad_h.at[pl.ds(pl.multiple_of(blk * SUB, SUB), SUB), :], grad.at[blk % IN_SLOTS], in_sem.at[blk % IN_SLOTS])
+    for blk in range(IN_SLOTS):
+        load(blk).start()
     boards = [pltpu.make_async_copy(src, dst, ride_in.at[i]) for i, (src, dst) in enumerate(zip(passed, hold))]
     leaves = [pltpu.make_async_copy(cut if i == 2 else src, dst, ride_out.at[i]) for i, (src, dst) in enumerate(zip(hold, given))]
     for cp in boards:
         cp.start()
     gain_out[...] = small[0:1, :]
     kv_out[...] = small[1:2, 0:32]
-    n_in = GROUP * TOK // SUB
-    n_out = out_h.shape[0] // ROW_BLK
-
-    def load(blk):
-        span = pl.ds(pl.multiple_of(blk * SUB, SUB), SUB)
-        return pltpu.make_async_copy(grad_h.at[span, :], grad.at[span, :], in_sem)
+
+    @pl.loop(0, out_h.shape[0] // 64)
+    def _(i):
+        acc[pl.ds(pl.multiple_of(i * 64, 64), 64), :] = jnp.zeros((64, 2048), F32)
 
     @pl.loop(0, n_in)
     def _(blk):
-        @pl.when(flags[blk] > 0)
+        first, last = starts[blk], starts[blk + 1]
+        slot = blk % IN_SLOTS
+        load(blk).wait()
+
+        def add(k):
+            acc[pl.ds(rows[k], 1), :] += grad[slot, pl.ds(toks[k] - blk * SUB, 1), :]
+        quads = (last - first) // UNROLL
+
+        @pl.loop(0, quads)
+        def _(i):
+            for j in range(UNROLL):
+                add(first + i * UNROLL + j)
+
+        @pl.loop(first + quads * UNROLL, last)
+        def _(k):
+            add(k)
+
+        @pl.when(blk < n_in - IN_SLOTS)
         def _():
-            load(blk).start()
-    nil[...] = jnp.zeros_like(nil)
-    acc[...] = jnp.zeros_like(acc)
-
-    @pl.loop(0, n_in)
-    def _(blk):
-        @pl.when(flags[blk] > 0)
-        def _():
-            load(blk).wait()
+            load(blk + IN_SLOTS).start()
     for cp in boards:
         cp.wait()
     cut[...] = hold[2][...].T[0:576, :]
     for cp in leaves:
         cp.start()
 
-    def store(blk, src):
-        return pltpu.make_async_copy(src, out_h.at[pl.ds(pl.multiple_of(blk * ROW_BLK, ROW_BLK), ROW_BLK), :], out_sem.at[blk % OUT_SLOTS])
+    def store(blk):
+        slot = blk % OUT_SLOTS
+        return pltpu.make_async_copy(ob.at[slot], out_h.at[pl.ds(pl.multiple_of(blk * ROW_BLK, ROW_BLK), ROW_BLK), :], out_sem.at[slot])
+
     @pl.loop(0, n_out)
     def _(blk):
-        first, last = starts[blk], starts[blk + 1]
-        slot = blk % OUT_SLOTS
-
         @pl.when(blk >= OUT_SLOTS)
         def _():
-            store(blk - OUT_SLOTS, nil).wait()
-
-        @pl.when(first == last)
-        def _():
-            store(blk, nil).start()
-
-        @pl.when(first < last)
-        def _():
-            def add(k):
-                acc[pl.ds(rows[k], 1), :] += grad[pl.ds(toks[k], 1), :]
-            quads = (last - first) // UNROLL
-
-            @pl.loop(0, quads)
-            def _(i):
-                for j in range(UNROLL):
-                    add(first + i * UNROLL + j)
-
-            @pl.loop(first + quads * UNROLL, last)
-            def _(k):
-                add(k)
-            @pl.loop(0, ROW_BLK // 32)
-            def _(r):
-                here = pl.ds(pl.multiple_of(r * 32, 32), 32)
-                ob[slot, here, :] = acc[here, :].astype(BF16)
-                acc[here, :] = jnp.zeros((32, 2048), F32)
-            store(blk, ob.at[slot]).start()
+            store(blk - OUT_SLOTS).wait()
+        ob[blk % OUT_SLOTS] = acc[pl.ds(pl.multiple_of(blk * ROW_BLK, ROW_BLK), ROW_BLK), :].astype(BF16)
+        store(blk).start()
     for blk in range(n_out - OUT_SLOTS, n_out):
-        store(blk, nil).wait()
+        store(blk).wait()
     for cp in leaves:
         cp.wait()
 
 
-def table_grad(starts, toks, rows, flags, small, row_grads, vocab_dev, passed):
+def table_grad(starts, toks, rows, small, row_grads, vocab_dev, passed):
     smem = pl.BlockSpec(memory_space=pltpu.SMEM)
     vmem = pl.BlockSpec(memory_space=pltpu.VMEM)
     dma = pltpu.SemaphoreType.DMA
@@ -653,13 +644,12 @@
     shapes += [jax.ShapeDtypeStruct((1, 128), F32), jax.ShapeDtypeStruct((1, 32), F32)]
     return pl.pallas_call(
         table_kernel, out_shape=tuple(shapes),
-        in_specs=[smem] * 4 + [vmem] + [ANY] * 6, out_specs=(ANY,) * 6 + (vmem,) * 2,
-        scratch_shapes=[pltpu.VMEM((GROUP * TOK, 2048), F32)]
-        + [pltpu.VMEM((ROW_BLK, 2048), F32), pltpu.VMEM((OUT_SLOTS, ROW_BLK, 2048), BF16), pltpu.VMEM((ROW_BLK, 2048), BF16), dma, dma((OUT_SLOTS,))]
+        in_specs=[smem] * 3 + [vmem] + [ANY] * 6, out_specs=(ANY,) * 6 + (vmem,) * 2,
+        scratch_shapes=[pltpu.VMEM((vocab_dev, 2048), F32), pltpu.VMEM((IN_SLOTS, SUB, 2048), F32), pltpu.VMEM((OUT_SLOTS, ROW_BLK, 2048), BF16), dma((IN_SLOTS,)), dma((OUT_SLOTS,))]
         + [pltpu.VMEM(p.shape, p.dtype) for p in passed] + [pltpu.VMEM((576, 128), F32), dma((5,)), dma((5,))],
-        compiler_params=pltpu.CompilerParams(vmem_limit_bytes=63 * 1024 * 1024),
+        compiler_params=pltpu.CompilerParams(vmem_limit_bytes=67043328),
         cost_estimate=pl.CostEstimate(flops=10**9, bytes_accessed=90 * 10**6, transcendentals=0), name='table_grad',
-    )(starts, toks, rows, flags, small, row_grads, *passed)
+    )(starts, toks, rows, small, row_grads, *passed)
 
 
 def small_kernel(src, out, loc_sem, s_sem, r_sem):
@@ -744,16 +734,16 @@
         owner = all_ids // vocab_dev
         mine = (owner == me)
         local = all_ids - me * vocab_dev
-        stamp = jnp.arange(GROUP * tok_count).reshape(GROUP, tok_count) * ROW_BLK
-        keys = lax.sort(jnp.where(mine, (local // ROW_BLK) * (8192 * ROW_BLK) + stamp + local % ROW_BLK, 2**30).reshape(-1))
-        starts = jnp.sum((mine & (local < ROW_BLK * jnp.arange(vocab_dev // ROW_BLK + 1)[:, None, None])).astype(jnp.int32), axis=(1, 2))
-        flags = jnp.sum(mine.reshape(-1, SUB).astype(jnp.int32), axis=1)
+        stamp = jnp.arange(GROUP * tok_count).reshape(GROUP, tok_count)
+        keys = lax.sort(jnp.where(mine, stamp * 8192 + local, 2**30).reshape(-1))
+        before = (jnp.arange(GROUP * tok_count)[None, :] < SUB * jnp.arange(GROUP * tok_count // SUB + 1)[:, None]) & mine.reshape(1, -1)
+        starts = jnp.sum(before.astype(jnp.int32), axis=1)
         picked = jnp.take(emb_table, jnp.where(mine, local, 0).reshape(-1), axis=0, mode='clip')
         core = me % 2
         near = lax.dynamic_index_in_dim(owner.reshape(RING, 2, tok_count), core, 1, keepdims=False)
         mask = jnp.stack([near == me, near == me + 1 - 2 * core]).astype(BF16)
         mask = jnp.broadcast_to(mask[..., None], (2, RING, tok_count, 128))
-        picked, keys, starts, flags, w_kv_down = lax.optimization_barrier((picked, keys, starts, flags, w_kv_down))
+        picked, keys, starts, w_kv_down = lax.optimization_barrier((picked, keys, starts, w_kv_down))
         tok_rows, full_kvb, full_kva, wo_last = spread(mask, picked.reshape(GROUP, tok_count, d_model), (w_kv_up, w_kv_down, w_out[:, WO_CUT:]))
         full_wq, full_wo = bundle[:, :3072], (bundle[:, 3072:], wo_last)
         tok_rows, grad_rows = lax.optimization_barrier((tok_rows, grad_rows))
@@ -763,7 +753,7 @@
         small = jnp.concatenate([d_gain.reshape(GROUP, 1, 128), jnp.pad(d_kv_gain.reshape(GROUP, 1, 32), ((0, 0), (0, 0), (0, 96))), jnp.zeros((GROUP, 6, 128), F32)], axis=1)
         block_out, _, row_grads, g_out, g_query, g_down, g_up, g_small = grad_shards(mix, all_dy, normed.T, jnp.pad(d_down, ((0, 0), (0, D_DOWN - d_down.shape[1]))), d_query, latent.T, d_up, small, tok_rows, bundle, wo_last, d_normed, picked, gain_full.reshape(1, -1))
         grad_table, block_out, g_query, g_down, g_up, g_out, g_gain, g_kv_gain = table_grad(
-            starts, (keys // ROW_BLK) & 8191, keys & (ROW_BLK - 1), flags, g_small, row_grads, vocab_dev,
+            starts, keys >> 13, keys & 8191, g_small, row_grads, vocab_dev,
             (block_out, g_query, g_down, g_up, g_out))
         return (block_out.reshape(seq_count, seq_len, d_model), grad_table, g_gain.reshape(-1), g_query, g_down.T, g_kv_gain.reshape(-1), g_up, g_out)
 

time: 680 us -> 679 us (level)
  no operation moved by 1% of the time
where the time goes in v8:
time: 679 us; the launch traced here: 668 us
  Pallas kernels  489 us (72%)
  local copies, waits for them, and re-layouts  88.1 us (13%)
  matrix products  47.4 us (7%)
  other arithmetic  25.8 us (4%)
  between operations  15.4 us (2%)
    pallas_call x1, Pallas kernels, grad_shards(): pl.pallas_call(grad_kernel, out_shape=(jax.ShapeDtypeStruct((TOK, 2048),...  304 us
    pallas_call x1, Pallas kernels, spread(): pl.pallas_call(lambda *refs: spread_kernel(n_w, *refs), out_shape=(jax.Sh...  140 us
    gather x1, local copies, waits for them, and re-layouts, device_step(): jnp.take(emb_table, jnp.where(mine, local, 0).reshape(-1), axis=0, mode='...  46.9 us
    pallas_call x1, Pallas kernels, table_grad(): pl.pallas_call(table_kernel, out_shape=tuple(shapes), in_specs=[smem] * 3...  35 us
  transfers between devices with their start and end apart: 2, of which 1 were waited for; matrix products, arithmetic and copies ran while one was open for 23% of the time, Pallas kernels for 22%

profile of v8, /device:TPU:0, one launch (start us, length us, event | category | flops | bytes accessed | tf_op | source)
XLA Modules:
  0.0 668.3 jit_solution(17098204699680793254)
XLA Ops:
  8.2 2.2 pad_maximum_fusion
  11.3 10.2 %small_gather.1 = f32[16,8,128]{2,1,0:T(8,128)} custom-call(f32[8,128]{1,0:T(8,128)} %fusion.81.src), custom_call_target="tpu_custom_call" | custom-call | flops 10000000 | bytes 100000 | tf_op jit(solution)/shard_map/small_gather/pallas_call | solution.py:673
  24.1 1.6 slice.58.refs_4_
  25.9 6.7 sort.14
  32.7 46.9 %gather_fusion = bf16[4608,2048]{1,0:T(8,128)(2,1)} fusion(bf16[6400,2048]{1,0:T(8,128)(2,1)} %param.11, s32[5120]{0:T(1024)S(1)} %pad_clamp_fusion), kind=kCustom, calls=%fused_computation | custom fusion | bytes 37767168 | tf_op jit(solution)/shard_map/jit(_take)/gather | solution.py:741
  81.5 1.6 broadcast_in_dim.68.refs_0_
  83.1 139.7 %spread.1 = (bf16[288,2048]{1,0:T(8,128)(2,1)}, bf16[512,4096]{1,0:T(8,128)(2,1)}, bf16[2048,576]{1,0:T(8,128)(2,1)}, bf16[2048,896]{1,0:T(8,128)(2,1)}) custom-call(bf16[2,8,288,128]{3,2,1,0:T(8,128)(2,1)} %broadcast_in_dim.68.refs_0_, bf16[16,288,2048]{2,1,0:T(8,128)(2,1)} %bitcast.117, bf16[32,4096]{1,0:T(8,128)(2,1)} %refs_2_.1, ...), custom_call_target="tpu_custom_call" | custom-call | flops 8000000000 | bytes 27000000 | tf_op jit(solution)/shard_map/spread/pallas_call | solution.py:556
  224.4 1.6 fusion.15
  226.0 1.4 slice_bitcast_fusion
  227.5 3.2 convolution_convert_fusion.7
  231.9 3.7 convolution_convert_fusion
  239.4 10.2 %fusion.6 = bf16[288,3072]{1,0:T(8,128)(2,1)} fusion(bf16[2048,4224]{1,0:T(8,128)(2,1)} %all-gather.3.cloned.1.call-done.wo_h, bf16[288,2048]{1,0:T(8,128)(2,1)S(1)} %copy-done, f32[2048]{0:T(1024)} %bitcast.133, f32[288]{0:T(512)} %copy-done.38), kind=kOutput, calls=%fused_computation.8 | convolution fusion | flops 3627122688 | bytes 15542272 | tf_op jit(solution)/shard_map/dot_general | solution.py:692
  249.6 5.1 reshape.370
  254.7 1.6 slice.86
  257.1 4.2 fusion.4
  261.3 1.4 fusion.43
  267.8 1.3 fusion.24
  271.5 1.4 copy.132
  272.8 2.7 copy.160
  278.3 1.6 reshape.374
  279.8 1.4 convert_multiply_fusion.1
  285.9 2.8 copy.138
  288.7 4.9 reshape.375.dq_h
  293.6 5.4 fusion.62
  299.1 1.6 fusion.72
  301.7 7.7 %fusion = f32[288,2048]{1,0:T(8,128)S(1)} fusion(bf16[288,3072]{1,0:T(8,128)(2,1)} %reshape.375.dq_h, bf16[2048,4224]{1,0:T(8,128)(2,1)} %all-gather.3.cloned.1.call-done.wo_h), kind=kOutput, calls=%fused_computation.1 | convolution fusion | flops 3623878656 | bytes 16711680 | tf_op jit(solution)/shard_map/dot_general | solution.py:706
  311.9 1.5 copy.139.nrm_h
  314.1 2.0 fusion.41
  316.6 1.3 copy.196
  319.4 2.3 all-gather.5.cloned.1.call-done.dy_h
  321.7 304.2 %grad_shards.1 = (bf16[288,2048]{1,0:T(8,128)(2,1)}, bf16[4608,2048]{1,0:T(8,128)(2,1)}, f32[4608,2048]{1,0:T(8,128)}, f32[128,2048]{1,0:T(8,128)}, f32[128,3072...) custom-call(bf16[288,2048]{1,0:T(8,128)(2,1)} %bitcast.124, ...), custom_call_target="tpu_custom_call" | custom-call | flops 8000000000 | bytes 20000000 | tf_op jit(solution)/shard_map/grad_shards/pallas_call | solution.py:372
  626.0 35.0 %table_grad.1 = (bf16[6400,2048]{1,0:T(8,128)(2,1)}, bf16[288,2048]{1,0:T(8,128)(2,1)}, f32[128,3072]{1,0:T(8,128)}, f32[576,128]{1,0:T(8,128)}, f32[32,4096]{1,...) custom-call(s32[65]{0:T(128)} %convert_reduce_fusion.starts, s32[4608]{0:T(1024)} %get-tuple-element.90.toks, ...), custom_call_target="tpu_custom_call" | custom-call | flops 1000000000 | bytes 90000000 | tf_op jit(solution)/shard_map/table_grad/pallas_call | solution.py:645
  (178 shorter events, 34.3 us)
Async XLA Ops:
  7.2 3.3 copy-start.40
  7.2 3.4 copy-start.42
  7.2 3.4 copy-start.43
  7.2 232.2 %all-gather.3.cloned.1.call-start = ((), (), s32[]{:S(2)}) async-start(), calls=%async_computation | async-start | bytes 18382848 | tf_op jit(solution)/shard_map/all_gather | solution.py:726
  10.4 311.3 %all-gather.5.cloned.1.call-start = ((), (), s32[]{:S(2)}) async-start(), calls=%async_computation.1 | async-start | bytes 20054016 | tf_op jit(solution)/shard_map/all_gather | solution.py:750
  32.6 47.9 %copy-start.27 = (bf16[128,576]{0,1:T(8,128)(2,1)S(1)}, bf16[128,576]{0,1:T(8,128)(2,1)}, u32[]{:S(2)}) copy-start(bf16[128,576]{0,1:T(8,128)(2,1)} %param.14) | copy-start | bytes 442372
  222.8 4.7 copy-start
  223.0 15.3 %copy-start.14 = (f32[96,64]{0,1:T(8,128)}, f32[96,64]{0,1:T(8,128)S(1)}, u32[]{:S(2)}) copy-start(f32[96,64]{0,1:T(8,128)S(1)} %get-tuple-element.92) | copy-start | bytes 73732
  223.0 15.3 %copy-start.16 = (f32[96,64]{0,1:T(8,128)}, f32[96,64]{0,1:T(8,128)S(1)}, u32[]{:S(2)}) copy-start(f32[96,64]{0,1:T(8,128)S(1)} %get-tuple-element.91) | copy-start | bytes 73732
  227.4 3.2 copy-start.29
  230.7 5.0 copy-start.7
  231.8 61.8 %copy-start.33 = (f32[512]{0:T(512)}, f32[512]{0:T(512)S(1)}, u32[]{:S(2)}) copy-start(f32[512]{0:T(512)S(1)} %mul.250) | copy-start | bytes 6148
  231.9 3.7 copy-start.36
  231.9 3.7 copy-start.34
  239.3 28.5 %copy-start.11 = (bf16[3,96,16,128]{3,2,1,0:T(8,128)(2,1)}, bf16[3,96,16,128]{3,2,1,0:T(8,128)(2,1)S(1)}, u32[]{:S(2)}) copy-start(bf16[3,96,16,128]{3,2,1,0:T(8,128)(2,1)S(1)} %get-tuple-element.74) | copy-start | bytes 3538948
  254.7 2.0 copy-start.1
  254.7 2.3 copy-start.10
  257.1 4.2 copy-start.6
  267.2 2.6 copy-start.2
  267.3 8.3 %copy-start.24 = (f32[3,16,96]{2,1,0:T(8,128)}, f32[3,16,96]{2,1,0:T(8,128)S(1)}, u32[]{:S(2)}) copy-start(f32[3,16,96]{2,1,0:T(8,128)S(1)} %get-tuple-element.63) | copy-start | bytes 55300
  267.8 7.8 %copy-start.22 = (f32[3,16,96]{2,1,0:T(8,128)}, f32[3,16,96]{2,1,0:T(8,128)S(1)}, u32[]{:S(2)}) copy-start(f32[3,16,96]{2,1,0:T(8,128)S(1)} %fusion.38) | copy-start | bytes 55300
  269.1 6.5 copy-start.12
  272.8 2.7 copy-start.28
  282.1 2.0 copy-start.13
  282.2 2.0 copy-start.23
  288.7 4.9 copy-start.8
  288.7 4.9 copy-start.35
  293.6 5.5 copy-start.37
  293.6 7.1 %copy-start.26 = (bf16[288,64]{0,1:T(8,128)(2,1)S(1)}, bf16[288,64]{0,1:T(8,128)(2,1)}, u32[]{:S(2)}) copy-start(bf16[288,64]{0,1:T(8,128)(2,1)} %reshape.374) | copy-start | bytes 110596
  301.7 7.8 %copy-start.44 = (bf16[2048,576]{1,0:T(8,128)(2,1)S(1)}, bf16[2048,576]{1,0:T(8,128)(2,1)}, u32[]{:S(2)}) copy-start(bf16[2048,576]{1,0:T(8,128)(2,1)} %get-tuple-element.42) | copy-start | bytes 7077892
  311.9 2.2 copy-start.4
  316.2 2.6 copy-start.41
  (15 other events, 19.0 us)
Sparse Core Ops, SparseCore 0:
  10.6 108.6 all-gather.2
  222.9 98.7 all-gather.4

commit v9 on v8

--- a/solution.py
+++ b/solution.py
@@ -232,8 +232,6 @@
             part = sum(jnp.dot(lhs[b], rhs_ref[b, :, c0 + c:c0 + c + w], preferred_element_type=F32) for b in range(2))
             bufs[p][step, :, c:c + w] = bufs[p][step, :, c:c + w] + part
 
-    for i in range(1, GROUP):
-        mix_send(i).start()
     dy_load(0).start()
     go[...] = jnp.zeros_like(go)
     for p in range(N_PARTS):
@@ -280,13 +278,18 @@
         def _():
             own_mix.wait()
             for i in range(1, GROUP):
+                mix_send(i).start()
+
+        @pl.when(step == 2)
+        def _():
+            for i in range(1, GROUP):
                 mix_send(i).wait()
 
-        @pl.when((step > 0) & (step < 5))
+        @pl.when((step > 1) & (step < 6))
         def _():
             @pl.loop(0, 4)
             def _(j):
-                blk = (step - 1) * 4 + j
+                blk = (step - 2) * 4 + j
                 dy_load(blk).wait()
 
                 @pl.when(blk < GROUP - 1)
@@ -295,7 +298,7 @@
                 for c, w in col_tiles(2048):
                     go[:, c:c + w] += lax.dot_general(mix[blk], dy[blk % 2, :, c:c + w], (((0,), (0,)), ((), ())), preferred_element_type=F32)
 
-        @pl.when(step == 5)
+        @pl.when(step == 6)
         def _():
             for i, (src, dst) in enumerate(((mix_h, mixf), (h0_h, h0))):
                 pltpu.make_async_copy(src, dst, y_sem.at[2, i]).wait()
@@ -380,6 +383,7 @@
 
 W_SHARDS = ((32, 4096), (128, 576), (128, 896))
 HALF_TOK = TOK // 2
+CUTS = ((0, 80), (80, 64))
 
 
 def spread_kernel(n_w, *refs):
@@ -456,21 +460,22 @@
                                             device_id={'fsdp': partner}, device_id_type=MESH)
     ways = (way0, way1)
 
-    def row_hop(way, step):
-        return pltpu.make_async_remote_copy(ways[way].at[step], ways[way].at[step + 1], hs_sem.at[way, step], hr_sem.at[way, step + 1],
+    def row_hop(way, cut, step):
+        lo, n = CUTS[cut]
+        return pltpu.make_async_remote_copy(ways[way].at[step, lo:lo + n, :], ways[way].at[step + 1, lo:lo + n, :], hs_sem.at[way, cut, step], hr_sem.at[way, cut, step + 1],
                                             device_id={'fsdp': peers[way]}, device_id_type=MESH)
 
-    def fill(way, step, first):
+    def fill(way, cut, step, first):
         q = (pos + 7 - step + way * (2 * step + 2)) % RING
         chip = chip_at(q)
-        for c in range(0, HALF_TOK, 48):
+        for c in range(CUTS[cut][0], sum(CUTS[cut]), 16):
             lo = way * HALF_TOK + c
-            mine, theirs = mask[0, chip, lo:lo + 48, :], mask[1, chip, lo:lo + 48, :]
+            mine, theirs = mask[0, chip, lo:lo + 16, :], mask[1, chip, lo:lo + 16, :]
             for w in range(0, 2048, 128):
-                part = own[q, lo:lo + 48, w:w + 128] * mine + mate[q, lo:lo + 48, w:w + 128] * theirs
+                part = own[q, lo:lo + 16, w:w + 128] * mine + mate[q, lo:lo + 16, w:w + 128] * theirs
                 if not first:
-                    part = part + ways[way][step, c:c + 48, w:w + 128]
-                ways[way][step, c:c + 48, w:w + 128] = part
+                    part = part + ways[way][step, c:c + 16, w:w + 128]
+                ways[way][step, c:c + 16, w:w + 128] = part
 
     kept = []
     for i in range(n_w):
@@ -487,8 +492,9 @@
         row_share((pos + j) % RING).wait_recv()
         if j in (7, 1):
             way = 0 if j == 7 else 1
-            fill(way, 0, True)
-            row_hop(way, 0).start()
+            for cut in range(2):
+                fill(way, cut, 0, True)
+                row_hop(way, cut, 0).start()
 
     @pl.loop(1, RING)
     def _(step):
@@ -501,13 +507,14 @@
                     hop(i, way, step).start()
                 share(i, way, step).start()
                 to_twin(i, way, step).start()
-        for way in range(2):
-            row_hop(way, step - 1).wait_recv()
-            fill(way, step, False)
-
-            @pl.when(step < RING - 1)
-            def _():
-                row_hop(way, step).start()
+        for cut in range(2):
+            for way in range(2):
+                row_hop(way, cut, step - 1).wait_recv()
+                fill(way, cut, step, False)
+
+                @pl.when(step < RING - 1)
+                def _():
+                    row_hop(way, cut, step).start()
 
         @pl.when(step > 1)
         def _():
@@ -534,7 +541,8 @@
         @pl.when(step < RING - 1)
         def _():
             for way in range(2):
-                row_hop(way, step).wait_send()
+                for cut in range(2):
+                    row_hop(way, cut, step).wait_send()
         for i in range(n_w):
             for way in range(2):
                 @pl.when(step < RING - 1)
@@ -558,7 +566,7 @@
         out_shape=(jax.ShapeDtypeStruct((TOK, 2048), BF16),) + tuple(jax.ShapeDtypeStruct((GROUP * r, w), BF16) for r, w in W_SHARDS),
         in_specs=[pl.BlockSpec(memory_space=pltpu.VMEM)] + [ANY] * (n_w + 1), out_specs=(ANY,) * (n_w + 1),
         scratch_shapes=[pltpu.VMEM(s, BF16) for s in W_SHARDS] + [pltpu.VMEM((RING, TOK, 2048), BF16)] * 2 + [pltpu.VMEM((RING, HALF_TOK, 2048), BF16)] * 2
-        + [dma((n_w,)), dma((n_w,))] + [dma((n_w, 2, RING))] * 4 + [dma((n_w,))] * 2 + [dma((n_w, 2, RING))] * 4 + [dma((RING,)) for _ in range(3)] + [dma((2, RING)) for _ in range(2)] + [dma((2,))],
+        + [dma((n_w,)), dma((n_w,))] + [dma((n_w, 2, RING))] * 4 + [dma((n_w,))] * 2 + [dma((n_w, 2, RING))] * 4 + [dma((RING,)) for _ in range(3)] + [dma((2, 2, RING)) for _ in range(2)] + [dma((2,))],
         compiler_params=pltpu.CompilerParams(collective_id=2, has_side_effects=True, vmem_limit_bytes=60 * 1024 * 1024),
         cost_estimate=pl.CostEstimate(flops=8 * 10**9, bytes_accessed=27 * 10**6, transcendentals=0), name='spread',
     )(mask, rows, *shards)

time: 679 us -> 679 us (level)
  no operation moved by 1% of the time
where the time goes in v9:
time: 679 us; the launch traced here: 668 us
  Pallas kernels  488 us (72%)
  local copies, waits for them, and re-layouts  88.1 us (13%)
  matrix products  47.4 us (7%)
  other arithmetic  25.8 us (4%)
  between operations  15.4 us (2%)
    pallas_call x1, Pallas kernels, grad_shards(): pl.pallas_call(grad_kernel, out_shape=(jax.ShapeDtypeStruct((TOK, 2048),...  304 us
    pallas_call x1, Pallas kernels, spread(): pl.pallas_call(lambda *refs: spread_kernel(n_w, *refs), out_shape=(jax.Sh...  140 us
    gather x1, local copies, waits for them, and re-layouts, device_step(): jnp.take(emb_table, jnp.where(mine, local, 0).reshape(-1), axis=0, mode='...  46.9 us
    pallas_call x1, Pallas kernels, table_grad(): pl.pallas_call(table_kernel, out_shape=tuple(shapes), in_specs=[smem] * 3...  34.3 us
  transfers between devices with their start and end apart: 2, of which 1 were waited for; matrix products, arithmetic and copies ran while one was open for 23% of the time, Pallas kernels for 22%

profile of v9, /device:TPU:0, one launch (start us, length us, event | category | flops | bytes accessed | tf_op | source)
XLA Modules:
  0.0 667.6 jit_solution(2303868214535829644)
XLA Ops:
  8.2 2.2 pad_maximum_fusion
  11.3 10.2 %small_gather.1 = f32[16,8,128]{2,1,0:T(8,128)} custom-call(f32[8,128]{1,0:T(8,128)} %fusion.81.src), custom_call_target="tpu_custom_call" | custom-call | flops 10000000 | bytes 100000 | tf_op jit(solution)/shard_map/small_gather/pallas_call | solution.py:681
  24.1 1.6 slice.58.refs_4_
  25.9 6.7 sort.14
  32.7 46.9 %gather_fusion = bf16[4608,2048]{1,0:T(8,128)(2,1)} fusion(bf16[6400,2048]{1,0:T(8,128)(2,1)} %param.11, s32[5120]{0:T(1024)S(1)} %pad_clamp_fusion), kind=kCustom, calls=%fused_computation | custom fusion | bytes 37767168 | tf_op jit(solution)/shard_map/jit(_take)/gather | solution.py:749
  81.5 1.6 broadcast_in_dim.68.refs_0_
  83.1 139.7 %spread.1 = (bf16[288,2048]{1,0:T(8,128)(2,1)}, bf16[512,4096]{1,0:T(8,128)(2,1)}, bf16[2048,576]{1,0:T(8,128)(2,1)}, bf16[2048,896]{1,0:T(8,128)(2,1)}) custom-call(bf16[2,8,288,128]{3,2,1,0:T(8,128)(2,1)} %broadcast_in_dim.68.refs_0_, bf16[16,288,2048]{2,1,0:T(8,128)(2,1)} %bitcast.117, bf16[32,4096]{1,0:T(8,128)(2,1)} %refs_2_.1, ...), custom_call_target="tpu_custom_call" | custom-call | flops 8000000000 | bytes 27000000 | tf_op jit(solution)/shard_map/spread/pallas_call | solution.py:564
  224.4 1.6 fusion.15
  226.0 1.4 slice_bitcast_fusion
  227.5 3.2 convolution_convert_fusion.7
  232.0 3.7 convolution_convert_fusion
  239.4 10.2 %fusion.6 = bf16[288,3072]{1,0:T(8,128)(2,1)} fusion(bf16[2048,4224]{1,0:T(8,128)(2,1)} %all-gather.3.cloned.1.call-done.wo_h, bf16[288,2048]{1,0:T(8,128)(2,1)S(1)} %copy-done, f32[2048]{0:T(1024)} %bitcast.133, f32[288]{0:T(512)} %copy-done.38), kind=kOutput, calls=%fused_computation.8 | convolution fusion | flops 3627122688 | bytes 15542272 | tf_op jit(solution)/shard_map/dot_general | solution.py:700
  249.6 5.1 reshape.370
  254.8 1.6 slice.86
  257.1 4.2 fusion.4
  261.3 1.4 fusion.43
  267.8 1.3 fusion.24
  271.5 1.4 copy.132
  272.9 2.7 copy.160
  278.3 1.6 reshape.374
  279.8 1.4 convert_multiply_fusion.1
  285.9 2.8 copy.138
  288.7 4.9 reshape.375.dq_h
  293.6 5.4 fusion.62
  299.1 1.6 fusion.72
  301.7 7.7 %fusion = f32[288,2048]{1,0:T(8,128)S(1)} fusion(bf16[288,3072]{1,0:T(8,128)(2,1)} %reshape.375.dq_h, bf16[2048,4224]{1,0:T(8,128)(2,1)} %all-gather.3.cloned.1.call-done.wo_h), kind=kOutput, calls=%fused_computation.1 | convolution fusion | flops 3623878656 | bytes 16711680 | tf_op jit(solution)/shard_map/dot_general | solution.py:714
  311.9 1.5 copy.139.nrm_h
  314.1 2.0 fusion.41
  316.7 1.3 copy.196
  319.5 2.3 all-gather.5.cloned.1.call-done.dy_h
  321.8 304.2 %grad_shards.1 = (bf16[288,2048]{1,0:T(8,128)(2,1)}, bf16[4608,2048]{1,0:T(8,128)(2,1)}, f32[4608,2048]{1,0:T(8,128)}, f32[128,2048]{1,0:T(8,128)}, f32[128,3072...) custom-call(bf16[288,2048]{1,0:T(8,128)(2,1)} %bitcast.124, ...), custom_call_target="tpu_custom_call" | custom-call | flops 8000000000 | bytes 20000000 | tf_op jit(solution)/shard_map/grad_shards/pallas_call | solution.py:375
  626.0 34.3 %table_grad.1 = (bf16[6400,2048]{1,0:T(8,128)(2,1)}, bf16[288,2048]{1,0:T(8,128)(2,1)}, f32[128,3072]{1,0:T(8,128)}, f32[576,128]{1,0:T(8,128)}, f32[32,4096]{1,...) custom-call(s32[65]{0:T(128)} %convert_reduce_fusion.starts, s32[4608]{0:T(1024)} %get-tuple-element.90.toks, ...), custom_call_target="tpu_custom_call" | custom-call | flops 1000000000 | bytes 90000000 | tf_op jit(solution)/shard_map/table_grad/pallas_call | solution.py:653
  (178 shorter events, 34.3 us)
Async XLA Ops:
  7.2 3.3 copy-start.40
  7.2 3.4 copy-start.42
  7.2 3.4 copy-start.43
  7.2 232.2 %all-gather.3.cloned.1.call-start = ((), (), s32[]{:S(2)}) async-start(), calls=%async_computation | async-start | bytes 18382848 | tf_op jit(solution)/shard_map/all_gather | solution.py:734
  10.4 311.3 %all-gather.5.cloned.1.call-start = ((), (), s32[]{:S(2)}) async-start(), calls=%async_computation.1 | async-start | bytes 20054016 | tf_op jit(solution)/shard_map/all_gather | solution.py:758
  32.6 47.9 %copy-start.27 = (bf16[128,576]{0,1:T(8,128)(2,1)S(1)}, bf16[128,576]{0,1:T(8,128)(2,1)}, u32[]{:S(2)}) copy-start(bf16[128,576]{0,1:T(8,128)(2,1)} %param.14) | copy-start | bytes 442372
  222.8 4.7 copy-start
  223.0 15.3 %copy-start.14 = (f32[96,64]{0,1:T(8,128)}, f32[96,64]{0,1:T(8,128)S(1)}, u32[]{:S(2)}) copy-start(f32[96,64]{0,1:T(8,128)S(1)} %get-tuple-element.92) | copy-start | bytes 73732
  223.0 15.3 %copy-start.16 = (f32[96,64]{0,1:T(8,128)}, f32[96,64]{0,1:T(8,128)S(1)}, u32[]{:S(2)}) copy-start(f32[96,64]{0,1:T(8,128)S(1)} %get-tuple-element.91) | copy-start | bytes 73732
  227.5 3.2 copy-start.29
  230.7 5.0 copy-start.7
  231.8 61.8 %copy-start.33 = (f32[512]{0:T(512)}, f32[512]{0:T(512)S(1)}, u32[]{:S(2)}) copy-start(f32[512]{0:T(512)S(1)} %mul.250) | copy-start | bytes 6148
  231.9 3.7 copy-start.36
  231.9 3.7 copy-start.34
  239.4 28.5 %copy-start.11 = (bf16[3,96,16,128]{3,2,1,0:T(8,128)(2,1)}, bf16[3,96,16,128]{3,2,1,0:T(8,128)(2,1)S(1)}, u32[]{:S(2)}) copy-start(bf16[3,96,16,128]{3,2,1,0:T(8,128)(2,1)S(1)} %get-tuple-element.74) | copy-start | bytes 3538948
  254.7 2.0 copy-start.1
  254.8 2.3 copy-start.10
  257.1 4.2 copy-start.6
  267.3 2.6 copy-start.2
  267.3 8.3 %copy-start.24 = (f32[3,16,96]{2,1,0:T(8,128)}, f32[3,16,96]{2,1,0:T(8,128)S(1)}, u32[]{:S(2)}) copy-start(f32[3,16,96]{2,1,0:T(8,128)S(1)} %get-tuple-element.63) | copy-start | bytes 55300
  267.8 7.8 %copy-start.22 = (f32[3,16,96]{2,1,0:T(8,128)}, f32[3,16,96]{2,1,0:T(8,128)S(1)}, u32[]{:S(2)}) copy-start(f32[3,16,96]{2,1,0:T(8,128)S(1)} %fusion.38) | copy-start | bytes 55300
  269.1 6.5 copy-start.12
  272.9 2.7 copy-start.28
  282.2 2.0 copy-start.13
  282.2 2.0 copy-start.23
  288.7 4.9 copy-start.8
  288.7 4.9 copy-start.35
  293.6 5.5 copy-start.37
  293.6 7.1 %copy-start.26 = (bf16[288,64]{0,1:T(8,128)(2,1)S(1)}, bf16[288,64]{0,1:T(8,128)(2,1)}, u32[]{:S(2)}) copy-start(bf16[288,64]{0,1:T(8,128)(2,1)} %reshape.374) | copy-start | bytes 110596
  301.7 7.8 %copy-start.44 = (bf16[2048,576]{1,0:T(8,128)(2,1)S(1)}, bf16[2048,576]{1,0:T(8,128)(2,1)}, u32[]{:S(2)}) copy-start(bf16[2048,576]{1,0:T(8,128)(2,1)} %get-tuple-element.42) | copy-start | bytes 7077892
  311.9 2.2 copy-start.4
  316.2 2.6 copy-start.41
  (15 other events, 19.0 us)
Sparse Core Ops, SparseCore 0:
  10.6 108.6 all-gather.2
  222.9 98.7 all-gather.4
